TPU v7x, 32 devices: a whole 2x2x4 slice. The times are simulated.
32 devices in a mesh: rep: 8 (over z, x), fsdp: 2 (over y), seq: 2 (over core).
Axes of the slice: x: 2, y: 2, z: 4, core: 2. Of those that a mesh axis runs over, the one named last changes fastest.
Arguments:
- tokens: bfloat16 [32768, 1024], P(('rep', 'fsdp', 'seq')), may hold values from -6 to 6
- segments: int32 [16, 2048], P(('rep', 'fsdp')), may hold values from 0 to 15, never falling along the last dimension, each value on 1 to 1024 neighbouring positions
- attn_norm: bfloat16 [1024], P(('fsdp', 'seq')), may hold values from 0.5 to 1.5
- w_q: bfloat16 [1024, 2048], P(('fsdp', 'seq')), may hold values from -0.1875 to 0.1875
- w_k: bfloat16 [1024, 1024], P(('fsdp', 'seq')), may hold values from -0.1875 to 0.1875
- w_v: bfloat16 [1024, 1024], P(('fsdp', 'seq')), may hold values from -0.1875 to 0.1875
- q_norm: bfloat16 [128], P(('fsdp', 'seq')), may hold values from 0.5 to 1.5
- k_norm: bfloat16 [128], P(('fsdp', 'seq')), may hold values from 0.5 to 1.5
- w_o: bfloat16 [2048, 1024], P(('fsdp', 'seq')), may hold values from -1 to 1
- mlp_norm: bfloat16 [1024], P(('fsdp', 'seq')), may hold values from 0.5 to 1.5
- w_gate: bfloat16 [1024, 3072], P(('fsdp', 'seq')), may hold values from -0.1875 to 0.1875
- w_up: bfloat16 [1024, 3072], P(('fsdp', 'seq')), may hold values from -0.1875 to 0.1875
- w_down: bfloat16 [3072, 1024], P(('fsdp', 'seq')), may hold values from -0.109375 to 0.109375
- cotangent: bfloat16 [32768, 1024], P(('rep', 'fsdp', 'seq')), may hold values from -6 to 6
Outputs:
- output: bfloat16 [32768, 1024], P(('rep', 'fsdp', 'seq'))
- tokens_grad: float32 [32768, 1024], P(('rep', 'fsdp', 'seq'))
- grad_attn_norm: float32 [1024], P(('fsdp', 'seq'))
- grad_w_q: float32 [1024, 2048], P(('fsdp', 'seq'))
- grad_w_k: float32 [1024, 1024], P(('fsdp', 'seq'))
- grad_w_v: float32 [1024, 1024], P(('fsdp', 'seq'))
- grad_q_norm: float32 [128], P(('fsdp', 'seq'))
- grad_k_norm: float32 [128], P(('fsdp', 'seq'))
- grad_w_o: float32 [2048, 1024], P(('fsdp', 'seq'))
- grad_mlp_norm: float32 [1024], P(('fsdp', 'seq'))
- grad_w_gate: float32 [1024, 3072], P(('fsdp', 'seq'))
- grad_w_up: float32 [1024, 3072], P(('fsdp', 'seq'))
- grad_w_down: float32 [3072, 1024], P(('fsdp', 'seq'))
Inputs may be any that keep to these rules, and one draw needn't show every extreme that they name: `segments`: within each sequence the segment numbers never fall, every number from 0 to the largest appears, each document has 1 to 1024 tokens and one has exactly 1024.
All inputs are finite; a program needn't handle non-finite values.
Results may differ from a plain program's by a relative error of at most 0.013.
Values may be sent and summed in bfloat16 or wider, within the bound.
No kernel may reach another device: no remote copies, remote signals or barrier semaphores. Data moves between devices by JAX's collectives and lax.ppermute only.
A program may use at most 512 MiB of HBM per device.

v0:
```python
import jax
import jax.numpy as jnp
from jax import lax
from jax.sharding import PartitionSpec as P

HQ = 16
KV = 8
HD = 128


EPSILON = 1e-06
ROPE_BASE = 1000000.0
MASKED = -1e30


def shifted(value, axis, by):
    size = lax.axis_size(axis)
    pairs = [(i, i + by) for i in range(size) if 0 <= i + by < size]
    return lax.ppermute(value, axis, pairs)


def rms_scale(values, gain_vec):
    return (
        values * lax.rsqrt(jnp.mean(values * values, axis=-1, keepdims=True) + EPSILON) * gain_vec
    )


def rotate(values, cosine, sine_tab):
    half_width = values.shape[-1] // 2
    turned = jnp.concatenate([-values[..., half_width:], values[..., :half_width]], axis=-1)
    return values * cosine + turned * sine_tab


def rope_rows(seg_row, first_row, row_count):
    own_seg = lax.dynamic_slice_in_dim(seg_row, first_row, row_count, 0)
    before = jnp.sum((seg_row[None, :] < own_seg[:, None]).astype(jnp.int32), axis=1)
    position = (first_row + jnp.arange(row_count, dtype=jnp.int32) - before).astype(jnp.float32)
    freq_index = jnp.arange(HD // 2, dtype=jnp.float32)
    inverse = ROPE_BASE ** (freq_index * (-2.0 / HD))
    angles = position[:, None] * inverse[None, :]
    angles = jnp.concatenate([angles, angles], axis=1)
    return (jnp.cos(angles), jnp.sin(angles))


def head_prep(raw_proj, gain_vec, cosine, sine_tab):
    shaped = raw_proj.reshape(raw_proj.shape[0], -1, HD)
    return rotate(rms_scale(shaped, gain_vec), cosine[:, None, :], sine_tab[:, None, :])


def plain_dot(left_mat, right_mat):
    return jnp.dot(left_mat, right_mat, preferred_element_type=jnp.float32)


def lhs_dot(left_mat, right_mat):
    return lax.dot_general(
        left_mat, right_mat, (((0,), (0,)), ((), ())), preferred_element_type=jnp.float32
    )


def rhs_dot(left_mat, right_mat):
    return lax.dot_general(
        left_mat, right_mat, (((1,), (1,)), ((), ())), preferred_element_type=jnp.float32
    )


def on_device(
    tokens,
    segments,
    attn_norm,
    w_q,
    w_k,
    w_v,
    q_norm,
    k_norm,
    w_o,
    mlp_norm,
    w_gate,
    w_up,
    w_down,
    cotangent,
):
    tok_rows = tokens.shape[0]
    groups = HQ // KV
    scaling = HD ** (-0.5)
    block_rows = min(512, tok_rows)
    block_count = tok_rows // block_rows
    offset = lax.axis_index("seq") * tok_rows
    seg_row = segments[0]
    cosine, sine_tab = rope_rows(seg_row, offset, tok_rows)
    padded_seg = jnp.concatenate([jnp.full((tok_rows,), -1, jnp.int32), seg_row])
    key_seg = lax.dynamic_slice_in_dim(padded_seg, offset, 2 * tok_rows, 0)
    key_index = offset - tok_rows + jnp.arange(2 * tok_rows, dtype=jnp.int32)
    query_index = (offset + jnp.arange(tok_rows, dtype=jnp.int32)).reshape(block_count, block_rows)
    query_seg = lax.dynamic_slice_in_dim(seg_row, offset, tok_rows, 0).reshape(
        block_count, block_rows
    )
    attn_gain, wq_full, wk_full, wv_full, qn_gain, kn_gain, wo_full = (
        lax.all_gather(attn_norm, ("fsdp", "seq"), axis=0, tiled=True),
        lax.all_gather(w_q, ("fsdp", "seq"), axis=0, tiled=True),
        lax.all_gather(w_k, ("fsdp", "seq"), axis=0, tiled=True),
        lax.all_gather(w_v, ("fsdp", "seq"), axis=0, tiled=True),
        lax.all_gather(q_norm, ("fsdp", "seq"), axis=0, tiled=True),
        lax.all_gather(k_norm, ("fsdp", "seq"), axis=0, tiled=True),
        lax.all_gather(w_o, ("fsdp", "seq"), axis=0, tiled=True),
    )
    hidden_in = tokens.astype(jnp.float32)
    normed = rms_scale(hidden_in, attn_gain.astype(jnp.float32)).astype(jnp.bfloat16)
    query_raw = plain_dot(normed, wq_full)
    key_raw = plain_dot(normed, wk_full)
    value_rows = plain_dot(normed, wv_full).astype(jnp.bfloat16)
    queries = head_prep(query_raw, qn_gain.astype(jnp.float32), cosine, sine_tab).astype(
        jnp.bfloat16
    )
    key_rows = (
        head_prep(key_raw, kn_gain.astype(jnp.float32), cosine, sine_tab)
        .astype(jnp.bfloat16)
        .reshape(tok_rows, KV * HD)
    )
    prior_keys, prior_values = shifted((key_rows, value_rows), "seq", 1)
    all_keys = jnp.concatenate([prior_keys, key_rows], 0).reshape(2 * tok_rows, KV, HD)
    all_values = jnp.concatenate([prior_values, value_rows], 0).reshape(2 * tok_rows, KV, HD)
    query_blocks = queries.reshape(block_count, block_rows, KV, groups, HD)

    def block_scores(query_block, row_index, row_seg):
        allowed = (key_index[None, :] <= row_index[:, None]) & (
            key_seg[None, :] == row_seg[:, None]
        )
        raw_scores = jnp.einsum(
            "qkgd,skd->kgqs", query_block, all_keys, preferred_element_type=jnp.float32
        )
        return jnp.where(allowed[None, None], raw_scores * scaling, MASKED)

    def attend(member):
        query_block, row_index, row_seg = member
        scores = block_scores(query_block, row_index, row_seg)
        highest = jnp.max(scores, axis=-1, keepdims=True)
        weights = jnp.exp(scores - highest)
        summed = jnp.sum(weights, axis=-1, keepdims=True)
        probs = (weights / summed).astype(jnp.bfloat16)
        mixed = jnp.einsum("kgqs,skd->qkgd", probs, all_values, preferred_element_type=jnp.float32)
        return (
            mixed.reshape(block_rows, HQ * HD).astype(jnp.bfloat16),
            highest[..., 0] + jnp.log(summed[..., 0]),
        )

    mixed_blocks, log_totals = lax.map(attend, (query_blocks, query_index, query_seg))
    attended = mixed_blocks.reshape(tok_rows, HQ * HD)
    middle = hidden_in + plain_dot(attended, wo_full)
    mlp_gain, wg_full, wu_full, wd_full = (
        lax.all_gather(mlp_norm, ("fsdp", "seq"), axis=0, tiled=True),
        lax.all_gather(w_gate, ("fsdp", "seq"), axis=0, tiled=True),
        lax.all_gather(w_up, ("fsdp", "seq"), axis=0, tiled=True),
        lax.all_gather(w_down, ("fsdp", "seq"), axis=0, tiled=True),
    )
    mlp_in = rms_scale(middle, mlp_gain.astype(jnp.float32)).astype(jnp.bfloat16)
    gate_val = plain_dot(mlp_in, wg_full)
    up_val = plain_dot(mlp_in, wu_full)
    sigmoid_val = 1.0 / (1.0 + jnp.exp(-gate_val))
    activated = gate_val * sigmoid_val
    hidden_act = (activated * up_val).astype(jnp.bfloat16)
    output = (middle + plain_dot(hidden_act, wd_full)).astype(jnp.bfloat16)
    mlp_gain_back, wg_back, wu_back, wd_back = (
        lax.all_gather(mlp_norm, ("fsdp", "seq"), axis=0, tiled=True),
        lax.all_gather(w_gate, ("fsdp", "seq"), axis=0, tiled=True),
        lax.all_gather(w_up, ("fsdp", "seq"), axis=0, tiled=True),
        lax.all_gather(w_down, ("fsdp", "seq"), axis=0, tiled=True),
    )
    cot_f32 = cotangent.astype(jnp.float32)
    d_down_w = lhs_dot(hidden_act, cotangent)
    d_hidden = rhs_dot(cotangent, wd_back)
    d_gate = (d_hidden * up_val * sigmoid_val * (1.0 + gate_val * (1.0 - sigmoid_val))).astype(
        jnp.bfloat16
    )
    d_up = (d_hidden * activated).astype(jnp.bfloat16)
    d_gate_w = lhs_dot(mlp_in, d_gate)
    d_up_w = lhs_dot(mlp_in, d_up)
    d_mlp_in = rhs_dot(d_gate, wg_back) + rhs_dot(d_up, wu_back)
    unused_mid, mid_pull = jax.vjp(rms_scale, middle, mlp_gain_back.astype(jnp.float32))
    d_mid_norm, d_mlp_gain = mid_pull(d_mlp_in)
    d_middle = cot_f32 + d_mid_norm
    d_branch = d_middle.astype(jnp.bfloat16)
    attn_gain_back, wq_back, wk_back, wv_back, qn_back, kn_back, wo_back = (
        lax.all_gather(attn_norm, ("fsdp", "seq"), axis=0, tiled=True),
        lax.all_gather(w_q, ("fsdp", "seq"), axis=0, tiled=True),
        lax.all_gather(w_k, ("fsdp", "seq"), axis=0, tiled=True),
        lax.all_gather(w_v, ("fsdp", "seq"), axis=0, tiled=True),
        lax.all_gather(q_norm, ("fsdp", "seq"), axis=0, tiled=True),
        lax.all_gather(k_norm, ("fsdp", "seq"), axis=0, tiled=True),
        lax.all_gather(w_o, ("fsdp", "seq"), axis=0, tiled=True),
    )
    d_out_w = lhs_dot(attended, d_branch)
    d_attended = rhs_dot(d_branch, wo_back).astype(jnp.bfloat16)

    def attend_back(carry_pair, member):
        d_keys, d_values = carry_pair
        query_block, row_index, row_seg, log_total, grad_block = member
        scores = block_scores(query_block, row_index, row_seg)
        probs = jnp.exp(scores - log_total[..., None])
        probs_low = probs.astype(jnp.bfloat16)
        grad_heads = grad_block.reshape(block_rows, KV, groups, HD)
        d_probs = jnp.einsum(
            "qkgd,skd->kgqs", grad_heads, all_values, preferred_element_type=jnp.float32
        )
        delta_row = jnp.sum(probs * d_probs, axis=-1, keepdims=True)
        d_scores = (scaling * probs * (d_probs - delta_row)).astype(jnp.bfloat16)
        d_query = jnp.einsum(
            "kgqs,skd->qkgd", d_scores, all_keys, preferred_element_type=jnp.float32
        )
        d_keys = d_keys + jnp.einsum(
            "kgqs,qkgd->skd", d_scores, query_block, preferred_element_type=jnp.float32
        )
        d_values = d_values + jnp.einsum(
            "kgqs,qkgd->skd", probs_low, grad_heads, preferred_element_type=jnp.float32
        )
        return ((d_keys, d_values), d_query.reshape(block_rows, HQ * HD))

    zero_kv = jnp.zeros((2 * tok_rows, KV, HD), jnp.float32)
    grad_pairs = d_attended.reshape(block_count, block_rows, HQ * HD)
    (d_keys, d_values), d_query_blocks = lax.scan(
        attend_back,
        (zero_kv, zero_kv),
        (query_blocks, query_index, query_seg, log_totals, grad_pairs),
    )
    later_dkeys, later_dvalues = (
        shifted(
            d_keys[:tok_rows].reshape(tok_rows, KV * HD).astype(jnp.bfloat16), "seq", -1
        ).astype(jnp.float32),
        shifted(
            d_values[:tok_rows].reshape(tok_rows, KV * HD).astype(jnp.bfloat16), "seq", -1
        ).astype(jnp.float32),
    )
    d_key_rows = d_keys[tok_rows:].reshape(tok_rows, KV * HD) + later_dkeys
    d_value_low = (d_values[tok_rows:].reshape(tok_rows, KV * HD) + later_dvalues).astype(
        jnp.bfloat16
    )
    unused_query, query_pull = jax.vjp(
        lambda raw_proj, gain_vec: head_prep(raw_proj, gain_vec, cosine, sine_tab),
        query_raw,
        qn_back.astype(jnp.float32),
    )
    d_query_raw, d_qn = query_pull(d_query_blocks.reshape(tok_rows, HQ, HD))
    unused_key, key_pull = jax.vjp(
        lambda raw_proj, gain_vec: head_prep(raw_proj, gain_vec, cosine, sine_tab),
        key_raw,
        kn_back.astype(jnp.float32),
    )
    d_key_raw, d_kn = key_pull(d_key_rows.reshape(tok_rows, KV, HD))
    d_query_low = d_query_raw.astype(jnp.bfloat16)
    d_key_low = d_key_raw.astype(jnp.bfloat16)
    d_wq = lhs_dot(normed, d_query_low)
    d_wk = lhs_dot(normed, d_key_low)
    d_wv = lhs_dot(normed, d_value_low)
    d_normed = (
        rhs_dot(d_query_low, wq_back) + rhs_dot(d_key_low, wk_back) + rhs_dot(d_value_low, wv_back)
    )
    unused_in, in_pull = jax.vjp(rms_scale, hidden_in, attn_gain_back.astype(jnp.float32))
    d_in_norm, d_attn_gain = in_pull(d_normed)
    tokens_grad = d_middle + d_in_norm
    shards = (
        lax.psum_scatter(d_attn_gain, ("fsdp", "seq"), scatter_dimension=0, tiled=True),
        lax.psum_scatter(d_wq, ("fsdp", "seq"), scatter_dimension=0, tiled=True),
        lax.psum_scatter(d_wk, ("fsdp", "seq"), scatter_dimension=0, tiled=True),
        lax.psum_scatter(d_wv, ("fsdp", "seq"), scatter_dimension=0, tiled=True),
        lax.psum_scatter(d_qn, ("fsdp", "seq"), scatter_dimension=0, tiled=True),
        lax.psum_scatter(d_kn, ("fsdp", "seq"), scatter_dimension=0, tiled=True),
        lax.psum_scatter(d_out_w, ("fsdp", "seq"), scatter_dimension=0, tiled=True),
        lax.psum_scatter(d_mlp_gain, ("fsdp", "seq"), scatter_dimension=0, tiled=True),
        lax.psum_scatter(d_gate_w, ("fsdp", "seq"), scatter_dimension=0, tiled=True),
        lax.psum_scatter(d_up_w, ("fsdp", "seq"), scatter_dimension=0, tiled=True),
        lax.psum_scatter(d_down_w, ("fsdp", "seq"), scatter_dimension=0, tiled=True),
    )
    totals = lax.psum(
        (
            shards[0],
            shards[1],
            shards[2],
            shards[3],
            shards[4],
            shards[5],
            shards[6],
            shards[7],
            shards[8],
            shards[9],
            shards[10],
        ),
        "rep",
    )
    return (
        output,
        tokens_grad,
        totals[0],
        totals[1],
        totals[2],
        totals[3],
        totals[4],
        totals[5],
        totals[6],
        totals[7],
        totals[8],
        totals[9],
        totals[10],
    )


def solution(mesh):
    placed = (
        P(("rep", "fsdp", "seq"), None),
        P(("rep", "fsdp"), None),
        P(("fsdp", "seq")),
        P(("fsdp", "seq"), None),
        P(("fsdp", "seq"), None),
        P(("fsdp", "seq"), None),
        P(("fsdp", "seq")),
        P(("fsdp", "seq")),
        P(("fsdp", "seq"), None),
        P(("fsdp", "seq")),
        P(("fsdp", "seq"), None),
        P(("fsdp", "seq"), None),
        P(("fsdp", "seq"), None),
        P(("rep", "fsdp", "seq"), None),
    )
    return jax.shard_map(
        on_device,
        mesh=mesh,
        in_specs=placed,
        out_specs=(
            P(("rep", "fsdp", "seq"), None),
            P(("rep", "fsdp", "seq"), None),
            P(("fsdp", "seq")),
            P(("fsdp", "seq"), None),
            P(("fsdp", "seq"), None),
            P(("fsdp", "seq"), None),
            P(("fsdp", "seq")),
            P(("fsdp", "seq")),
            P(("fsdp", "seq"), None),
            P(("fsdp", "seq")),
            P(("fsdp", "seq"), None),
            P(("fsdp", "seq"), None),
            P(("fsdp", "seq"), None),
        ),
        check_vma=False,
    )
```

profile of v0, /device:TPU:0, one launch (start us, length us, event | category | flops | bytes accessed | tf_op | source)
XLA Modules:
  0.0 2134.5 jit_solution(12227881398264224540)
XLA Ops:
  13.0 8.4 all-reduce.14
  34.9 5.5 convolution_convert_fusion.1
  43.9 15.2 all-gather.12.cloned.1.call-done
  71.1 5.4 all-gather.1
  81.3 8.4 fusion.66
  99.5 6.9 copy.138
  111.0 6.5 copy.137
  117.6 9.2 fusion.80
  126.8 9.3 copy.132
  136.1 12.1 reshape.423
  148.2 21.7 %copy.135 = f32[2,512,8,2,128]{1,0,4,3,2:T(2,128)} copy(f32[2,512,8,2,128]{4,3,2,1,0:T(2,128)} %reshape.423) | data formatting | bytes 16777216 | tf_op jit(solution)/shard_map/reshape | solution.py:46
  183.4 6.7 concatenate.42
  190.1 6.7 concatenate.43
  196.8 13.4 fusion.45
  210.3 11.2 copy.136
  221.5 164.4 %while.28 = (s32[]{:T(128)}, bf16[2,512,2048]{2,1,0:T(8,128)(2,1)}, f32[2,8,2,512]{3,2,1,0:T(2,128)S(1)}, s32[2,512]{1,0:T(2,128)S(1)}, s32[2048]{0:T(1024)S(1)}...) while((s32[]{:T(128)}, bf16[2,512,2048]{2,1,0:T(8,128)(2,1)}, ...), condition=%wide.region_7.8_spmd.clone, body=%wide.region_4.7_spmd.clone.sunk | while | flops 8795449344 | bytes 226791568 | solution.py:146
  222.6 28.5 %bitcast_reduce_fusion.2 = (f32[8,2,512]{2,1,0:T(2,128)S(1)}, f32[8,512,2,2048]{3,1,2,0:T(8,128)}) fusion(pred[512,2048]{1,0:T(8,128)(4,1)S(1)} %compare_and_fusion.4, bf16[2048,8,128]{2,0,1:T(8,128)(2,1)} %get-tuple-element.681, bf16[2,512,8,2,128]{4,1,3,2,0:T(8,128)(2,1)} %get-tuple-element.680, s32[]{:T(128)S(6)} %copy.217), kind=kOutput, calls=%fused_computation.3.clone.1 | convolution fusion | flops 4345290752 | bytes 74481664 | tf_op jit(solution)/shard_map/while/body/eval_jaxpr/qkgd,skd->kgqs/dot_general | solution.py:128
  251.1 21.8 %fusion.149 = f32[8,2,512]{2,1,0:T(2,128)S(1)} fusion(f32[8,512,2,2048]{3,1,2,0:T(8,128)} %get-tuple-element.633, f32[8,2,512]{2,1,0:T(2,128)S(1)} %get-tuple-element.634, pred[512,2048]{1,0:T(8,128)(4,1)S(1)} %compare_and_fusion.4), kind=kLoop, calls=%fused_computation.7.clone.1 | loop fusion | flops 67100672 | bytes 68222976 | tf_op jit(solution)/shard_map/while/body/eval_jaxpr/reduce_sum | solution.py:138
  273.0 27.7 %fusion.150 = bf16[8,2,512,128]{2,3,1,0:T(8,128)(2,1)} fusion(bf16[2048,8,128]{0,2,1:T(8,128)(2,1)} %get-tuple-element.682, f32[8,512,2,2048]{3,1,2,0:T(8,128)} %get-tuple-element.633, f32[8,2,512]{2,1,0:T(2,128)S(1)} %fusion.149, f32[8,2,512]{2,1,0:T(2,128)S(1)} %get-tuple-element.634, pred[512,2048]{1,0:T(8,128)(4,1)S(1)} %compare_and_fusion.4), kind=kOutput, calls=%fused_computation.15.clone.1 | convolution fusion | flops 4379901952 | bytes 74514432 | tf_op jit(solution)/shard_map/while/body/eval_jaxpr/kgqs,skd->qkgd/dot_general | solution.py:140
  306.1 26.1 %bitcast_reduce_fusion.2 = (f32[8,2,512]{2,1,0:T(2,128)S(1)}, f32[8,512,2,2048]{3,1,2,0:T(8,128)}) fusion(pred[512,2048]{1,0:T(8,128)(4,1)S(1)} %compare_and_fusion.4, bf16[2048,8,128]{2,0,1:T(8,128)(2,1)} %get-tuple-element.681, bf16[2,512,8,2,128]{4,1,3,2,0:T(8,128)(2,1)} %get-tuple-element.680, s32[]{:T(128)S(6)} %copy.217), kind=kOutput, calls=%fused_computation.3.clone.1 | convolution fusion | flops 4345290752 | bytes 74481664 | tf_op jit(solution)/shard_map/while/body/eval_jaxpr/qkgd,skd->kgqs/dot_general | solution.py:128
  332.1 21.5 %fusion.149 = f32[8,2,512]{2,1,0:T(2,128)S(1)} fusion(f32[8,512,2,2048]{3,1,2,0:T(8,128)} %get-tuple-element.633, f32[8,2,512]{2,1,0:T(2,128)S(1)} %get-tuple-element.634, pred[512,2048]{1,0:T(8,128)(4,1)S(1)} %compare_and_fusion.4), kind=kLoop, calls=%fused_computation.7.clone.1 | loop fusion | flops 67100672 | bytes 68222976 | tf_op jit(solution)/shard_map/while/body/eval_jaxpr/reduce_sum | solution.py:138
  353.7 27.6 %fusion.150 = bf16[8,2,512,128]{2,3,1,0:T(8,128)(2,1)} fusion(bf16[2048,8,128]{0,2,1:T(8,128)(2,1)} %get-tuple-element.682, f32[8,512,2,2048]{3,1,2,0:T(8,128)} %get-tuple-element.633, f32[8,2,512]{2,1,0:T(2,128)S(1)} %fusion.149, f32[8,2,512]{2,1,0:T(2,128)S(1)} %get-tuple-element.634, pred[512,2048]{1,0:T(8,128)(4,1)S(1)} %compare_and_fusion.4), kind=kOutput, calls=%fused_computation.15.clone.1 | convolution fusion | flops 4379901952 | bytes 74514432 | tf_op jit(solution)/shard_map/while/body/eval_jaxpr/kgqs,skd->qkgd/dot_general | solution.py:140
  386.0 8.8 multiply_reduce_fusion.7
  398.5 12.5 fusion.87
  410.9 12.3 fusion.86
  423.3 23.9 %multiply_convert_fusion = (bf16[1024,3072]{1,0:T(8,128)(2,1)}, bf16[1024,3072]{1,0:T(8,128)(2,1)}, bf16[1024,3072]{1,0:T(8,128)(2,1)}) fusion(f32[1024,3072]{1,0:T(8,128)} %fusion.86, f32[1024,3072]{1,0:T(8,128)} %fusion.87, bf16[1024,1024]{1,0:T(8,128)(2,1)S(1)} %copy-done.20, bf16[3072,1024]{1,0:T(8,128)(2,1)} %all-gather.22.cloned.1.call-done), kind=kOutput, calls=%fused_computation.57 | convolution fusion | flops 6489636864 | bytes 52428800 | tf_op jit(solution)/shard_map/dot_general | solution.py:61
  447.2 8.9 fusion.88
  456.2 12.1 multiply_reduce_fusion.3
  470.5 6.2 convolution_convert_fusion
  476.6 580.0 %while.29 = (s32[]{:T(128)}, f32[2048,8,128]{0,2,1:T(8,128)}, f32[2048,8,128]{0,2,1:T(8,128)}, f32[2,512,2048]{1,0,2:T(2,128)}, bf16[2,512,8,2,128]{4,1,3,2,0:T(...) while((s32[]{:T(128)}, f32[2048,8,128]{0,2,1:T(8,128)}, ...), condition=%wide.region_12.13_spmd.clone, body=%wide.region_10.12_spmd.clone.sunk | while | flops 21754800128 | bytes 592318592 | solution.py:219
  484.4 26.7 %fusion.160 = f32[8,512,2,2048]{3,1,2,0:T(8,128)} fusion(bf16[2048,8,128]{0,2,1:T(8,128)(2,1)} %get-tuple-element.723, bf16[2,512,8,2,128]{4,1,3,2,0:T(8,128)(2,1)} %get-tuple-element.719, s32[]{:T(128)S(6)} %copy.227), kind=kOutput, calls=%fused_computation.38.clone.1 | convolution fusion | flops 4294967296 | bytes 73400320 | tf_op jit(solution)/shard_map/while/body/eval_jaxpr/qkgd,skd->kgqs/dot_general | solution.py:128
  511.1 30.7 %bitcast_add_fusion.8 = f32[2048,8,128]{0,2,1:T(8,128)} fusion(f32[2048,8,128]{0,2,1:T(8,128)} %get-tuple-element.702, bf16[512,8,2,128]{0,3,2,1:T(8,128)(2,1)S(1)} %bitcast.266, f32[8,512,2,2048]{3,1,2,0:T(8,128)} %fusion.160, f32[8,2,512]{2,1,0:T(2,128)S(1)} %dynamic-slice_bitcast_fusion.2, pred[512,2048]{1,0:T(8,128)(4,1)S(1)} %compare_and_fusion.5, ...), kind=kOutput, calls=%fused_computation.34.clone.1 | convolution fusion | flops 4366270464 | bytes 87064576 | tf_op jit(solution)/shard_map/while/body/eval_jaxpr/kgqs,qkgd->skd/dot_general | solution.py:212
  541.8 50.7 %fusion.161 = (f32[8,2,512]{2,1,0:T(2,128)S(1)}, f32[8,512,2,2048]{3,1,2,0:T(8,128)}) fusion(f32[8,512,2,2048]{3,1,2,0:T(8,128)} %fusion.160, f32[8,2,512]{2,1,0:T(2,128)S(1)} %dynamic-slice_bitcast_fusion.2, pred[512,2048]{1,0:T(8,128)(4,1)S(1)} %compare_and_fusion.5, bf16[512,8,2,128]{0,3,2,1:T(8,128)(2,1)S(1)} %bitcast.267, ...), kind=kOutput, calls=%fused_computation.26.clone.1 | convolution fusion | flops 4378845184 | bytes 141623296 | tf_op jit(solution)/shard_map/while/body/eval_jaxpr/qkgd,skd->kgqs/dot_general | solution.py:201
  592.6 52.8 %fusion.162 = bf16[8,2,512,2048]{3,2,1,0:T(8,128)(2,1)} fusion(f32[8,512,2,2048]{3,1,2,0:T(8,128)} %get-tuple-element.650, f32[8,512,2,2048]{3,1,2,0:T(8,128)} %fusion.160, f32[8,2,512]{2,1,0:T(2,128)S(1)} %get-tuple-element.651, f32[8,2,512]{2,1,0:T(2,128)S(1)} %dynamic-slice_bitcast_fusion.2, pred[512,2048]{1,0:T(8,128)(4,1)S(1)} %compare_and_fusion.5), kind=kLoop, calls=%fused_computation.28.clone.1 | loop fusion | flops 117440512 | bytes 168886272 | tf_op jit(solution)/shard_map/while/body/eval_jaxpr/convert_element_type | solution.py:205
  645.4 18.4 fusion.163
  663.7 17.3 bitcast_add_fusion.7
  681.1 8.5 copy.208
  689.6 74.5 %dynamic_update_slice.22 = f32[2,512,2048]{1,0,2:T(2,128)} dynamic-update-slice(f32[2,512,2048]{1,0,2:T(2,128)} %get-tuple-element.703, f32[1,512,2048]{1,0,2:T(1,128)} %copy.208, s32[]{:T(128)S(6)} %copy.227, s32[]{:T(128)} %constant.47.clone.1..sunk, s32[]{:T(128)} %constant.47.clone.1..sunk) | dynamic-update-slice | bytes 8388612 | tf_op jit(solution)/shard_map/while/body/jit(dynamic_update_index_in_dim)/dynamic_update_slice | solution.py:219
  771.7 26.7 %fusion.160 = f32[8,512,2,2048]{3,1,2,0:T(8,128)} fusion(bf16[2048,8,128]{0,2,1:T(8,128)(2,1)} %get-tuple-element.723, bf16[2,512,8,2,128]{4,1,3,2,0:T(8,128)(2,1)} %get-tuple-element.719, s32[]{:T(128)S(6)} %copy.227), kind=kOutput, calls=%fused_computation.38.clone.1 | convolution fusion | flops 4294967296 | bytes 73400320 | tf_op jit(solution)/shard_map/while/body/eval_jaxpr/qkgd,skd->kgqs/dot_general | solution.py:128
  798.4 33.1 %bitcast_add_fusion.8 = f32[2048,8,128]{0,2,1:T(8,128)} fusion(f32[2048,8,128]{0,2,1:T(8,128)} %get-tuple-element.702, bf16[512,8,2,128]{0,3,2,1:T(8,128)(2,1)S(1)} %bitcast.266, f32[8,512,2,2048]{3,1,2,0:T(8,128)} %fusion.160, f32[8,2,512]{2,1,0:T(2,128)S(1)} %dynamic-slice_bitcast_fusion.2, pred[512,2048]{1,0:T(8,128)(4,1)S(1)} %compare_and_fusion.5, ...), kind=kOutput, calls=%fused_computation.34.clone.1 | convolution fusion | flops 4366270464 | bytes 87064576 | tf_op jit(solution)/shard_map/while/body/eval_jaxpr/kgqs,qkgd->skd/dot_general | solution.py:212
  831.5 50.7 %fusion.161 = (f32[8,2,512]{2,1,0:T(2,128)S(1)}, f32[8,512,2,2048]{3,1,2,0:T(8,128)}) fusion(f32[8,512,2,2048]{3,1,2,0:T(8,128)} %fusion.160, f32[8,2,512]{2,1,0:T(2,128)S(1)} %dynamic-slice_bitcast_fusion.2, pred[512,2048]{1,0:T(8,128)(4,1)S(1)} %compare_and_fusion.5, bf16[512,8,2,128]{0,3,2,1:T(8,128)(2,1)S(1)} %bitcast.267, ...), kind=kOutput, calls=%fused_computation.26.clone.1 | convolution fusion | flops 4378845184 | bytes 141623296 | tf_op jit(solution)/shard_map/while/body/eval_jaxpr/qkgd,skd->kgqs/dot_general | solution.py:201
  882.3 52.8 %fusion.162 = bf16[8,2,512,2048]{3,2,1,0:T(8,128)(2,1)} fusion(f32[8,512,2,2048]{3,1,2,0:T(8,128)} %get-tuple-element.650, f32[8,512,2,2048]{3,1,2,0:T(8,128)} %fusion.160, f32[8,2,512]{2,1,0:T(2,128)S(1)} %get-tuple-element.651, f32[8,2,512]{2,1,0:T(2,128)S(1)} %dynamic-slice_bitcast_fusion.2, pred[512,2048]{1,0:T(8,128)(4,1)S(1)} %compare_and_fusion.5), kind=kLoop, calls=%fused_computation.28.clone.1 | loop fusion | flops 117440512 | bytes 168886272 | tf_op jit(solution)/shard_map/while/body/eval_jaxpr/convert_element_type | solution.py:205
  935.1 18.4 fusion.163
  953.4 19.7 bitcast_add_fusion.7
  973.1 8.5 copy.208
  981.6 74.5 %dynamic_update_slice.22 = f32[2,512,2048]{1,0,2:T(2,128)} dynamic-update-slice(f32[2,512,2048]{1,0,2:T(2,128)} %get-tuple-element.703, f32[1,512,2048]{1,0,2:T(1,128)} %copy.208, s32[]{:T(128)S(6)} %copy.227, s32[]{:T(128)} %constant.47.clone.1..sunk, s32[]{:T(128)} %constant.47.clone.1..sunk) | dynamic-update-slice | bytes 8388612 | tf_op jit(solution)/shard_map/while/body/jit(dynamic_update_index_in_dim)/dynamic_update_slice | solution.py:219
  1096.4 12.0 fusion.60
  1108.7 11.8 reshape.461
  1127.9 16.5 multiply_reduce_fusion
  1144.4 7.8 fusion.43
  1154.2 6.7 fusion.75
  1161.0 12.1 fusion.90
  1173.4 13.4 fusion.89
  1186.9 12.8 fusion.91
  1199.8 45.7 %reduce-scatter.14.cloned.1.call-done = f32[512,1024]{1,0:T(8,128)} async-done(((f32[2048,1024]{1,0:T(8,128)}), f32[512,1024]{1,0:T(8,128)}) %reduce-scatter.14.cloned.1.call-update) | async-done | bytes 2097168 | tf_op jit(solution)/shard_map/reduce_scatter | solution.py:266
  1245.5 74.0 %reduce-scatter.8.cloned.1.call-done = f32[256,2048]{1,0:T(8,128)} async-done(((f32[1024,2048]{1,0:T(8,128)}), f32[256,2048]{1,0:T(8,128)}) %reduce-scatter.8.cloned.1.call-update) | async-done | bytes 2097168 | tf_op jit(solution)/shard_map/reduce_scatter | solution.py:261
  1319.5 102.1 %reduce-scatter.18.cloned.1.call-done = f32[256,3072]{1,0:T(8,128)} async-done(((f32[1024,3072]{1,0:T(8,128)}), f32[256,3072]{1,0:T(8,128)}) %reduce-scatter.18.cloned.1.call-update) | async-done | bytes 3145744 | tf_op jit(solution)/shard_map/reduce_scatter | solution.py:269
  1421.6 102.2 %reduce-scatter.16.cloned.1.call-done = f32[256,3072]{1,0:T(8,128)} async-done(((f32[1024,3072]{1,0:T(8,128)}), f32[256,3072]{1,0:T(8,128)}) %reduce-scatter.16.cloned.1.call-update) | async-done | bytes 3145744 | tf_op jit(solution)/shard_map/reduce_scatter | solution.py:268
  1523.8 102.1 %reduce-scatter.20.cloned.1.call-done = f32[768,1024]{1,0:T(8,128)} async-done(((f32[3072,1024]{1,0:T(8,128)}), f32[768,1024]{1,0:T(8,128)}) %reduce-scatter.20.cloned.1.call-update) | async-done | bytes 3145744 | tf_op jit(solution)/shard_map/reduce_scatter | solution.py:270
  1627.2 12.3 add_convert_fusion
  1643.4 7.6 fusion.92
  1665.1 6.3 all-reduce.13
  1671.7 23.2 %all-reduce.11 = (f32[256]{0:T(256)}, f32[32]{0:T(128)}, f32[32]{0:T(128)}, f32[256]{0:T(256)}) all-reduce(f32[256]{0:T(256)S(1)} %dynamic-slice.4, f32[32]{0:T(128)S(1)} %dynamic-slice.6, f32[32]{0:T(128)S(1)} %dynamic-slice.8, f32[256]{0:T(256)S(1)} %dynamic-slice.10), channel_id=1, replica_groups=mesh['rep'=8,'fsdp'=2,'seq'=2] {'rep'}, use_global_device_ids=true, to_apply=%region_18.19 | all-reduce | flops 576 | bytes 4608 | tf_op jit(solution)/shard_map/psum | solution.py:272
  1695.0 418.3 %all-reduce.17.cloned.1.call-done = (f32[256,2048]{1,0:T(8,128)}, f32[256,1024]{1,0:T(8,128)}, f32[256,1024]{1,0:T(8,128)}, f32[512,1024]{1,0:T(8,128)}, f32[256...) async-done(((f32[256,2048]{1,0:T(8,128)}, f32[256,1024]{1,0:T(8,128)}, f32[256,1024]{1,0:T(8,128)}, f32[512,1024]{1,0:T(8,128)}, f32[256,3072]{1,0:T(8,128)}, ...) | async-done | bytes 15728656 | tf_op jit(solution)/shard_map/psum | solution.py:272
  (303 shorter events, 180.2 us)
Async XLA Ops:
  7.2 4.1 copy-start.57
  7.2 5.3 copy-start.61
  7.2 5.6 copy-start.62
  7.2 14.2 copy-start.63
  7.2 27.7 %all-gather.14.cloned.1.call-start = ((), (), s32[]{:S(2)}) async-start(), calls=%async_computation.9 | async-start | bytes 2621440 | tf_op jit(solution)/shard_map/all_gather | solution.py:101
  8.0 51.1 %all-gather.12.cloned.1.call-start = ((), (), s32[]{:S(2)}) async-start(), calls=%async_computation.8 | async-start | bytes 2621440 | tf_op jit(solution)/shard_map/all_gather | solution.py:100
  8.7 108.8 %all-gather.10.cloned.1.call-start = ((), (), s32[]{:S(2)}) async-start(), calls=%async_computation.7 | async-start | bytes 5242880 | tf_op jit(solution)/shard_map/all_gather | solution.py:99
  9.4 20.6 copy-start.50
  9.4 376.5 %all-gather.16.cloned.1.call-start = ((), (), s32[]{:S(2)}) async-start(), calls=%async_computation.10 | async-start | bytes 5242880 | tf_op jit(solution)/shard_map/all_gather | solution.py:104
  10.0 387.2 %all-gather.20.cloned.1.call-start = ((), (), s32[]{:S(2)}) async-start(), calls=%async_computation.12 | async-start | bytes 7864320 | tf_op jit(solution)/shard_map/all_gather | solution.py:152
  10.6 400.3 %all-gather.18.cloned.1.call-start = ((), (), s32[]{:S(2)}) async-start(), calls=%async_computation.11 | async-start | bytes 7864320 | tf_op jit(solution)/shard_map/all_gather | solution.py:151
  11.2 412.1 %all-gather.22.cloned.1.call-start = ((), (), s32[]{:S(2)}) async-start(), calls=%async_computation.13 | async-start | bytes 7864320 | tf_op jit(solution)/shard_map/all_gather | solution.py:153
  21.4 42.0 %copy-start.53 = (f32[128]{0:T(128)}, f32[128]{0:T(128)S(1)}, u32[]{:S(2)}) copy-start(f32[128]{0:T(128)S(1)} %convert_element_type.131) | copy-start | bytes 1540
  26.6 90.9 %copy-start.41 = (f32[4,1,256]{2,1,0:T(1,128)}, f32[4,1,256]{2,1,0:T(1,128)S(1)}, u32[]{:S(2)}) copy-start(f32[4,1,256]{2,1,0:T(1,128)S(1)} %convert_element_type.153) | copy-start | bytes 12292
  29.5 88.0 %copy-start.2 = (bf16[1024,1024]{0,1:T(8,128)(2,1)}, bf16[1024,1024]{0,1:T(8,128)(2,1)S(1)}, u32[]{:S(2)}) copy-start(bf16[1024,1024]{0,1:T(8,128)(2,1)S(1)} %copy.131) | copy-start | bytes 6291460
  33.7 30.8 %copy-start.10 = (f32[1024,128]{0,1:T(8,128)}, f32[1024,128]{0,1:T(8,128)S(1)}, u32[]{:S(2)}) copy-start(f32[1024,128]{0,1:T(8,128)S(1)} %get-tuple-element.485) | copy-start | bytes 1572868
  33.7 31.3 %copy-start.8 = (f32[1024,128]{0,1:T(8,128)}, f32[1024,128]{0,1:T(8,128)S(1)}, u32[]{:S(2)}) copy-start(f32[1024,128]{0,1:T(8,128)S(1)} %get-tuple-element.484) | copy-start | bytes 1572868
  34.2 6.2 copy-start.47
  34.2 83.3 %copy-start.45 = (f32[1024]{0:T(1024)}, f32[1024]{0:T(1024)S(1)}, u32[]{:S(2)}) copy-start(f32[1024]{0:T(1024)S(1)} %fusion.69) | copy-start | bytes 12292
  40.4 49.2 %collective-permute-start.1 = (bf16[1024,1024]{1,0:T(8,128)(2,1)}, bf16[1024,1024]{1,0:T(8,128)(2,1)}, u32[]{:S(2)}, u32[]{:S(2)}) collective-permute-start(bf16[1024,1024]{1,0:T(8,128)(2,1)} %convolution_convert_fusion.1), channel_id=1, source_target_pairs={{0,1},{2,3},{4,5},{6,7},{8,9},{10,11},{12,13},{14,15},{16,17},{18,... | collective-permute-start | bytes 6291464 | tf_op jit(solution)/shard_map/ppermute | solution.py:19
  65.3 5.8 copy-start.64
  67.5 38.9 %collective-permute-start = (bf16[1024,1024]{0,1:T(8,128)(2,1)}, bf16[1024,1024]{0,1:T(8,128)(2,1)}, u32[]{:S(2)}, u32[]{:S(2)}) collective-permute-start(bf16[1024,1024]{0,1:T(8,128)(2,1)} %fusion.56), channel_id=1, source_target_pairs={{0,1},{2,3},{4,5},{6,7},{8,9},{10,11},{12,13},{14,15},{16,17},{18,... | collective-permute-start | bytes 6291464 | tf_op jit(solution)/shard_map/ppermute | solution.py:19
  71.0 1128.8 %reduce-scatter.10.cloned.1.call-start = ((), (), s32[]{:S(2)}) async-start(), calls=%async_computation.15 | async-start | bytes 5242880 | tf_op jit(solution)/shard_map/reduce_scatter | solution.py:262
  71.1 125.7 %copy-start.51 = (f32[128]{0:T(128)}, f32[128]{0:T(128)S(1)}, u32[]{:S(2)}) copy-start(f32[128]{0:T(128)S(1)} %convert_element_type.127) | copy-start | bytes 1540
  174.4 4.8 copy-start.33
  174.4 4.8 copy-start.25
  386.0 10.8 copy-start.49
  410.9 12.3 copy-start.20
  423.3 23.9 %copy-start.58 = (bf16[1024,3072]{1,0:T(8,128)(2,1)S(1)}, bf16[1024,3072]{1,0:T(8,128)(2,1)}, u32[]{:S(2)}) copy-start(bf16[1024,3072]{1,0:T(8,128)(2,1)} %all-gather.18.cloned.1.call-done) | copy-start | bytes 18874372
  447.2 9.0 copy-start.5
  456.2 12.1 copy-start.14
  470.5 6.2 copy-start.6
  476.8 7.5 copy-start.29
  476.8 7.5 copy-start.35
  689.6 74.5 %copy-start.30 = (s32[2048]{0:T(1024)S(1)}, s32[2048]{0:T(1024)}, u32[]{:S(2)}) copy-start(s32[2048]{0:T(1024)} %copy-done.29) | copy-start | bytes 24580 | tf_op jit(solution)/shard_map/while
  689.6 74.5 %copy-start.36 = (f32[2,8,2,512]{3,2,1,0:T(2,128)S(1)}, f32[2,8,2,512]{3,2,1,0:T(2,128)}, u32[]{:S(2)}) copy-start(f32[2,8,2,512]{3,2,1,0:T(2,128)} %copy-done.35) | copy-start | bytes 196612 | tf_op jit(solution)/shard_map/while
  689.6 74.5 %copy-start.38 = (s32[2,512]{1,0:T(2,128)S(1)}, s32[2,512]{1,0:T(2,128)}, u32[]{:S(2)}) copy-start(s32[2,512]{1,0:T(2,128)} %copy-done.37) | copy-start | bytes 12292 | tf_op jit(solution)/shard_map/while
  689.6 74.5 %copy-start.40 = (s32[2,512]{1,0:T(2,128)S(1)}, s32[2,512]{1,0:T(2,128)}, u32[]{:S(2)}) copy-start(s32[2,512]{1,0:T(2,128)} %copy-done.39) | copy-start | bytes 12292 | tf_op jit(solution)/shard_map/while
  764.1 7.5 copy-start.29
  764.2 7.5 copy-start.35
  981.6 74.5 %copy-start.30 = (s32[2048]{0:T(1024)S(1)}, s32[2048]{0:T(1024)}, u32[]{:S(2)}) copy-start(s32[2048]{0:T(1024)} %copy-done.29) | copy-start | bytes 24580 | tf_op jit(solution)/shard_map/while
  981.6 74.5 %copy-start.36 = (f32[2,8,2,512]{3,2,1,0:T(2,128)S(1)}, f32[2,8,2,512]{3,2,1,0:T(2,128)}, u32[]{:S(2)}) copy-start(f32[2,8,2,512]{3,2,1,0:T(2,128)} %copy-done.35) | copy-start | bytes 196612 | tf_op jit(solution)/shard_map/while
  981.6 74.5 %copy-start.38 = (s32[2,512]{1,0:T(2,128)S(1)}, s32[2,512]{1,0:T(2,128)}, u32[]{:S(2)}) copy-start(s32[2,512]{1,0:T(2,128)} %copy-done.37) | copy-start | bytes 12292 | tf_op jit(solution)/shard_map/while
  981.6 74.5 %copy-start.40 = (s32[2,512]{1,0:T(2,128)S(1)}, s32[2,512]{1,0:T(2,128)}, u32[]{:S(2)}) copy-start(s32[2,512]{1,0:T(2,128)} %copy-done.39) | copy-start | bytes 12292 | tf_op jit(solution)/shard_map/while
  1059.1 6.1 collective-permute-start.2
  1078.6 121.1 %reduce-scatter.12.cloned.1.call-start = ((), (), s32[]{:S(2)}) async-start(), calls=%async_computation.16 | async-start | bytes 5242880 | tf_op jit(solution)/shard_map/reduce_scatter | solution.py:263
  1081.2 8.6 collective-permute-start.3
  1096.3 149.1 %reduce-scatter.14.cloned.1.call-start = ((), (), s32[]{:S(2)}) async-start(), calls=%async_computation.17 | async-start | bytes 10485760 | tf_op jit(solution)/shard_map/reduce_scatter | solution.py:266
  1108.4 211.1 %reduce-scatter.8.cloned.1.call-start = ((), (), s32[]{:S(2)}) async-start(), calls=%async_computation.14 | async-start | bytes 10485760 | tf_op jit(solution)/shard_map/reduce_scatter | solution.py:261
  1127.9 16.5 copy-start.34
  1161.0 260.6 %reduce-scatter.18.cloned.1.call-start = ((), (), s32[]{:S(2)}) async-start(), calls=%async_computation.19 | async-start | bytes 15728640 | tf_op jit(solution)/shard_map/reduce_scatter | solution.py:269
  1173.1 350.7 %reduce-scatter.16.cloned.1.call-start = ((), (), s32[]{:S(2)}) async-start(), calls=%async_computation.18 | async-start | bytes 15728640 | tf_op jit(solution)/shard_map/reduce_scatter | solution.py:268
  1186.8 439.0 %reduce-scatter.20.cloned.1.call-start = ((), (), s32[]{:S(2)}) async-start(), calls=%async_computation.20 | async-start | bytes 15728640 | tf_op jit(solution)/shard_map/reduce_scatter | solution.py:270
  1199.7 913.6 %all-reduce.17.cloned.1.call-start = ((), (), s32[]{:S(2)}) async-start(), calls=%async_computation.21 | async-start | bytes 31457280 | tf_op jit(solution)/shard_map/psum | solution.py:272
  1643.4 7.7 copy-start.24
  1643.4 7.7 copy-start.60
  1653.5 3.2 copy-start.48
  1653.5 3.2 copy-start.7
  1659.8 5.4 copy-start.55
  1659.8 5.4 copy-start.56
  2113.3 3.3 copy-start.28
  2113.3 4.3 copy-start.27
  2113.3 5.2 copy-start.22
  2116.6 3.3 copy-start.19
  (28 other events, 56.6 us)
Sparse Core Ops, SparseCore 0:
  9.6 25.2 all-gather.13
  36.5 22.5 all-gather.11
  60.7 34.4 all-gather.9
  96.6 34.4 all-gather.15
  132.5 46.3 all-gather.19
  180.3 46.3 all-gather.17
  228.2 46.3 all-gather.21
  1078.8 45.5 reduce-scatter.9
  1126.9 44.5 reduce-scatter.11
  1174.0 71.4 reduce-scatter.13
  1248.0 71.4 reduce-scatter.7
  1321.9 99.6 reduce-scatter.17
  1424.2 99.5 reduce-scatter.15
  1526.3 99.5 reduce-scatter.19
  1631.4 481.7 all-reduce.16
where the time goes:
time: 2160 us; the launch traced here: 2130 us
  waiting for transfers between devices  871 us (40%)
  matrix products  597 us (28%)
  local copies, waits for them, and re-layouts  342 us (16%)
  other arithmetic  248 us (11%)
  blocking collectives  48.5 us (2%)
    psum x1, waiting for transfers between devices, on_device(): lax.psum((shards[0], shards[1], shards[2], shards[3], shards[4], shards[5...  418 us
    dynamic_update_slice x4, local copies, waits for them, and re-layouts, on_device(): lax.scan(attend_back, (zero_kv, zero_kv), (query_blocks, query_index, que...  166 us
    dot_general x4, matrix products, block_scores(): jnp.einsum('qkgd,skd->kgqs', query_block, all_keys, preferred_element_typ...  108 us
    convert_element_type x2, other arithmetic, attend_back(): d_scores = (scaling * probs * (d_probs - delta_row)).astype(jnp.bfloat16)  106 us
    reduce_scatter x1, waiting for transfers between devices, on_device(): lax.psum_scatter(d_gate_w, ('fsdp', 'seq'), scatter_dimension=0, tiled=True)  102 us
    reduce_scatter x1, waiting for transfers between devices, on_device(): lax.psum_scatter(d_up_w, ('fsdp', 'seq'), scatter_dimension=0, tiled=True)  102 us
    reduce_scatter x1, waiting for transfers between devices, on_device(): lax.psum_scatter(d_down_w, ('fsdp', 'seq'), scatter_dimension=0, tiled=True)  102 us
    dot_general x2, matrix products, attend_back(): jnp.einsum('qkgd,skd->kgqs', grad_heads, all_values, preferred_element_ty...  101 us
  transfers between devices with their start and end apart: 19, of which 10 were waited for; matrix products, arithmetic and copies ran while one was open for 24% of the time, Pallas kernels for 0%

commit v1 on v0

v1 whole, which is shorter than its diff:
```python
import jax
import jax.numpy as jnp
from jax import lax
from jax.experimental import pallas as pl
from jax.experimental.pallas import tpu as pltpu
from jax.sharding import PartitionSpec as P

HQ = 16
KV = 8
HD = 128
EPSILON = 1e-06
ROPE_BASE = 1000000.0
SCALE = HD**-0.5
LOG2E = 1.4426950408889634
BLK = 256
BF = jnp.bfloat16
F32 = jnp.float32


def nn(a, b):
    return lax.dot_general(a, b, (((1,), (0,)), ((), ())), preferred_element_type=F32)


def nt(a, b):
    return lax.dot_general(a, b, (((1,), (1,)), ((), ())), preferred_element_type=F32)


def tn(a, b):
    return lax.dot_general(a, b, (((0,), (0,)), ((), ())), preferred_element_type=F32)


def full_spec(shape):
    return pl.BlockSpec(shape, lambda *_: (0,) * len(shape), pipeline_mode=pl.Buffered(1))


def qkv_kernel(x_ref, gain_ref, w_ref, cos_ref, sin_ref, hg_ref, normed_ref, qkv_ref, raw_ref):
    x = x_ref[...].astype(F32)
    scale = lax.rsqrt(jnp.mean(x * x, axis=1, keepdims=True) + EPSILON)
    normed = (x * scale * gain_ref[...]).astype(BF)
    normed_ref[...] = normed
    cosine = cos_ref[...]
    sine = sin_ref[...]
    groups = w_ref.shape[1] // (4 * HD)
    for g in range(groups):
        acc = nn(normed, w_ref[:, g * 512 : (g + 1) * 512])
        for h in range(3):
            t = acc[:, h * HD : (h + 1) * HD]
            gain = hg_ref[0:1, :] if h < 2 else hg_ref[1:2, :]
            n = t * lax.rsqrt(jnp.mean(t * t, axis=1, keepdims=True) + EPSILON) * gain
            turned = n * cosine + pltpu.roll(n, HD // 2, 1) * sine
            qkv_ref[:, g * 512 + h * HD : g * 512 + (h + 1) * HD] = turned.astype(BF)
            raw_ref[:, g * 384 + h * HD : g * 384 + (h + 1) * HD] = t.astype(BF)
        qkv_ref[:, g * 512 + 384 : (g + 1) * 512] = acc[:, 384:].astype(BF)


def project(x_all, gain, w_qkv, cosine, sine, head_gains):
    length, width = x_all.shape
    cols = w_qkv.shape[1]
    rows = lambda n: pl.BlockSpec((BLK, n), lambda t: (t, 0))
    return pl.pallas_call(
        qkv_kernel,
        grid=(length // BLK,),
        in_specs=[
            rows(width),
            full_spec((1, width)),
            full_spec((width, cols)),
            rows(HD),
            rows(HD),
            full_spec((2, HD)),
        ],
        out_specs=[rows(width), rows(cols), rows(cols // 4 * 3)],
        out_shape=[
            jax.ShapeDtypeStruct((length, width), BF),
            jax.ShapeDtypeStruct((length, cols), BF),
            jax.ShapeDtypeStruct((length, cols // 4 * 3), BF),
        ],
        name="project",
    )(x_all, gain, w_qkv, cosine, sine, head_gains)


def stack_heads(block):
    return jnp.concatenate([block[:, :HD], block[:, HD:]], axis=0)


def attend_kernel(low_ref, qkv_ref, start_ref, out_ref, lse_ref, acc, total):
    blocks = qkv_ref.shape[0] // BLK

    def query_block(qb, carry):
        r0 = pl.multiple_of(qb * BLK, BLK)
        q2 = stack_heads(qkv_ref[pl.ds(r0, BLK), 0:256])
        first = start_ref[pl.ds(r0, BLK), :]
        first2 = jnp.concatenate([first, first], axis=0)

        def tile(k0, diagonal):
            k = qkv_ref[pl.ds(k0, BLK), 256:384]
            v = qkv_ref[pl.ds(k0, BLK), 384:512]
            s = nt(q2, k) * (SCALE * LOG2E)
            col = lax.broadcasted_iota(jnp.int32, (2 * BLK, BLK), 1)
            mask = col >= first2 - k0
            if diagonal:
                row = lax.broadcasted_iota(jnp.int32, (2 * BLK, BLK), 0) & (BLK - 1)
                mask = mask & (col <= row)
            p = jnp.where(mask, jnp.exp2(s), 0.0)
            part = p[:, :HD]
            for n in range(1, BLK // HD):
                part = part + p[:, n * HD : (n + 1) * HD]
            return part, nn(p.astype(BF), v)

        part, mixed = tile(r0, True)
        total[...] = part
        acc[...] = mixed

        def step(kb, inner):
            more, mixed_more = tile(pl.multiple_of(kb * BLK, BLK), False)
            total[...] += more
            acc[...] += mixed_more
            return inner

        lax.fori_loop(low_ref[qb], qb, step, 0)
        sums = total[...]
        o = (acc[...] / jnp.sum(sums, axis=1, keepdims=True)).astype(BF)
        out_ref[pl.ds(r0, BLK), 0:HD] = o[:BLK]
        out_ref[pl.ds(r0, BLK), HD : 2 * HD] = o[BLK:]
        line = jnp.log2(jnp.sum(jnp.transpose(sums), axis=0, keepdims=True))
        lse_ref[0, 0:1, pl.ds(r0, BLK)] = line[:, :BLK]
        lse_ref[0, 1:2, pl.ds(r0, BLK)] = line[:, BLK:]
        return carry

    lax.fori_loop(0, blocks, query_block, 0)


def attend(low, qkv, start):
    length, cols = qkv.shape
    groups = cols // 512
    return pl.pallas_call(
        attend_kernel,
        grid_spec=pltpu.PrefetchScalarGridSpec(
            num_scalar_prefetch=1,
            grid=(groups,),
            in_specs=[
                pl.BlockSpec((length, 512), lambda g, low: (0, g)),
                full_spec((length, 1)),
            ],
            out_specs=[
                pl.BlockSpec((length, 256), lambda g, low: (0, g)),
                pl.BlockSpec((1, 2, length), lambda g, low: (g, 0, 0)),
            ],
            scratch_shapes=[
                pltpu.VMEM((2 * BLK, HD), F32),
                pltpu.VMEM((2 * BLK, HD), F32),
            ],
        ),
        out_shape=[
            jax.ShapeDtypeStruct((length, groups * 256), BF),
            jax.ShapeDtypeStruct((groups, 2, length), F32),
        ],
        name="attend",
    )(low, qkv, start.reshape(length, 1))


def head_back(d, raw, gain, cosine, sine):
    dn = d * cosine + pltpu.roll(d * sine, HD // 2, 1)
    raw = raw.astype(F32)
    r = lax.rsqrt(jnp.mean(raw * raw, axis=1, keepdims=True) + EPSILON)
    n = raw * r
    dg = jnp.sum(dn * n, axis=0, keepdims=True)
    scaled = dn * gain
    dv = r * (scaled - n * jnp.mean(scaled * n, axis=1, keepdims=True))
    return dv.astype(BF), dg


def attend_back_kernel(
    low_ref,
    qkv_ref,
    do_ref,
    o_ref,
    lse_ref,
    start_ref,
    raw_ref,
    cos_ref,
    sin_ref,
    hg_ref,
    out_ref,
    dg_ref,
    dk_acc,
    dv_acc,
    dq_acc,
):
    blocks = qkv_ref.shape[0] // BLK
    dg_ref[...] = jnp.zeros_like(dg_ref)

    def query_block(qb, carry):
        r0 = pl.multiple_of(qb * BLK, BLK)
        rows = pl.ds(r0, BLK)
        q2 = stack_heads(qkv_ref[rows, 0:256])
        do2 = stack_heads(do_ref[rows, :])
        o2 = stack_heads(o_ref[rows, :])
        delta = jnp.sum(jnp.transpose(do2.astype(F32) * o2.astype(F32)), axis=0, keepdims=True)
        lse = jnp.concatenate([lse_ref[0, 0:1, rows], lse_ref[0, 1:2, rows]], axis=1)
        first = start_ref[0:1, rows]
        first2 = jnp.concatenate([first, first], axis=1)

        def tile(k0, diagonal):
            k = qkv_ref[pl.ds(k0, BLK), 256:384]
            v = qkv_ref[pl.ds(k0, BLK), 384:512]
            key = lax.broadcasted_iota(jnp.int32, (BLK, 2 * BLK), 0)
            mask = key >= first2 - k0
            if diagonal:
                query = lax.broadcasted_iota(jnp.int32, (BLK, 2 * BLK), 1) & (BLK - 1)
                mask = mask & (key <= query)
            p = jnp.where(mask, jnp.exp2(nt(k, q2) * (SCALE * LOG2E) - lse), 0.0)
            ds = (p * (nt(v, do2) - delta)).astype(BF)
            return nn(ds, q2), nn(p.astype(BF), do2), tn(ds, k)

        dk, dv, dq = tile(r0, True)
        dk_acc[rows, :] = dk
        dv_acc[rows, :] = dv
        dq_acc[...] = dq

        def step(kb, inner):
            k0 = pl.multiple_of(kb * BLK, BLK)
            dk, dv, dq = tile(k0, False)
            dk_acc[pl.ds(k0, BLK), :] += dk
            dv_acc[pl.ds(k0, BLK), :] += dv
            dq_acc[...] += dq
            return inner

        lax.fori_loop(low_ref[qb], qb, step, 0)
        cosine = cos_ref[rows, :]
        sine = sin_ref[rows, :]
        for h in range(2):
            d_raw, dg = head_back(
                dq_acc[h * BLK : (h + 1) * BLK, :] * SCALE,
                raw_ref[rows, h * HD : (h + 1) * HD],
                hg_ref[0:1, :],
                cosine,
                sine,
            )
            out_ref[rows, h * HD : (h + 1) * HD] = d_raw
            dg_ref[0, 0:1, :] += dg
        return carry

    lax.fori_loop(0, blocks, query_block, 0)

    def key_block(kb, carry):
        rows = pl.ds(pl.multiple_of(kb * BLK, BLK), BLK)
        d_raw, dg = head_back(
            dk_acc[rows, :] * SCALE,
            raw_ref[rows, 256:384],
            hg_ref[1:2, :],
            cos_ref[rows, :],
            sin_ref[rows, :],
        )
        out_ref[rows, 256:384] = d_raw
        out_ref[rows, 384:512] = dv_acc[rows, :].astype(BF)
        dg_ref[0, 1:2, :] += dg
        return carry

    lax.fori_loop(0, blocks, key_block, 0)


def attend_back(low, qkv, d_att, att, lse, start, raw, cosine, sine, head_gains):
    length, cols = qkv.shape
    groups = cols // 512
    column = lambda n: pl.BlockSpec((length, n), lambda g, low: (0, g))
    return pl.pallas_call(
        attend_back_kernel,
        grid_spec=pltpu.PrefetchScalarGridSpec(
            num_scalar_prefetch=1,
            grid=(groups,),
            in_specs=[
                column(512),
                column(256),
                column(256),
                pl.BlockSpec((1, 2, length), lambda g, low: (g, 0, 0)),
                full_spec((1, length)),
                column(384),
                full_spec((length, HD)),
                full_spec((length, HD)),
                full_spec((2, HD)),
            ],
            out_specs=[
                column(512),
                pl.BlockSpec((1, 2, HD), lambda g, low: (g, 0, 0)),
            ],
            scratch_shapes=[
                pltpu.VMEM((length, HD), F32),
                pltpu.VMEM((length, HD), F32),
                pltpu.VMEM((2 * BLK, HD), F32),
            ],
        ),
        out_shape=[
            jax.ShapeDtypeStruct((length, cols), BF),
            jax.ShapeDtypeStruct((groups, 2, HD), F32),
        ],
        name="attend_back",
    )(low, qkv, d_att, att, lse, start.reshape(1, length), raw, cosine, sine, head_gains)


def mlp_kernel(m_ref, g_ref, wgu_ref, wd_ref, hid_ref, dgu_ref):
    m = m_ref[...]
    g = g_ref[...]
    half = wd_ref.shape[0]
    step = 512
    for n in range(0, half, step):
        gate = nn(m, wgu_ref[:, n : n + step])
        up = nn(m, wgu_ref[:, half + n : half + n + step])
        dh = nt(g, wd_ref[n : n + step, :])
        sig = 1.0 / (1.0 + jnp.exp(-gate))
        act = gate * sig
        hid_ref[:, n : n + step] = (act * up).astype(BF)
        dgu_ref[:, n : n + step] = (dh * up * (sig + act * (1.0 - sig))).astype(BF)
        dgu_ref[:, half + n : half + n + step] = (dh * act).astype(BF)


def mlp(mlp_in, cot, w_gu, w_down):
    length, width = mlp_in.shape
    half = w_down.shape[0]
    rows = lambda n: pl.BlockSpec((BLK, n), lambda t: (t, 0))
    return pl.pallas_call(
        mlp_kernel,
        grid=(length // BLK,),
        in_specs=[rows(width), rows(width), full_spec((width, 2 * half)), full_spec((half, width))],
        out_specs=[rows(half), rows(2 * half)],
        out_shape=[
            jax.ShapeDtypeStruct((length, half), BF),
            jax.ShapeDtypeStruct((length, 2 * half), BF),
        ],
        name="mlp",
    )(mlp_in, cot, w_gu, w_down)


def swap(value, axis):
    size = lax.axis_size(axis)
    return lax.ppermute(value, axis, [(i, i ^ 1) for i in range(size)])


def ordered(first_is_mine, mine, other):
    return jnp.where(
        first_is_mine,
        jnp.concatenate([mine, other], axis=0),
        jnp.concatenate([other, mine], axis=0),
    )


def part(value, index, count, axis=0):
    size = value.shape[axis] // count
    return lax.dynamic_slice_in_dim(value, index * size, size, axis)


def columns(value, *ranges):
    return [value[:, a:b] for a, b in ranges]


def pack_qkv(w_q, w_k, w_v):
    halves = []
    for c in range(2):
        pieces = []
        for kv in (2 * c, 2 * c + 1, 4 + 2 * c, 5 + 2 * c):
            pieces.append(w_q[:, kv * 256 : (kv + 1) * 256])
            pieces.append(w_k[:, kv * HD : (kv + 1) * HD])
            pieces.append(w_v[:, kv * HD : (kv + 1) * HD])
        halves.append(jnp.concatenate(pieces, axis=1))
    return halves


def unpack_qkv(halves):
    w_q, w_k, w_v = ([None] * KV for _ in range(3))
    for c in range(2):
        for n, kv in enumerate((2 * c, 2 * c + 1, 4 + 2 * c, 5 + 2 * c)):
            block = halves[c][:, n * 512 : (n + 1) * 512]
            w_q[kv], w_k[kv], w_v[kv] = block[:, :256], block[:, 256:384], block[:, 384:]
    return tuple(jnp.concatenate(w, axis=1) for w in (w_q, w_k, w_v))


def pack_gu(w_gate, w_up):
    quarter = w_gate.shape[1] // 4
    halves = []
    for c in range(2):
        pieces = []
        for w in (w_gate, w_up):
            pieces.append(w[:, c * quarter : (c + 1) * quarter])
            pieces.append(w[:, (2 + c) * quarter : (3 + c) * quarter])
        halves.append(jnp.concatenate(pieces, axis=1))
    return halves


def unpack_gu(halves):
    quarter = halves[0].shape[1] // 4
    out = []
    for n in range(2):
        q = [h[:, (2 * n + k) * quarter : (2 * n + k + 1) * quarter] for k in range(2) for h in halves]
        out.append(jnp.concatenate(q, axis=1))
    return tuple(out)


def take_rows(full, core):
    quarters = full.reshape(4, full.shape[0] // 4, full.shape[1])
    return jnp.concatenate(
        [
            lax.dynamic_index_in_dim(quarters, core, 0, keepdims=False),
            lax.dynamic_index_in_dim(quarters, 2 + core, 0, keepdims=False),
        ],
        axis=0,
    )


def gather_any(value):
    return lax.all_gather(value, ("fsdp", "seq"), axis=0, tiled=True)


class Exchange:
    def __init__(self):
        self.core = lax.axis_index("seq")
        self.row = lax.axis_index("fsdp")
        self.side = lax.axis_index("rep") % 2
        self.pairs = lax.axis_size("fsdp") == 2 and lax.axis_size("rep") % 2 == 0

    def over_fsdp(self, mine, split):
        if split:
            here = swap(part(mine, self.side, 2), "fsdp")
            there = swap(here, "rep")
            other = ordered(self.side == 0, here, there)
        else:
            other = swap(mine, "fsdp")
        return ordered(self.row == 0, mine, other)

    def rows(self, shard, split=True):
        if not self.pairs:
            return take_rows(gather_any(shard), self.core)
        return self.over_fsdp(shard, split)

    def cols(self, halves, split=True):
        if not self.pairs:
            full = [gather_any(h) for h in halves]
            return jnp.where(self.core == 0, full[0], full[1])
        mine = jnp.where(self.core == 0, halves[0], halves[1])
        other = jnp.where(self.core == 0, halves[1], halves[0])
        local = ordered(self.core == 0, mine, swap(other, "seq"))
        return self.over_fsdp(local, split)

    def over_rep(self, value):
        size = lax.axis_size("rep")
        mine = part(value, self.side, 2) + swap(part(value, 1 - self.side, 2), "rep")
        if size > 2:
            groups = [[i for i in range(size) if i % 2 == s] for s in range(2)]
            mine = lax.psum(mine, "rep", axis_index_groups=groups)
        return ordered(self.side == 0, mine, swap(mine, "rep"))

    def sum_rows(self, grad):
        if not self.pairs:
            quarter = grad.shape[0] // 2
            full = jnp.zeros((4, quarter, grad.shape[1]), BF)
            full = lax.dynamic_update_slice(full, grad[None, :quarter], (self.core, 0, 0))
            full = lax.dynamic_update_slice(full, grad[None, quarter:], (2 + self.core, 0, 0))
            return self.scatter_any(full.reshape(4 * quarter, grad.shape[1])).astype(F32)
        mine = part(grad, self.row, 2) + swap(part(grad, 1 - self.row, 2), "fsdp")
        return self.over_rep(mine).astype(F32)

    def scatter_any(self, full):
        shard = lax.psum_scatter(full, ("fsdp", "seq"), scatter_dimension=0, tiled=True)
        return lax.psum(shard, "rep")

    def sum_cols(self, grad):
        if not self.pairs:
            zero = jnp.zeros_like(grad)
            halves = [
                self.scatter_any(jnp.where(self.core == c, grad, zero)).astype(F32) for c in range(2)
            ]
            return halves
        mine = part(grad, self.row, 2) + swap(part(grad, 1 - self.row, 2), "fsdp")
        mine = self.over_rep(mine)
        keep = part(mine, self.core, 2)
        got = swap(part(mine, 1 - self.core, 2), "seq")
        return [
            jnp.where(self.core == 0, keep, got).astype(F32),
            jnp.where(self.core == 0, got, keep).astype(F32),
        ]


def norm_back(d, v, gain):
    r = lax.rsqrt(jnp.mean(v * v, axis=1, keepdims=True) + EPSILON)
    n = v * r
    scaled = d * gain
    dv = r * (scaled - n * jnp.mean(scaled * n, axis=1, keepdims=True))
    return dv, jnp.sum(d * n, axis=0)


def on_device(
    tokens,
    segments,
    attn_norm,
    w_q,
    w_k,
    w_v,
    q_norm,
    k_norm,
    w_o,
    mlp_norm,
    w_gate,
    w_up,
    w_down,
    cotangent,
):
    ex = Exchange()
    rows, width = tokens.shape
    length = 2 * rows
    core = ex.core

    sizes = (attn_norm.shape[0], mlp_norm.shape[0], q_norm.shape[0], k_norm.shape[0])
    gains = gather_any(jnp.concatenate([attn_norm, mlp_norm, q_norm, k_norm])[None, :]).astype(F32)
    offsets = [0, sizes[0], sizes[0] + sizes[1], sizes[0] + sizes[1] + sizes[2], sum(sizes)]
    attn_gain, mlp_gain, q_gain, k_gain = (
        gains[:, offsets[n] : offsets[n + 1]].reshape(1, -1) for n in range(4)
    )
    head_gains = jnp.concatenate([q_gain, k_gain], axis=0)

    wqkv = ex.cols(pack_qkv(w_q, w_k, w_v), split=False)
    wo = ex.rows(w_o)
    wgu = ex.cols(pack_gu(w_gate, w_up))
    wd = ex.rows(w_down)

    tokens_other = swap(tokens, "seq")
    cot_other = swap(cotangent, "seq")
    x_all = ordered(core == 0, tokens, tokens_other)

    seg = segments[0]
    start = jnp.sum((seg[None, :] < seg[:, None]).astype(jnp.int32), axis=1)
    position = (jnp.arange(length, dtype=jnp.int32) - start).astype(F32)
    inverse = ROPE_BASE ** (jnp.arange(HD // 2, dtype=F32) * (-2.0 / HD))
    angles = position[:, None] * inverse[None, :]
    cos_half, sin_half = jnp.cos(angles), jnp.sin(angles)
    cosine = jnp.concatenate([cos_half, cos_half], axis=1)
    sine = jnp.concatenate([-sin_half, sin_half], axis=1)
    low = start[::BLK] // BLK

    normed, qkv, raw = project(x_all, attn_gain, wqkv, cosine, sine, head_gains)
    attended, lse = attend(low, qkv, start)

    mixed_other = nn(part(attended, 1 - core, 2), wo).astype(BF)
    mixed_mine = nn(part(attended, core, 2), wo)
    middle = tokens.astype(F32) + mixed_mine + swap(mixed_other, "seq").astype(F32)
    scale = lax.rsqrt(jnp.mean(middle * middle, axis=1, keepdims=True) + EPSILON)
    mlp_mine = (middle * scale * mlp_gain).astype(BF)
    mlp_in = jnp.concatenate([mlp_mine, swap(mlp_mine, "seq")], axis=0)
    cot_local = jnp.concatenate([cotangent, cot_other], axis=0)

    hidden, d_gu = mlp(mlp_in, cot_local, wgu, wd)
    g_down = ex.sum_rows(tn(hidden, cot_local).astype(BF))
    g_gu = ex.sum_cols(tn(mlp_in, d_gu).astype(BF))

    d_in_other = nt(d_gu[rows:], wgu).astype(BF)
    d_in = nt(d_gu[:rows], wgu) + swap(d_in_other, "seq").astype(F32)
    d_mid, dg_mlp = norm_back(d_in, middle, mlp_gain)
    d_middle = cotangent.astype(F32) + d_mid
    d_branch = d_middle.astype(BF)
    branch_all = ordered(core == 0, d_branch, swap(d_branch, "seq"))
    d_att = nt(branch_all, wo).astype(BF)
    g_o = ex.sum_rows(tn(attended, branch_all).astype(BF))

    d_qkv, dg_heads = attend_back(
        low, qkv, d_att, attended, lse, start, raw, cosine, sine, head_gains
    )
    g_qkv = ex.sum_cols(tn(normed, d_qkv).astype(BF))

    d_norm_other = nt(part(d_qkv, 1 - core, 2), wqkv).astype(BF)
    d_normed = nt(part(d_qkv, core, 2), wqkv) + swap(d_norm_other, "seq").astype(F32)
    d_tok, dg_attn = norm_back(d_normed, tokens.astype(F32), attn_gain)
    tokens_grad = d_middle + d_tok

    out_other = nn(hidden[rows:], wd).astype(BF)
    output = (middle + nn(hidden[:rows], wd) + swap(out_other, "seq").astype(F32)).astype(BF)

    dg_heads = jnp.sum(dg_heads, axis=0)
    small = lax.psum(
        jnp.concatenate([dg_attn, dg_mlp, dg_heads[0], dg_heads[1]]), ("rep", "fsdp", "seq")
    )
    shard = ex.row * 2 + core
    pieces = []
    at = 0
    for size in sizes:
        total = size * lax.axis_size("fsdp") * 2
        pieces.append(lax.dynamic_slice_in_dim(small[at : at + total], shard * size, size, 0))
        at += total
    g_q, g_k, g_v = unpack_qkv(g_qkv)
    g_gate, g_up = unpack_gu(g_gu)
    return (
        output,
        tokens_grad,
        pieces[0],
        g_q,
        g_k,
        g_v,
        pieces[2],
        pieces[3],
        g_o,
        pieces[1],
        g_gate,
        g_up,
        g_down,
    )


def solution(mesh):
    token_rows = P(("rep", "fsdp", "seq"), None)
    vec = P(("fsdp", "seq"))
    mat = P(("fsdp", "seq"), None)
    return jax.shard_map(
        on_device,
        mesh=mesh,
        in_specs=(
            token_rows,
            P(("rep", "fsdp"), None),
            vec,
            mat,
            mat,
            mat,
            vec,
            vec,
            mat,
            vec,
            mat,
            mat,
            mat,
            token_rows,
        ),
        out_specs=(
            token_rows,
            token_rows,
            vec,
            mat,
            mat,
            mat,
            vec,
            vec,
            mat,
            vec,
            mat,
            mat,
            mat,
        ),
        check_vma=False,
    )
```

time: 2160 us -> 911 us (0.42)
  waiting for transfers between devices: 871 us -> 315 us
  matrix products: 597 us -> 115 us
  local copies, waits for them, and re-layouts: 342 us -> 46.4 us
  Pallas kernels: 0 us -> 171 us
  other arithmetic: 248 us -> 98.9 us
  blocking collectives: 48.5 us -> 120 us
    dot_general x35 -> x13, matrix products: 597 us -> 115 us  [the longest x5 50.1 us: nt(): lax.dot_general(a, b, (((1,), (1,)), ((), ())), preferred_element_type=F32)]
    reduce_scatter x7 -> x0, waiting for transfers between devices: 426 us -> none  [the longest x1 102 us: on_device(): lax.psum_scatter(d_gate_w, ('fsdp', 'seq'), scatter_dimension=0, tiled=True)]
    psum x1, waiting for transfers between devices: 418 us -> 117 us  [over_rep(): mine = lax.psum(mine, 'rep', axis_index_groups=groups)]
    ppermute x4 -> x31, waiting for transfers between devices: 6.49 us -> 198 us  [swap(): return lax.ppermute(value, axis, [(i, i ^ 1) for i in range(size)])]
    dynamic_update_slice x8 -> x0, local copies, waits for them, and re-layouts: 175 us -> none  [the longest x4 166 us: on_device(): lax.scan(attend_back, (zero_kv, zero_kv), (query_blocks, query_index, que...]
    pallas_call x0 -> x4, Pallas kernels: none -> 171 us  [the longest x1 79.3 us: attend_back(): pl.pallas_call(attend_back_kernel, grid_spec=pltpu.PrefetchScalarGridSpec...]
    convert_element_type x14 -> x7, other arithmetic: 132 us -> 8.84 us  [the longest x2 4 us: sum_rows(): return self.over_rep(mine).astype(F32)]
    reduce_sum x7 -> x3, other arithmetic: 68.6 us -> 2.3 us  [the longest x1 1.81 us: on_device(): start = jnp.sum((seg[None, :] < seg[:, None]).astype(jnp.int32), axis=1)]
  transfers between devices with their start and end apart: 19 -> 32, of which waited for: 10 -> 10; matrix products, arithmetic and copies ran while one was open for 24% -> 25% of each run, Pallas kernels for 0% -> 16%
where the time goes in v1:
time: 911 us; the launch traced here: 905 us
  waiting for transfers between devices  315 us (35%)
  Pallas kernels  171 us (19%)
  blocking collectives  120 us (13%)
  matrix products  115 us (13%)
  other arithmetic  98.9 us (11%)
  local copies, waits for them, and re-layouts  46.4 us (5%)
  starting transfers between devices  22.8 us (3%)
  between operations  16 us (2%)
    ppermute x31, waiting for transfers between devices, swap(): return lax.ppermute(value, axis, [(i, i ^ 1) for i in range(size)])  198 us
    psum x1, waiting for transfers between devices, over_rep(): mine = lax.psum(mine, 'rep', axis_index_groups=groups)  117 us
    pallas_call x1, Pallas kernels, attend_back(): pl.pallas_call(attend_back_kernel, grid_spec=pltpu.PrefetchScalarGridSpec...  79.3 us
    psum x1, blocking collectives, on_device(): lax.psum(jnp.concatenate([dg_attn, dg_mlp, dg_heads[0], dg_heads[1]]), ('...  77.8 us
    dot_general x5, matrix products, nt(): lax.dot_general(a, b, (((1,), (1,)), ((), ())), preferred_element_type=F32)  50.1 us
    pallas_call x1, Pallas kernels, attend(): pl.pallas_call(attend_kernel, grid_spec=pltpu.PrefetchScalarGridSpec(num_...  46.1 us
    dot_general x4, matrix products, tn(): lax.dot_general(a, b, (((0,), (0,)), ((), ())), preferred_element_type=F32)  42.8 us
    unnamed x1, blocking collectives  42.5 us
  transfers between devices with their start and end apart: 32, of which 10 were waited for; matrix products, arithmetic and copies ran while one was open for 25% of the time, Pallas kernels for 16%

profile of v1, /device:TPU:0, one launch (start us, length us, event | category | flops | bytes accessed | tf_op | source)
XLA Modules:
  0.0 905.3 jit_solution(8828112678486657746)
XLA Ops:
  7.3 1.9 constant_dynamic-slice_fusion.12
  9.2 3.0 collective-permute-start.3
  27.5 2.0 broadcast_select_fusion.1
  29.6 1.8 convert_reduce_fusion
  31.5 2.4 maximum_select_fusion.8
  33.9 5.5 fusion.46
  41.1 42.5 %all-reduce = bf16[2304]{0:T(1024)(128)(2,1)S(1)} all-reduce(bf16[2304]{0:T(1024)(128)(2,1)S(1)} %dynamic-update-slice), channel_id=2, replica_groups=mesh['rep'=8,'fsdp'=2,'seq'=2] {'fsdp','seq'}, use_global_device_ids=true, to_apply=%add | all-reduce | flops 2304 | bytes 9216
  83.7 3.8 pad_maximum_fusion.5
  92.6 8.7 collective-permute-done.4
  101.3 2.0 maximum_select_fusion.13
  103.3 5.1 maximum_select_fusion.1.x_ref
  108.4 6.2 maximum_select_fusion.2.w_ref
  114.6 17.1 %project.1 = (bf16[2048,1024]{1,0:T(8,128)(2,1)}, bf16[2048,2048]{1,0:T(8,128)(2,1)}, bf16[2048,1536]{1,0:T(8,128)(2,1)}) custom-call(bf16[2048,1024]{1,0:T(8,128)(2,1)} %maximum_select_fusion.1.x_ref, f32[1,1024]{1,0:T(1,128)} %bitcast.40, bf16[1024,2048]{1,0:T(8,128)(2,1)} %maximum_select_fusion.2.w_ref, f32[2048,128]{1,0:T(8,128)} %get-tuple-element.111.cos_ref, ...), custom_call_target="tpu_custom_call" | custom-call | tf_op jit(solution)/shard_map/project/pallas_call | solution.py:60
  131.7 46.1 %attend.1 = (bf16[2048,1024]{1,0:T(8,128)(2,1)}, f32[4,2,2048]{2,1,0:T(2,128)}) custom-call(s32[8]{0:T(128)} %and_select_fusion.low_ref, bf16[2048,2048]{1,0:T(8,128)(2,1)} %get-tuple-element.22.qkv_ref, s32[2048,1]{1,0:T(8,128)} %copy.28.start_ref), custom_call_target="tpu_custom_call" | custom-call | tf_op jit(solution)/shard_map/attend/pallas_call | solution.py:135
  177.8 5.4 fusion.30
  183.2 2.6 maximum_select_fusion.4
  187.3 2.1 constant_dynamic-slice_fusion.10
  191.1 49.9 %collective-permute-done.11 = bf16[384,1024]{1,0:T(8,128)(2,1)} collective-permute-done((bf16[384,1024]{1,0:T(8,128)(2,1)}, bf16[384,1024]{1,0:T(8,128)(2,1)}, u32[]{:S(2)}, u32[]{:S(2)}) %collective-permute-start.11) | collective-permute-done | bytes 786464 | tf_op jit(solution)/shard_map/ppermute | solution.py:335
  243.0 6.8 multiply_reduce_fusion.2
  249.9 2.0 multiply_convert_fusion
  252.4 1.9 constant_dynamic-update-slice_fusion.17
  254.3 7.4 collective-permute-done.12
  261.7 2.7 maximum_select_fusion.11
  264.4 3.1 maximum_select_fusion.6.wd_ref
  267.5 1.8 constant_dynamic-update-slice_fusion.16.g_ref
  269.3 1.9 copy-done.8
  271.3 22.9 %collective-permute-done.10 = bf16[256,3072]{1,0:T(8,128)(2,1)} collective-permute-done((bf16[256,3072]{1,0:T(8,128)(2,1)}, bf16[256,3072]{1,0:T(8,128)(2,1)}, u32[]{:S(2)}, u32[]{:S(2)}) %collective-permute-start.10) | collective-permute-done | bytes 1572896 | tf_op jit(solution)/shard_map/ppermute | solution.py:335
  294.1 3.3 maximum_select_fusion.5
  297.5 5.0 maximum_select_fusion.wgu_ref
  302.5 4.6 pad_maximum_fusion.m_ref
  307.1 28.5 %mlp.1 = (bf16[2048,1536]{1,0:T(8,128)(2,1)}, bf16[2048,3072]{1,0:T(8,128)(2,1)}) custom-call(bf16[2048,1024]{1,0:T(8,128)(2,1)} %pad_maximum_fusion.m_ref, bf16[2048,1024]{1,0:T(8,128)(2,1)} %copy-done.8, bf16[1024,3072]{1,0:T(8,128)(2,1)} %maximum_select_fusion.wgu_ref, bf16[1536,1024]{1,0:T(8,128)(2,1)} %maximum_select_fusion.6.wd_ref), custom_call_target="tpu_custom_call" | custom-call | tf_op jit(solution)/shard_map/mlp/pallas_call | solution.py:320
  335.6 11.8 %fusion.39 = bf16[1024,1024]{1,0:T(8,128)(2,1)} fusion(bf16[1024,3072]{1,0:T(8,128)(2,1)} %maximum_select_fusion.wgu_ref, bf16[2048,3072]{1,0:T(8,128)(2,1)} %get-tuple-element.25), kind=kOutput, calls=%fused_computation.62 | convolution fusion | flops 6443499520 | bytes 14680064 | tf_op jit(solution)/shard_map/dot_general | solution.py:25
  347.4 7.2 convolution_convert_fusion.1
  356.8 10.4 %multiply_reduce_fusion = (f32[1024]{0:T(1024)S(1)}, f32[1024]{0:T(1024)S(1)}, f32[1024,1024]{1,0:T(8,128)S(1)}) fusion(f32[1024,1024]{1,0:T(8,128)S(1)} %copy-done.1, f32[1024]{0:T(1024)S(1)} %add_rsqrt_fusion.1, f32[1024]{0:T(1024)S(1)} %bitcast.37, bf16[1024,1024]{1,0:T(8,128)(2,1)} %collective-permute-done.14, bf16[1024,3072]{1,0:T(8,128)(2,1)S(1)} %bitcast.31, ...), kind=kOutput, calls=%fused_computation.24 | convolution fusion | flops 6450837504 | bytes 23085056 | tf_op jit(solution)/shard_map/dot_general | solution.py:25
  369.6 17.8 %convolution_convert_fusion = bf16[1024,3072]{1,0:T(8,128)(2,1)S(1)} fusion(bf16[2048,3072]{1,0:T(8,128)(2,1)} %get-tuple-element.25, bf16[1024,1024]{1,0:T(8,128)(2,1)} %collective-permute-done.6, bf16[1024,1024]{1,0:T(8,128)(2,1)} %multiply_convert_fusion), kind=kOutput, calls=%fused_computation.12 | convolution fusion | flops 12896436224 | bytes 23068672 | tf_op jit(solution)/shard_map/dot_general | solution.py:29
  387.6 3.0 copy-done.11
  393.2 2.1 dynamic-slice_add_fusion.2
  398.9 6.8 convolution_convert_fusion.3.do_ref
  405.7 79.3 %attend_back.1 = (bf16[2048,2048]{1,0:T(8,128)(2,1)}, f32[4,2,128]{2,1,0:T(2,128)}) custom-call(s32[8]{0:T(128)} %and_select_fusion.low_ref, bf16[2048,2048]{1,0:T(8,128)(2,1)} %get-tuple-element.22.qkv_ref, bf16[2048,1024]{1,0:T(8,128)(2,1)} %convolution_convert_fusion.3.do_ref, bf16[2048,1024]{1,0:T(8,128)(2,1)} %get-tuple-element.23.o_ref, ...), custom_call_target="tpu_custom_call" | custom-call | tf_op jit(solution)/shard_map/attend_back/pallas_call | solution.py:266
  485.0 12.8 %convolution_convert_fusion.2 = bf16[1024,2048]{1,0:T(8,128)(2,1)S(1)} fusion(bf16[2048,1024]{1,0:T(8,128)(2,1)} %get-tuple-element.30, bf16[2048,2048]{1,0:T(8,128)(2,1)} %get-tuple-element.28), kind=kOutput, calls=%fused_computation.37 | convolution fusion | flops 8592031744 | bytes 16777216 | tf_op jit(solution)/shard_map/dot_general | solution.py:29
  497.8 1.9 copy-done.13
  501.8 5.1 convolution_convert_fusion.4
  509.5 3.0 dynamic-slice_add_fusion
  515.2 2.7 dynamic-slice_add_fusion.6
  517.9 53.0 %collective-permute-done.21 = bf16[512,1024]{1,0:T(8,128)(2,1)} collective-permute-done((bf16[512,1024]{1,0:T(8,128)(2,1)}, bf16[512,1024]{1,0:T(8,128)(2,1)}, u32[]{:S(2)}, u32[]{:S(2)}) %collective-permute-start.21) | collective-permute-done | bytes 1048608 | tf_op jit(solution)/shard_map/ppermute | solution.py:335
  570.9 1.9 dynamic-slice_add_fusion.4
  572.9 2.4 dynamic-slice_add_fusion.1
  577.6 3.1 dynamic-slice_add_fusion.3
  580.7 29.5 %collective-permute-done.22 = bf16[256,1024]{1,0:T(8,128)(2,1)S(1)} collective-permute-done((bf16[256,1024]{1,0:T(8,128)(2,1)S(1)}, bf16[256,1024]{1,0:T(8,128)(2,1)S(1)}, u32[]{:S(2)}, u32[]{:S(2)}) %collective-permute-start.22) | collective-permute-done | bytes 524320 | tf_op jit(solution)/shard_map/ppermute | solution.py:335
  612.6 9.5 %fusion.36 = bf16[1024,1024]{1,0:T(8,128)(2,1)} fusion(bf16[1024,2048]{1,0:T(8,128)(2,1)} %maximum_select_fusion.2.w_ref, bf16[2048,2048]{1,0:T(8,128)(2,1)} %get-tuple-element.28, s32[]{:T(128)S(6)} %select_n.228), kind=kOutput, calls=%fused_computation.60 | convolution fusion | flops 4296015872 | bytes 10485764 | tf_op jit(solution)/shard_map/dot_general | solution.py:25
  622.1 4.7 fusion.33
  627.3 5.4 fusion.20
  632.7 11.8 %fusion.11 = (f32[1024]{0:T(1024)S(1)}, f32[1024]{0:T(1024)S(1)}, f32[1024,1024]{1,0:T(8,128)}) fusion(bf16[1024,1024]{1,0:T(8,128)(2,1)} %param.14, f32[1024]{0:T(1024)S(1)} %add_rsqrt_fusion, f32[1024]{0:T(1024)S(1)} %bitcast.41, bf16[1024,1024]{1,0:T(8,128)(2,1)} %collective-permute-done.16, bf16[1024,2048]{1,0:T(8,128)(2,1)} %maximum_select_fusion.2.w_ref, ...), kind=kOutput, calls=%fused_computation.17 | convolution fusion | flops 4304402432 | bytes 16793604 | tf_op jit(solution)/shard_map/dot_general | solution.py:25
  644.5 117.0 %all-reduce.4.cloned.1.call-done = (bf16[256,2048]{1,0:T(8,128)(2,1)}, bf16[256,1024]{1,0:T(8,128)(2,1)}, bf16[256,3072]{1,0:T(8,128)(2,1)}, bf16[384,1024]{1,0:T(8,128)(2,1)}) async-done(((bf16[256,2048]{1,0:T(8,128)(2,1)}, bf16[256,1024]{1,0:T(8,128)(2,1)}, bf16[256,3072]{1,0:T(8,128)(2,1)}, bf16[384,1024]{1,0:T(8,128)(2,1)}), (bf16[256,2048]{1,0:T(8,128)(2,1)}, bf16[256,1024]{1,0:T(8,128)(2,1)}, ...) | async-done | bytes 3932176 | tf_op jit(solution)/shard_map/psum | solution.py:447
  763.5 11.3 %fusion.10 = (f32[1024,1024]{1,0:T(8,128)}, bf16[1024,1024]{1,0:T(8,128)(2,1)}) fusion(bf16[1024,1024]{1,0:T(8,128)(2,1)} %param.14, f32[1024,1024]{1,0:T(8,128)} %get-tuple-element.110, f32[1024]{0:T(1024)S(1)} %broadcast_multiply_fusion, f32[1024]{0:T(1024)S(1)} %bitcast.42, f32[1024]{0:T(1024)S(1)} %add_rsqrt_fusion, ...), kind=kLoop, calls=%fused_computation.16 | loop fusion | flops 18874368 | bytes 29384704 | tf_op jit(solution)/shard_map/add | solution.py:569
  774.8 77.8 %psum.35 = f32[2304]{0:T(1024)S(1)} all-reduce(f32[2304]{0:T(1024)S(1)} %pad_maximum_fusion.7), channel_id=1, replica_groups=mesh['rep'=8,'fsdp'=2,'seq'=2] {'rep','fsdp','seq'}, use_global_device_ids=true, to_apply=%region_8.9 | all-reduce | flops 2304 | bytes 18432 | tf_op jit(solution)/shard_map/psum | solution.py:575
  852.7 2.3 collective-permute-start.30
  857.4 2.4 maximum_select_fusion.10
  860.0 22.6 %collective-permute-done.23 = bf16[256,1024]{1,0:T(8,128)(2,1)S(1)} collective-permute-done((bf16[256,1024]{1,0:T(8,128)(2,1)}, bf16[256,1024]{1,0:T(8,128)(2,1)S(1)}, u32[]{:S(2)}, u32[]{:S(2)}) %collective-permute-start.23) | collective-permute-done | bytes 524320 | tf_op jit(solution)/shard_map/ppermute | solution.py:335
  884.4 2.2 fusion.44
  886.7 2.5 maximum_select_fusion.7
  890.5 2.3 collective-permute-done.27
  894.2 2.1 pad_maximum_fusion.2
  896.2 2.1 pad_maximum_fusion.1
  (247 shorter events, 59.7 us)
Async XLA Ops:
  7.2 13.2 %copy-start.28 = (bf16[256,2048]{1,0:T(8,128)(2,1)S(1)}, bf16[256,2048]{1,0:T(8,128)(2,1)}, u32[]{:S(2)}) copy-start(bf16[256,2048]{1,0:T(8,128)(2,1)} %param.17) | copy-start | bytes 3145732
  7.2 754.3 %all-reduce.4.cloned.1.call-start = ((), (), s32[]{:S(2)}) async-start(), calls=%async_computation | async-start | bytes 7864320 | tf_op jit(solution)/shard_map/psum | solution.py:447
  9.2 78.4 %collective-permute-start.3 = (bf16[256,1024]{1,0:T(8,128)(2,1)}, bf16[256,1024]{1,0:T(8,128)(2,1)}, u32[]{:S(2)}, u32[]{:S(2)}) collective-permute-start(bf16[256,1024]{1,0:T(8,128)(2,1)} %constant_dynamic-slice_fusion.12), channel_id=1, source_target_pairs={{0,2},{2,0},{1,3},{3,1},{4,6},{6,4},{5,7},{7,5},{8,10},{10,8},{9,1... | collective-permute-start | bytes 1572872 | tf_op jit(solution)/shard_map/ppermute | solution.py:335
  26.7 4.8 collective-permute-start.1
  26.8 76.5 %collective-permute-start = (bf16[1024,1024]{1,0:T(8,128)(2,1)S(1)}, bf16[1024,1024]{1,0:T(8,128)(2,1)}, u32[]{:S(2)}, u32[]{:S(2)}) collective-permute-start(bf16[1024,1024]{1,0:T(8,128)(2,1)S(1)} %copy-done.4), channel_id=1, source_target_pairs={{0,1},{1,0},{2,3},{3,2},{4,5},{5,4},{6,7},{7,6},{8,9},{9,8},{10,11... | collective-permute-start | bytes 6291464 | tf_op jit(solution)/shard_map/ppermute | solution.py:335
  29.5 153.7 %collective-permute-start.8 = (bf16[256,3072]{1,0:T(8,128)(2,1)}, bf16[256,3072]{1,0:T(8,128)(2,1)}, u32[]{:S(2)}, u32[]{:S(2)}) collective-permute-start(bf16[256,3072]{1,0:T(8,128)(2,1)} %get-tuple-element.54), channel_id=1, source_target_pairs={{0,1},{1,0},{2,3},{3,2},{4,5},{5,4},{6,7},{7,6},{8,9},{9,8},{10,11... | collective-permute-start | bytes 4718600 | tf_op jit(solution)/shard_map/ppermute | solution.py:335
  31.4 59.2 %copy-start.33 = (s32[2048]{0:T(1024)}, s32[2048]{0:T(1024)S(1)}, u32[]{:S(2)}) copy-start(s32[2048]{0:T(1024)S(1)} %convert_reduce_fusion) | copy-start | bytes 24580
  31.4 8.0 copy-start.38
  31.5 8.0 copy-start.39
  31.5 7.9 copy-start.40
  31.5 7.9 copy-start.41
  31.5 8.1 copy-start.46
  33.9 74.5 %collective-permute-start.2 = (bf16[512,2048]{1,0:T(8,128)(2,1)}, bf16[512,2048]{1,0:T(8,128)(2,1)}, u32[]{:S(2)}, u32[]{:S(2)}) collective-permute-start(bf16[512,2048]{1,0:T(8,128)(2,1)} %maximum_select_fusion.8), channel_id=1, source_target_pairs={{0,2},{2,0},{1,3},{3,1},{4,6},{6,4},{5,7},{7,5},{8,10},{10,8},{9,1... | collective-permute-start | bytes 6291464 | tf_op jit(solution)/shard_map/ppermute | solution.py:335
  87.6 13.7 %collective-permute-start.4 = (bf16[256,1024]{1,0:T(8,128)(2,1)}, bf16[256,1024]{1,0:T(8,128)(2,1)}, u32[]{:S(2)}, u32[]{:S(2)}) collective-permute-start(bf16[256,1024]{1,0:T(8,128)(2,1)} %collective-permute-done.3), channel_id=1, source_target_pairs={{0,4},{4,0},{8,12},{12,8},{16,20},{20,16},{24,28},{28,24},{1,5},{5... | collective-permute-start | bytes 1572872 | tf_op jit(solution)/shard_map/ppermute | solution.py:335
  103.3 74.5 %copy-start.26 = (bf16[512,1024]{1,0:T(8,128)(2,1)}, bf16[512,1024]{1,0:T(8,128)(2,1)S(1)}, u32[]{:S(2)}) copy-start(bf16[512,1024]{1,0:T(8,128)(2,1)S(1)} %maximum_select_fusion.13) | copy-start | bytes 3145732
  131.7 46.1 %copy-start.31 = (bf16[512,1024]{1,0:T(8,128)(2,1)S(1)}, bf16[512,1024]{1,0:T(8,128)(2,1)}, u32[]{:S(2)}) copy-start(bf16[512,1024]{1,0:T(8,128)(2,1)} %param.22) | copy-start | bytes 3145732
  183.2 59.9 %collective-permute-start.5 = (bf16[1024,1024]{1,0:T(8,128)(2,1)}, bf16[1024,1024]{1,0:T(8,128)(2,1)}, u32[]{:S(2)}, u32[]{:S(2)}) collective-permute-start(bf16[1024,1024]{1,0:T(8,128)(2,1)} %fusion.30), channel_id=1, source_target_pairs={{0,1},{1,0},{2,3},{3,2},{4,5},{5,4},{6,7},{7,6},{8,9},{9,8},{10,11... | collective-permute-start | bytes 6291464 | tf_op jit(solution)/shard_map/ppermute | solution.py:335
  187.0 55.5 %collective-permute-start.9 = (bf16[256,3072]{1,0:T(8,128)(2,1)}, bf16[256,3072]{1,0:T(8,128)(2,1)}, u32[]{:S(2)}, u32[]{:S(2)}) collective-permute-start(bf16[256,3072]{1,0:T(8,128)(2,1)} %constant_dynamic-slice_fusion.11), channel_id=1, source_target_pairs={{0,2},{2,0},{1,3},{3,1},{4,6},{6,4},{5,7},{7,5},{8,10},{10,8},{9,1... | collective-permute-start | bytes 4718600 | tf_op jit(solution)/shard_map/ppermute | solution.py:335
  189.4 51.6 %collective-permute-start.11 = (bf16[384,1024]{1,0:T(8,128)(2,1)}, bf16[384,1024]{1,0:T(8,128)(2,1)}, u32[]{:S(2)}, u32[]{:S(2)}) collective-permute-start(bf16[384,1024]{1,0:T(8,128)(2,1)} %constant_dynamic-slice_fusion.10), channel_id=1, source_target_pairs={{0,2},{2,0},{1,3},{3,1},{4,6},{6,4},{5,7},{7,5},{8,10},{10,8},{9,1... | collective-permute-start | bytes 2359304 | tf_op jit(solution)/shard_map/ppermute | solution.py:335
  191.1 76.4 %collective-permute-start.7 = (bf16[1024,1024]{1,0:T(8,128)(2,1)}, bf16[1024,1024]{1,0:T(8,128)(2,1)}, u32[]{:S(2)}, u32[]{:S(2)}) collective-permute-start(bf16[1024,1024]{1,0:T(8,128)(2,1)} %param.27), channel_id=1, source_target_pairs={{0,1},{1,0},{2,3},{3,2},{4,5},{5,4},{6,7},{7,6},{8,9},{9,8},{10,11... | collective-permute-start | bytes 6291464 | tf_op jit(solution)/shard_map/ppermute | solution.py:335
  241.0 20.7 %collective-permute-start.12 = (bf16[384,1024]{1,0:T(8,128)(2,1)}, bf16[384,1024]{1,0:T(8,128)(2,1)}, u32[]{:S(2)}, u32[]{:S(2)}) collective-permute-start(bf16[384,1024]{1,0:T(8,128)(2,1)} %collective-permute-done.11), channel_id=1, source_target_pairs={{0,4},{4,0},{8,12},{12,8},{16,20},{20,16},{24,28},{28,24},{1,5},{5... | collective-permute-start | bytes 2359304 | tf_op jit(solution)/shard_map/ppermute | solution.py:335
  242.5 51.6 %collective-permute-start.10 = (bf16[256,3072]{1,0:T(8,128)(2,1)}, bf16[256,3072]{1,0:T(8,128)(2,1)}, u32[]{:S(2)}, u32[]{:S(2)}) collective-permute-start(bf16[256,3072]{1,0:T(8,128)(2,1)} %collective-permute-done.9), channel_id=1, source_target_pairs={{0,4},{4,0},{8,12},{12,8},{16,20},{20,16},{24,28},{28,24},{1,5},{5... | collective-permute-start | bytes 4718600 | tf_op jit(solution)/shard_map/ppermute | solution.py:335
  252.4 50.0 %collective-permute-start.6 = (bf16[1024,1024]{1,0:T(8,128)(2,1)}, bf16[1024,1024]{1,0:T(8,128)(2,1)}, u32[]{:S(2)}, u32[]{:S(2)}) collective-permute-start(bf16[1024,1024]{1,0:T(8,128)(2,1)} %multiply_convert_fusion), channel_id=1, source_target_pairs={{0,1},{1,0},{2,3},{3,2},{4,5},{5,4},{6,7},{7,6},{8,9},{9,8},{10,11... | collective-permute-start | bytes 6291464 | tf_op jit(solution)/shard_map/ppermute | solution.py:335
  252.4 12.0 %copy-start.16 = (bf16[768,1024]{1,0:T(8,128)(2,1)S(1)}, bf16[768,1024]{1,0:T(8,128)(2,1)}, u32[]{:S(2)}) copy-start(bf16[768,1024]{1,0:T(8,128)(2,1)} %param.26) | copy-start | bytes 4718596
  307.1 49.7 %slice-start = ((s8[6291456]{0:T(1024)(128)(4,1)}), s8[2097152]{0:T(1024)(128)(4,1)S(1)}, s32[]{:S(2)}) async-start(s8[6291456]{0:T(1024)(128)(4,1)} %bitcast.30), calls=%async_computation.1 | async-start | bytes 4194304
  335.6 11.8 %copy-start.9 = (bf16[2048,1024]{1,0:T(8,128)(2,1)S(1)}, bf16[2048,1024]{1,0:T(8,128)(2,1)}, u32[]{:S(2)}) copy-start(bf16[2048,1024]{1,0:T(8,128)(2,1)} %copy-done.8) | copy-start | bytes 12582916
  335.6 11.8 %copy-start.42 = (bf16[2048,1536]{1,0:T(8,128)(2,1)S(1)}, bf16[2048,1536]{1,0:T(8,128)(2,1)}, u32[]{:S(2)}) copy-start(bf16[2048,1536]{1,0:T(8,128)(2,1)} %get-tuple-element.24) | copy-start | bytes 18874372
  335.6 21.2 %slice-start.1 = ((s8[6291456]{0:T(1024)(128)(4,1)}), s8[4194304]{0:T(1024)(128)(4,1)S(1)}, s32[]{:S(2)}) async-start(s8[6291456]{0:T(1024)(128)(4,1)} %bitcast.30), calls=%async_computation.2 | async-start | bytes 8388608
  347.4 9.4 %collective-permute-start.14 = (bf16[1024,1024]{1,0:T(8,128)(2,1)}, bf16[1024,1024]{1,0:T(8,128)(2,1)}, u32[]{:S(2)}, u32[]{:S(2)}) collective-permute-start(bf16[1024,1024]{1,0:T(8,128)(2,1)} %fusion.39), channel_id=1, source_target_pairs={{0,1},{1,0},{2,3},{3,2},{4,5},{5,4},{6,7},{7,6},{8,9},{9,8},{10,11... | collective-permute-start | bytes 6291464 | tf_op jit(solution)/shard_map/ppermute | solution.py:335
  347.4 9.4 %copy-start.1 = (f32[1024,1024]{1,0:T(8,128)S(1)}, f32[1024,1024]{1,0:T(8,128)}, u32[]{:S(2)}) copy-start(f32[1024,1024]{1,0:T(8,128)} %copy-done) | copy-start | bytes 12582916
  356.1 11.1 %copy-start.2 = (bf16[1024,1024]{1,0:T(8,128)(2,1)S(1)}, bf16[1024,1024]{1,0:T(8,128)(2,1)}, u32[]{:S(2)}) copy-start(bf16[1024,1024]{1,0:T(8,128)(2,1)} %param.27) | copy-start | bytes 6291460
  356.1 37.1 %collective-permute-start.28 = (bf16[768,1024]{1,0:T(8,128)(2,1)}, bf16[768,1024]{1,0:T(8,128)(2,1)}, u32[]{:S(2)}, u32[]{:S(2)}) collective-permute-start(bf16[768,1024]{1,0:T(8,128)(2,1)} %constant_dynamic-slice_fusion.1), channel_id=1, source_target_pairs={{0,2},{2,0},{1,3},{3,1},{4,6},{6,4},{5,7},{7,5},{8,10},{10,8},{9,1... | collective-permute-start | bytes 4718600 | tf_op jit(solution)/shard_map/ppermute | solution.py:335
  369.1 29.7 %copy-start.19 = (bf16[1024,1024]{1,0:T(8,128)(2,1)}, bf16[1024,1024]{1,0:T(8,128)(2,1)S(1)}, u32[]{:S(2)}) copy-start(bf16[1024,1024]{1,0:T(8,128)(2,1)S(1)} %fusion.53) | copy-start | bytes 6291460
  369.1 29.7 %collective-permute-start.15 = (bf16[1024,1024]{1,0:T(8,128)(2,1)S(1)}, bf16[1024,1024]{1,0:T(8,128)(2,1)S(1)}, u32[]{:S(2)}, u32[]{:S(2)}) collective-permute-start(bf16[1024,1024]{1,0:T(8,128)(2,1)S(1)} %fusion.53), channel_id=1, source_target_pairs={{0,1},{1,0},{2,3},{3,2},{4,5},{5,4},{6,7},{7,6},{8,9},{9,8},{10,11... | collective-permute-start | bytes 6291464 | tf_op jit(solution)/shard_map/ppermute | solution.py:335
  390.6 8.3 copy-start.27
  390.6 8.3 copy-start.32
  390.6 118.9 %collective-permute-start.24 = (bf16[512,3072]{1,0:T(8,128)(2,1)S(1)}, bf16[512,3072]{1,0:T(8,128)(2,1)}, u32[]{:S(2)}, u32[]{:S(2)}) collective-permute-start(bf16[512,3072]{1,0:T(8,128)(2,1)S(1)} %constant_dynamic-slice_fusion.4), channel_id=1, source_target_pairs={{0,2},{2,0},{1,3},{3,1},{4,6},{6,4},{5,7},{7,5},{8,10},{10,8},{9,1... | collective-permute-start | bytes 9437192 | tf_op jit(solution)/shard_map/ppermute | solution.py:335
  397.4 117.8 %collective-permute-start.29 = (bf16[384,1024]{1,0:T(8,128)(2,1)}, bf16[384,1024]{1,0:T(8,128)(2,1)}, u32[]{:S(2)}, u32[]{:S(2)}) collective-permute-start(bf16[384,1024]{1,0:T(8,128)(2,1)} %constant_dynamic-slice_fusion), channel_id=1, source_target_pairs={{0,4},{4,0},{8,12},{12,8},{16,20},{20,16},{24,28},{28,24},{1,5},{5... | collective-permute-start | bytes 2359304 | tf_op jit(solution)/shard_map/ppermute | solution.py:335
  485.0 16.9 %copy-start.15 = (bf16[2048,1024]{1,0:T(8,128)(2,1)S(1)}, bf16[2048,1024]{1,0:T(8,128)(2,1)}, u32[]{:S(2)}) copy-start(bf16[2048,1024]{1,0:T(8,128)(2,1)} %get-tuple-element.23.o_ref) | copy-start | bytes 12582916
  485.0 16.9 %copy-start.20 = (bf16[1024,1024]{1,0:T(8,128)(2,1)S(1)}, bf16[1024,1024]{1,0:T(8,128)(2,1)}, u32[]{:S(2)}) copy-start(bf16[1024,1024]{1,0:T(8,128)(2,1)} %copy-done.19) | copy-start | bytes 6291460
  485.0 16.9 %copy-start.44 = (bf16[1024,1024]{1,0:T(8,128)(2,1)S(1)}, bf16[1024,1024]{1,0:T(8,128)(2,1)}, u32[]{:S(2)}) copy-start(bf16[1024,1024]{1,0:T(8,128)(2,1)} %copy-done.43) | copy-start | bytes 6291460
  499.8 9.7 %slice-start.2 = ((s8[6291456]{0:T(1024)(128)(4,1)}), s8[4194304]{0:T(1024)(128)(4,1)S(1)}, s32[]{:S(2)}) async-start(s8[6291456]{0:T(1024)(128)(4,1)} %bitcast.32), calls=%async_computation.3 | async-start | bytes 8388608
  501.2 8.2 slice-start.3
  501.2 71.6 %collective-permute-start.17 = (bf16[512,2048]{1,0:T(8,128)(2,1)}, bf16[512,2048]{1,0:T(8,128)(2,1)}, u32[]{:S(2)}, u32[]{:S(2)}) collective-permute-start(bf16[512,2048]{1,0:T(8,128)(2,1)} %constant_dynamic-slice_fusion.9), channel_id=1, source_target_pairs={{0,2},{2,0},{1,3},{3,1},{4,6},{6,4},{5,7},{7,5},{8,10},{10,8},{9,1... | collective-permute-start | bytes 6291464 | tf_op jit(solution)/shard_map/ppermute | solution.py:335
  508.0 62.9 %collective-permute-start.21 = (bf16[512,1024]{1,0:T(8,128)(2,1)}, bf16[512,1024]{1,0:T(8,128)(2,1)}, u32[]{:S(2)}, u32[]{:S(2)}) collective-permute-start(bf16[512,1024]{1,0:T(8,128)(2,1)} %constant_dynamic-slice_fusion.6), channel_id=1, source_target_pairs={{0,2},{2,0},{1,3},{3,1},{4,6},{6,4},{5,7},{7,5},{8,10},{10,8},{9,1... | collective-permute-start | bytes 3145736 | tf_op jit(solution)/shard_map/ppermute | solution.py:335
  513.8 63.8 %collective-permute-start.25 = (bf16[256,3072]{1,0:T(8,128)(2,1)}, bf16[256,3072]{1,0:T(8,128)(2,1)}, u32[]{:S(2)}, u32[]{:S(2)}) collective-permute-start(bf16[256,3072]{1,0:T(8,128)(2,1)} %constant_dynamic-slice_fusion.3), channel_id=1, source_target_pairs={{0,4},{4,0},{8,12},{12,8},{16,20},{20,16},{24,28},{28,24},{1,5},{5... | collective-permute-start | bytes 4718600 | tf_op jit(solution)/shard_map/ppermute | solution.py:335
  515.2 57.7 %copy-start.14 = (bf16[1024,2048]{1,0:T(8,128)(2,1)S(1)}, bf16[1024,2048]{1,0:T(8,128)(2,1)}, u32[]{:S(2)}) copy-start(bf16[1024,2048]{1,0:T(8,128)(2,1)} %copy-done.13) | copy-start | bytes 12582916
  575.4 35.8 %collective-permute-start.18 = (bf16[256,2048]{1,0:T(8,128)(2,1)S(1)}, bf16[256,2048]{1,0:T(8,128)(2,1)S(1)}, u32[]{:S(2)}, u32[]{:S(2)}) collective-permute-start(bf16[256,2048]{1,0:T(8,128)(2,1)S(1)} %constant_dynamic-slice_fusion.8), channel_id=1, source_target_pairs={{0,4},{4,0},{8,12},{12,8},{16,20},{20,16},{24,28},{28,24},{1,5},{5... | collective-permute-start | bytes 3145736 | tf_op jit(solution)/shard_map/ppermute | solution.py:335
  576.1 34.1 %collective-permute-start.22 = (bf16[256,1024]{1,0:T(8,128)(2,1)S(1)}, bf16[256,1024]{1,0:T(8,128)(2,1)S(1)}, u32[]{:S(2)}, u32[]{:S(2)}) collective-permute-start(bf16[256,1024]{1,0:T(8,128)(2,1)S(1)} %constant_dynamic-slice_fusion.5), channel_id=1, source_target_pairs={{0,4},{4,0},{8,12},{12,8},{16,20},{20,16},{24,28},{28,24},{1,5},{5... | collective-permute-start | bytes 1572872 | tf_op jit(solution)/shard_map/ppermute | solution.py:335
  611.2 10.9 %slice-start.4 = ((s8[6291456]{0:T(1024)(128)(4,1)}), s8[2097152]{0:T(1024)(128)(4,1)S(1)}, s32[]{:S(2)}) async-start(s8[6291456]{0:T(1024)(128)(4,1)} %bitcast.43), calls=%async_computation.5 | async-start | bytes 4194304
  612.6 9.5 %copy-start.7 = (bf16[1536,1024]{1,0:T(8,128)(2,1)S(1)}, bf16[1536,1024]{1,0:T(8,128)(2,1)}, u32[]{:S(2)}) copy-start(bf16[1536,1024]{1,0:T(8,128)(2,1)} %maximum_select_fusion.6.wd_ref) | copy-start | bytes 9437188
  612.6 9.5 %slice-start.5 = ((s8[6291456]{0:T(1024)(128)(4,1)}), s8[4194304]{0:T(1024)(128)(4,1)S(1)}, s32[]{:S(2)}) async-start(s8[6291456]{0:T(1024)(128)(4,1)} %bitcast.43), calls=%async_computation.6 | async-start | bytes 8388608
  622.1 10.6 %collective-permute-start.16 = (bf16[1024,1024]{1,0:T(8,128)(2,1)}, bf16[1024,1024]{1,0:T(8,128)(2,1)}, u32[]{:S(2)}, u32[]{:S(2)}) collective-permute-start(bf16[1024,1024]{1,0:T(8,128)(2,1)} %fusion.36), channel_id=1, source_target_pairs={{0,1},{1,0},{2,3},{3,2},{4,5},{5,4},{6,7},{7,6},{8,9},{9,8},{10,11... | collective-permute-start | bytes 6291464 | tf_op jit(solution)/shard_map/ppermute | solution.py:335
  626.8 136.7 %collective-permute-start.13 = (bf16[1024,1024]{1,0:T(8,128)(2,1)}, bf16[1024,1024]{1,0:T(8,128)(2,1)}, u32[]{:S(2)}, u32[]{:S(2)}) collective-permute-start(bf16[1024,1024]{1,0:T(8,128)(2,1)} %fusion.33), channel_id=1, source_target_pairs={{0,1},{1,0},{2,3},{3,2},{4,5},{5,4},{6,7},{7,6},{8,9},{9,8},{10,11... | collective-permute-start | bytes 6291464 | tf_op jit(solution)/shard_map/ppermute | solution.py:335
  632.7 130.8 %copy-start.3 = (bf16[1024,1024]{1,0:T(8,128)(2,1)S(1)}, bf16[1024,1024]{1,0:T(8,128)(2,1)}, u32[]{:S(2)}) copy-start(bf16[1024,1024]{1,0:T(8,128)(2,1)} %param.27) | copy-start | bytes 6291460
  761.5 95.9 %collective-permute-start.19 = (bf16[256,2048]{1,0:T(8,128)(2,1)}, bf16[256,2048]{1,0:T(8,128)(2,1)}, u32[]{:S(2)}, u32[]{:S(2)}) collective-permute-start(bf16[256,2048]{1,0:T(8,128)(2,1)} %get-tuple-element.35), channel_id=1, source_target_pairs={{0,4},{4,0},{8,12},{12,8},{16,20},{20,16},{24,28},{28,24},{1,5},{5... | collective-permute-start | bytes 3145736 | tf_op jit(solution)/shard_map/ppermute | solution.py:335
  762.9 123.7 %collective-permute-start.26 = (bf16[256,3072]{1,0:T(8,128)(2,1)}, bf16[256,3072]{1,0:T(8,128)(2,1)}, u32[]{:S(2)}, u32[]{:S(2)}) collective-permute-start(bf16[256,3072]{1,0:T(8,128)(2,1)} %get-tuple-element.37), channel_id=1, source_target_pairs={{0,4},{4,0},{8,12},{12,8},{16,20},{20,16},{24,28},{28,24},{1,5},{5... | collective-permute-start | bytes 4718600 | tf_op jit(solution)/shard_map/ppermute | solution.py:335
  763.5 93.9 %copy-start.25 = (bf16[256,2048]{1,0:T(8,128)(2,1)S(1)}, bf16[256,2048]{1,0:T(8,128)(2,1)}, u32[]{:S(2)}) copy-start(bf16[256,2048]{1,0:T(8,128)(2,1)} %get-tuple-element.35) | copy-start | bytes 3145732
  852.7 31.8 %collective-permute-start.30 = (bf16[384,1024]{1,0:T(8,128)(2,1)}, bf16[384,1024]{1,0:T(8,128)(2,1)S(1)}, u32[]{:S(2)}, u32[]{:S(2)}) collective-permute-start(bf16[384,1024]{1,0:T(8,128)(2,1)} %get-tuple-element.38), channel_id=1, source_target_pairs={{0,4},{4,0},{8,12},{12,8},{16,20},{20,16},{24,28},{28,24},{1,5},{5... | collective-permute-start | bytes 2359304 | tf_op jit(solution)/shard_map/ppermute | solution.py:335
  857.4 25.3 %copy-start.30 = (bf16[256,1024]{1,0:T(8,128)(2,1)S(1)}, bf16[256,1024]{1,0:T(8,128)(2,1)}, u32[]{:S(2)}) copy-start(bf16[256,1024]{1,0:T(8,128)(2,1)} %get-tuple-element.36) | copy-start | bytes 1572868
  857.4 25.3 %collective-permute-start.23 = (bf16[256,1024]{1,0:T(8,128)(2,1)}, bf16[256,1024]{1,0:T(8,128)(2,1)S(1)}, u32[]{:S(2)}, u32[]{:S(2)}) collective-permute-start(bf16[256,1024]{1,0:T(8,128)(2,1)} %get-tuple-element.36), channel_id=1, source_target_pairs={{0,4},{4,0},{8,12},{12,8},{16,20},{20,16},{24,28},{28,24},{1,5},{5... | collective-permute-start | bytes 1572872 | tf_op jit(solution)/shard_map/ppermute | solution.py:335
  859.8 24.6 %copy-start.29 = (bf16[384,1024]{1,0:T(8,128)(2,1)S(1)}, bf16[384,1024]{1,0:T(8,128)(2,1)}, u32[]{:S(2)}) copy-start(bf16[384,1024]{1,0:T(8,128)(2,1)} %get-tuple-element.38) | copy-start | bytes 2359300
  859.9 29.5 %collective-permute-start.20 = (bf16[256,2048]{1,0:T(8,128)(2,1)S(1)}, bf16[256,2048]{1,0:T(8,128)(2,1)S(1)}, u32[]{:S(2)}, u32[]{:S(2)}) collective-permute-start(bf16[256,2048]{1,0:T(8,128)(2,1)S(1)} %constant_dynamic-slice_fusion.7), channel_id=1, source_target_pairs={{0,1},{1,0},{2,3},{3,2},{4,5},{5,4},{6,7},{7,6},{8,9},{9,8},{10,11... | collective-permute-start | bytes 3145736 | tf_op jit(solution)/shard_map/ppermute | solution.py:335
  889.3 3.5 collective-permute-start.27
  (21 other events, 81.1 us)
Sparse Core Ops, SparseCore 0:
  612.7 148.7 all-reduce.3

commit v2 on v1

v2 whole, which is shorter than its diff:
```python
import functools

import jax
import jax.numpy as jnp
from jax import lax
from jax.experimental import pallas as pl
from jax.experimental.pallas import tpu as pltpu
from jax.sharding import PartitionSpec as P

HQ = 16
KV = 8
HD = 128
EPSILON = 1e-06
ROPE_BASE = 1000000.0
SCALE = HD**-0.5
LOG2E = 1.4426950408889634
BLK = 256
BF = jnp.bfloat16
F32 = jnp.float32


def nn(a, b):
    return lax.dot_general(a, b, (((1,), (0,)), ((), ())), preferred_element_type=F32)


def nt(a, b):
    return lax.dot_general(a, b, (((1,), (1,)), ((), ())), preferred_element_type=F32)


def tn(a, b):
    return lax.dot_general(a, b, (((0,), (0,)), ((), ())), preferred_element_type=F32)


def cost(micros):
    return pl.CostEstimate(flops=int(micros * 1.0e7), transcendentals=0, bytes_accessed=0)


def full_spec(shape):
    return pl.BlockSpec(shape, lambda *_: (0,) * len(shape), pipeline_mode=pl.Buffered(1))


class Weight:
    def __init__(self, pieces, base):
        self.pieces = [p for p, _ in pieces]
        self.starts = [s for _, s in pieces]
        self.base = base
        self.shape = (sum(p.shape[0] for p in self.pieces), self.pieces[0].shape[1])


def tiled(name, body, steps, info, inputs, weights, outputs, micros):
    n_in, n_out = len(inputs), len(outputs)
    pieces = [p for w in weights for p in w.pieces]

    def kernel(info_ref, *refs):
        ins = refs[:n_in]
        parts = refs[n_in : n_in + len(pieces)]
        outs = refs[n_in + len(pieces) : n_in + len(pieces) + n_out]
        rest = refs[n_in + len(pieces) + n_out :]
        held, sems = rest[: len(weights)], rest[len(weights) :]

        if pieces:

            @pl.when(pl.program_id(0) == 0)
            def _():
                copies = []
                at = 0
                for n, w in enumerate(weights):
                    for k, piece in enumerate(w.pieces):
                        first = pl.multiple_of(info_ref[w.base + k], 128)
                        target = held[n].at[pl.ds(first, piece.shape[0]), :]
                        copies.append(pltpu.make_async_copy(parts[at], target, sems[0].at[at]))
                        at += 1
                for copy in copies:
                    copy.start()
                for copy in copies:
                    copy.wait()

        body(info_ref, ins, held, outs)

    scratch = [pltpu.VMEM(w.shape, BF) for w in weights]
    if pieces:
        scratch.append(pltpu.SemaphoreType.DMA((len(pieces),)))
    return pl.pallas_call(
        kernel,
        grid_spec=pltpu.PrefetchScalarGridSpec(
            num_scalar_prefetch=1,
            grid=(steps,),
            in_specs=[pl.BlockSpec(block, index) for _, block, index in inputs]
            + [pl.BlockSpec(memory_space=pl.ANY)] * len(pieces),
            out_specs=[pl.BlockSpec(block, index) for _, block, index in outputs],
            scratch_shapes=scratch,
        ),
        out_shape=[shape for shape, _, _ in outputs],
        cost_estimate=cost(micros),
        name=name,
    )(info, *[a for a, _, _ in inputs], *pieces)


def struct(rows, cols, dtype=BF):
    return jax.ShapeDtypeStruct((rows, cols), dtype)


def at_row(t, i):
    return (t, 0)


def once(t, i):
    return (0, 0)


def block(array, index=at_row):
    return (array, (BLK, array.shape[1]), index)


def const(array):
    return (array, array.shape, once)


def result(rows, cols, dtype=BF, index=at_row):
    return (struct(rows, cols, dtype), (BLK, cols), index)


class Order:
    def __init__(self, rows):
        self.half = rows // BLK

    def own(self, t, i):
        return (t + self.half * i[0], 0)

    def other(self, t, i):
        return (t + self.half * (1 - i[0]), 0)

    def global_(self, t, i):
        return ((t + self.half * i[0]) % (2 * self.half), 0)

    def first(self, t, i):
        return (jnp.minimum(t, self.half - 1), 0)

    def second(self, t, i):
        return (jnp.maximum(t - self.half, 0), 0)

    def later(self, t, i):
        return (t + self.half, 0)


def both(order, a, b):
    return jnp.where(pl.program_id(0) < order.half, a[...], b[...])


def project(order, info, tokens, other, gain, weight, cosine, sine, head_gains):
    rows, width = tokens.shape
    cols = weight.shape[1]

    def body(info_ref, ins, held, outs):
        own_ref, other_ref, gain_ref, cos_ref, sin_ref, hg_ref = ins
        normed_ref, qkv_ref, raw_ref = outs
        x = both(order, own_ref, other_ref).astype(F32)
        scale = lax.rsqrt(jnp.mean(x * x, axis=1, keepdims=True) + EPSILON)
        normed = (x * scale * gain_ref[...]).astype(BF)
        normed_ref[...] = normed
        cos_tab, sin_tab = cos_ref[...], sin_ref[...]
        for g in range(cols // 512):
            acc = nn(normed, held[0][:, g * 512 : (g + 1) * 512])
            for h in range(3):
                t = acc[:, h * HD : (h + 1) * HD]
                head_gain = hg_ref[0:1, :] if h < 2 else hg_ref[1:2, :]
                n = t * lax.rsqrt(jnp.mean(t * t, axis=1, keepdims=True) + EPSILON) * head_gain
                turned = n * cos_tab + pltpu.roll(n, HD // 2, 1) * sin_tab
                qkv_ref[:, g * 512 + h * HD : g * 512 + (h + 1) * HD] = turned.astype(BF)
                raw_ref[:, g * 384 + h * HD : g * 384 + (h + 1) * HD] = t.astype(BF)
            qkv_ref[:, g * 512 + 384 : (g + 1) * 512] = acc[:, 384:].astype(BF)

    place = order.global_
    return tiled(
        "project",
        body,
        2 * order.half,
        info,
        [
            block(tokens, order.first),
            block(other, order.second),
            const(gain),
            block(cosine, place),
            block(sine, place),
            const(head_gains),
        ],
        [weight],
        [
            result(2 * rows, width, BF, place),
            result(2 * rows, cols, BF, place),
            result(2 * rows, cols // 4 * 3, BF, place),
        ],
        17,
    )


def times(name, order, info, inputs, index, weight, transposed, micros):
    rows = inputs[0].shape[0] // 2
    cols = weight.shape[0] if transposed else weight.shape[1]

    def body(info_ref, ins, held, outs):
        outs[0][...] = product(ins, held[0], transposed).astype(BF)

    return tiled(
        name,
        body,
        order.half,
        info,
        [block(a, index) for a in inputs],
        [weight],
        [result(rows, cols)],
        micros,
    )[0]


def product(ins, held, transposed):
    total = None
    at = 0
    for a in ins:
        size = a.shape[1]
        if transposed:
            term = nt(a[...], held[:, at : at + size])
        else:
            term = nn(a[...], held[at : at + size, :])
        total = term if total is None else total + term
        at += size
    return total


def mix_own(order, info, attended, tokens, got, gain, weight):
    rows, width = tokens.shape

    def body(info_ref, ins, held, outs):
        att_ref, tok_ref, got_ref, gain_ref = ins
        middle = (
            tok_ref[...].astype(F32) + nn(att_ref[...], held[0][...]) + got_ref[...].astype(F32)
        )
        outs[0][...] = middle
        scale = lax.rsqrt(jnp.mean(middle * middle, axis=1, keepdims=True) + EPSILON)
        outs[1][...] = (middle * scale * gain_ref[...]).astype(BF)

    return tiled(
        "mix_own",
        body,
        order.half,
        info,
        [block(attended, order.own), block(tokens), block(got), const(gain)],
        [weight],
        [result(rows, width, F32), result(rows, width)],
        6,
    )


def mlp(order, info, m_own, m_other, g_own, g_other, w_gu, w_down):
    rows, width = m_own.shape
    half = w_down.shape[0]
    step = 512

    def body(info_ref, ins, held, outs):
        hid_ref, dgu_ref, m_ref, g_ref = outs
        gu, down = held
        m = both(order, ins[0], ins[1])
        g = both(order, ins[2], ins[3])
        m_ref[...] = m
        g_ref[...] = g
        for n in range(0, half, step):
            gate = nn(m, gu[:, n : n + step])
            up = nn(m, gu[:, half + n : half + n + step])
            dh = nt(g, down[n : n + step, :])
            sig = 1.0 / (1.0 + jnp.exp(-gate))
            act = gate * sig
            hid_ref[:, n : n + step] = (act * up).astype(BF)
            dgu_ref[:, n : n + step] = (dh * up * (sig + act * (1.0 - sig))).astype(BF)
            dgu_ref[:, half + n : half + n + step] = (dh * act).astype(BF)

    return tiled(
        "mlp",
        body,
        2 * order.half,
        info,
        [
            block(m_own, order.first),
            block(m_other, order.second),
            block(g_own, order.first),
            block(g_other, order.second),
        ],
        [w_gu, w_down],
        [
            result(2 * rows, half),
            result(2 * rows, 2 * half),
            result(2 * rows, width),
            result(2 * rows, width),
        ],
        30,
    )


def norm_back(d, v, gain):
    r = lax.rsqrt(jnp.mean(v * v, axis=1, keepdims=True) + EPSILON)
    n = v * r
    scaled = d * gain
    dv = r * (scaled - n * jnp.mean(scaled * n, axis=1, keepdims=True))
    return dv, jnp.sum(d * n, axis=0, keepdims=True)


def add_over_steps(ref, value):
    @pl.when(pl.program_id(0) == 0)
    def _():
        ref[...] = value

    @pl.when(pl.program_id(0) > 0)
    def _():
        ref[...] += value


def branch_own(order, info, d_gu, got, middle, cot, gain, weight):
    rows, width = middle.shape

    def body(info_ref, ins, held, outs):
        d_ref, got_ref, mid_ref, cot_ref, gain_ref = ins
        d = product([d_ref], held[0], True) + got_ref[...].astype(F32)
        dv, dg = norm_back(d, mid_ref[...], gain_ref[...])
        d_middle = cot_ref[...].astype(F32) + dv
        outs[0][...] = d_middle
        outs[1][...] = d_middle.astype(BF)
        add_over_steps(outs[2], dg)

    return tiled(
        "branch_own",
        body,
        order.half,
        info,
        [block(d_gu), block(got), block(middle), block(cot), const(gain)],
        [weight],
        [
            result(rows, width, F32),
            result(rows, width),
            (struct(1, width, F32), (1, width), once),
        ],
        11,
    )


def attended_back(order, info, own, other, weight):
    rows, width = own.shape

    def body(info_ref, ins, held, outs):
        branch = both(order, ins[0], ins[1])
        outs[1][...] = branch
        outs[0][...] = nt(branch, held[0][...]).astype(BF)

    place = order.global_
    return tiled(
        "attended_back",
        body,
        2 * order.half,
        info,
        [block(own, order.first), block(other, order.second)],
        [weight],
        [result(2 * rows, weight.shape[0], BF, place), result(2 * rows, width, BF, place)],
        8,
    )


def tokens_own(order, info, d_parts, got, tokens, d_middle, gain, weight):
    rows, width = tokens.shape

    def body(info_ref, ins, held, outs):
        parts, (got_ref, tok_ref, mid_ref, gain_ref) = ins[: len(d_parts)], ins[len(d_parts) :]
        d = product(parts, held[0], True) + got_ref[...].astype(F32)
        dv, dg = norm_back(d, tok_ref[...].astype(F32), gain_ref[...])
        outs[0][...] = mid_ref[...] + dv
        add_over_steps(outs[1], dg)

    return tiled(
        "tokens_own",
        body,
        order.half,
        info,
        [block(d, order.own) for d in d_parts]
        + [block(got), block(tokens), block(d_middle), const(gain)],
        [weight],
        [result(rows, width, F32), (struct(1, width, F32), (1, width), once)],
        9,
    )


def output_own(order, info, hidden, middle, got, weight):
    rows, width = middle.shape

    def body(info_ref, ins, held, outs):
        hid_ref, mid_ref, got_ref = ins
        total = mid_ref[...] + nn(hid_ref[...], held[0][...]) + got_ref[...].astype(F32)
        outs[0][...] = total.astype(BF)

    return tiled(
        "output_own",
        body,
        order.half,
        info,
        [block(hidden), block(middle), block(got)],
        [weight],
        [result(rows, width)],
        6,
    )[0]


def stack_heads(block):
    return jnp.concatenate([block[:, :HD], block[:, HD:]], axis=0)


def attend_kernel(low_ref, qkv_ref, start_ref, out_ref, lse_ref, acc, total):
    blocks = qkv_ref.shape[0] // BLK

    def query_block(qb, carry):
        r0 = pl.multiple_of(qb * BLK, BLK)
        q2 = stack_heads(qkv_ref[pl.ds(r0, BLK), 0:256])
        first = start_ref[pl.ds(r0, BLK), :]
        first2 = jnp.concatenate([first, first], axis=0)

        def tile(k0, diagonal):
            k = qkv_ref[pl.ds(k0, BLK), 256:384]
            v = qkv_ref[pl.ds(k0, BLK), 384:512]
            s = nt(q2, k) * (SCALE * LOG2E)
            col = lax.broadcasted_iota(jnp.int32, (2 * BLK, BLK), 1)
            mask = col >= first2 - k0
            if diagonal:
                row = lax.broadcasted_iota(jnp.int32, (2 * BLK, BLK), 0) & (BLK - 1)
                mask = mask & (col <= row)
            p = jnp.where(mask, jnp.exp2(s), 0.0)
            part = p[:, :HD]
            for n in range(1, BLK // HD):
                part = part + p[:, n * HD : (n + 1) * HD]
            return part, nn(p.astype(BF), v)

        part, mixed = tile(r0, True)
        total[...] = part
        acc[...] = mixed

        def step(kb, inner):
            more, mixed_more = tile(pl.multiple_of(kb * BLK, BLK), False)
            total[...] += more
            acc[...] += mixed_more
            return inner

        lax.fori_loop(low_ref[qb], qb, step, 0)
        sums = total[...]
        o = (acc[...] / jnp.sum(sums, axis=1, keepdims=True)).astype(BF)
        out_ref[pl.ds(r0, BLK), 0:HD] = o[:BLK]
        out_ref[pl.ds(r0, BLK), HD : 2 * HD] = o[BLK:]
        line = jnp.log2(jnp.sum(jnp.transpose(sums), axis=0, keepdims=True))
        lse_ref[0, 0:1, pl.ds(r0, BLK)] = line[:, :BLK]
        lse_ref[0, 1:2, pl.ds(r0, BLK)] = line[:, BLK:]
        return carry

    lax.fori_loop(0, blocks, query_block, 0)


def attend(low, qkv, start, at, groups, earlier=None):
    length, cols = qkv.shape
    whole = cols // 512
    anywhere = [pl.BlockSpec(memory_space=pl.ANY)] * (2 if earlier else 0)

    def body(low_ref, qkv_ref, start_ref, *rest):
        attend_kernel(low_ref, qkv_ref, start_ref, *rest[len(anywhere) :])

    return pl.pallas_call(
        body,
        grid_spec=pltpu.PrefetchScalarGridSpec(
            num_scalar_prefetch=1,
            grid=(groups,),
            in_specs=[
                pl.BlockSpec((length, 512), lambda g, low: (0, g + at)),
                full_spec((length, 1)),
                *anywhere,
            ],
            out_specs=[
                pl.BlockSpec((length, 256), lambda g, low: (0, g + at)),
                pl.BlockSpec((1, 2, length), lambda g, low: (g + at, 0, 0)),
            ],
            scratch_shapes=[
                pltpu.VMEM((2 * BLK, HD), F32),
                pltpu.VMEM((2 * BLK, HD), F32),
            ],
        ),
        out_shape=[
            jax.ShapeDtypeStruct((length, whole * 256), BF),
            jax.ShapeDtypeStruct((whole, 2, length), F32),
        ],
        input_output_aliases={3: 0, 4: 1} if earlier else {},
        cost_estimate=cost(11.5 * groups),
        name="attend",
    )(low, qkv, start.reshape(length, 1), *(earlier or ()))


def head_back(d, raw, gain, cosine, sine):
    dn = d * cosine + pltpu.roll(d * sine, HD // 2, 1)
    raw = raw.astype(F32)
    r = lax.rsqrt(jnp.mean(raw * raw, axis=1, keepdims=True) + EPSILON)
    n = raw * r
    dg = jnp.sum(dn * n, axis=0, keepdims=True)
    scaled = dn * gain
    dv = r * (scaled - n * jnp.mean(scaled * n, axis=1, keepdims=True))
    return dv.astype(BF), dg


def attend_back_kernel(
    low_ref,
    qkv_ref,
    do_ref,
    o_ref,
    lse_ref,
    start_ref,
    raw_ref,
    cos_ref,
    sin_ref,
    hg_ref,
    out_ref,
    dg_ref,
    dk_acc,
    dv_acc,
    dq_acc,
):
    blocks = qkv_ref.shape[0] // BLK
    dg_ref[...] = jnp.zeros_like(dg_ref)

    def query_block(qb, carry):
        r0 = pl.multiple_of(qb * BLK, BLK)
        rows = pl.ds(r0, BLK)
        q2 = stack_heads(qkv_ref[rows, 0:256])
        do2 = stack_heads(do_ref[rows, :])
        o2 = stack_heads(o_ref[rows, :])
        delta = jnp.sum(jnp.transpose(do2.astype(F32) * o2.astype(F32)), axis=0, keepdims=True)
        lse = jnp.concatenate([lse_ref[0, 0:1, rows], lse_ref[0, 1:2, rows]], axis=1)
        first = start_ref[0:1, rows]
        first2 = jnp.concatenate([first, first], axis=1)

        def tile(k0, diagonal):
            k = qkv_ref[pl.ds(k0, BLK), 256:384]
            v = qkv_ref[pl.ds(k0, BLK), 384:512]
            key = lax.broadcasted_iota(jnp.int32, (BLK, 2 * BLK), 0)
            mask = key >= first2 - k0
            if diagonal:
                query = lax.broadcasted_iota(jnp.int32, (BLK, 2 * BLK), 1) & (BLK - 1)
                mask = mask & (key <= query)
            p = jnp.where(mask, jnp.exp2(nt(k, q2) * (SCALE * LOG2E) - lse), 0.0)
            ds = (p * (nt(v, do2) - delta)).astype(BF)
            return nn(ds, q2), nn(p.astype(BF), do2), tn(ds, k)

        dk, dv, dq = tile(r0, True)
        dk_acc[rows, :] = dk
        dv_acc[rows, :] = dv
        dq_acc[...] = dq

        def step(kb, inner):
            k0 = pl.multiple_of(kb * BLK, BLK)
            dk, dv, dq = tile(k0, False)
            dk_acc[pl.ds(k0, BLK), :] += dk
            dv_acc[pl.ds(k0, BLK), :] += dv
            dq_acc[...] += dq
            return inner

        lax.fori_loop(low_ref[qb], qb, step, 0)
        cosine = cos_ref[rows, :]
        sine = sin_ref[rows, :]
        for h in range(2):
            d_raw, dg = head_back(
                dq_acc[h * BLK : (h + 1) * BLK, :] * SCALE,
                raw_ref[rows, h * HD : (h + 1) * HD],
                hg_ref[0:1, :],
                cosine,
                sine,
            )
            out_ref[rows, h * HD : (h + 1) * HD] = d_raw
            dg_ref[0:1, :] += dg
        return carry

    lax.fori_loop(0, blocks, query_block, 0)

    def key_block(kb, carry):
        rows = pl.ds(pl.multiple_of(kb * BLK, BLK), BLK)
        d_raw, dg = head_back(
            dk_acc[rows, :] * SCALE,
            raw_ref[rows, 256:384],
            hg_ref[1:2, :],
            cos_ref[rows, :],
            sin_ref[rows, :],
        )
        out_ref[rows, 256:384] = d_raw
        out_ref[rows, 384:512] = dv_acc[rows, :].astype(BF)
        dg_ref[1:2, :] += dg
        return carry

    lax.fori_loop(0, blocks, key_block, 0)


def attend_back(low, qkv, d_att, att, lse, start, raw, cosine, sine, head_gains, at, earlier):
    length = qkv.shape[0]
    anywhere = [] if earlier is None else [pl.BlockSpec(memory_space=pl.ANY)]

    def body(*refs):
        attend_back_kernel(*refs[:10], *refs[10 + len(anywhere) :])

    column = lambda n: pl.BlockSpec((length, n), lambda g, low: (0, g + at))
    return pl.pallas_call(
        body,
        grid_spec=pltpu.PrefetchScalarGridSpec(
            num_scalar_prefetch=1,
            grid=(1,),
            in_specs=[
                column(512),
                column(256),
                column(256),
                pl.BlockSpec((1, 2, length), lambda g, low: (g + at, 0, 0)),
                full_spec((1, length)),
                column(384),
                full_spec((length, HD)),
                full_spec((length, HD)),
                full_spec((2, HD)),
                *anywhere,
            ],
            out_specs=[
                pl.BlockSpec((length, 512), lambda g, low: (0, at % 3)),
                pl.BlockSpec((2, HD), lambda g, low: (0, 0)),
            ],
            scratch_shapes=[
                pltpu.VMEM((length, HD), F32),
                pltpu.VMEM((length, HD), F32),
                pltpu.VMEM((2 * BLK, HD), F32),
            ],
        ),
        out_shape=[
            jax.ShapeDtypeStruct((length, 1536 if at < 3 else 512), BF),
            jax.ShapeDtypeStruct((2, HD), F32),
        ],
        input_output_aliases={} if earlier is None else {10: 0},
        cost_estimate=cost(21),
        name="attend_back",
    )(low, qkv, d_att, att, lse, start.reshape(1, length), raw, cosine, sine, head_gains, *([] if earlier is None else [earlier]))


def core_heads(c):
    return (2 * c, 2 * c + 1, 4 + 2 * c, 5 + 2 * c)


def qkv_columns(c):
    out = []
    for kv in core_heads(c):
        out += [(0, kv * 256, 256), (1, kv * HD, HD), (2, kv * HD, HD)]
    return out


def gu_columns(c, quarter):
    return [(n, k * quarter, quarter) for n in range(2) for k in (c, 2 + c)]


def pack(name, info, arrays, layout):
    rows = arrays[0].shape[0]
    cols = sum(a.shape[1] for a in arrays) // 2

    def body(info_ref, ins, held, outs):
        for c in range(2):

            @pl.when(info_ref[0] == c)
            def _():
                for target, half in ((outs[0], c), (outs[1], 1 - c)):
                    at = 0
                    for n, first, size in layout(half):
                        target[:, at : at + size] = ins[n][:, first : first + size]
                        at += size

    return tiled(
        name,
        body,
        1,
        info,
        [const(a) for a in arrays],
        [],
        [(struct(rows, cols), (rows, cols), once)] * 2,
        3,
    )


def unpack(name, info, keeps, gots, widths, layout):
    rows = keeps[0].shape[0]
    count = len(keeps)

    def body(info_ref, ins, held, outs):
        for c in range(2):

            @pl.when(info_ref[0] == c)
            def _():
                for half in range(2):
                    source = ins[:count] if half == c else ins[count:]
                    at = 0
                    for n, first, size in layout(half):
                        ref = source[at // source[0].shape[1]]
                        col = at % source[0].shape[1]
                        outs[n][:, first : first + size] = ref[:, col : col + size].astype(F32)
                        at += size

    return tiled(
        name,
        body,
        1,
        info,
        [const(a) for a in keeps + gots],
        [],
        [(struct(rows, w, F32), (rows, w), once) for w in widths],
        4,
    )


def swap(value, axis, bit=0):
    size = lax.axis_size(axis)
    return lax.ppermute(value, axis, [(i, i ^ (1 << bit)) for i in range(size)])


def ordered(first_is_mine, mine, other):
    return jnp.where(
        first_is_mine,
        jnp.concatenate([mine, other], axis=0),
        jnp.concatenate([other, mine], axis=0),
    )


def part(value, index, count, axis=0):
    size = value.shape[axis] // count
    return lax.dynamic_slice_in_dim(value, index * size, size, axis)


def gather_any(value):
    return lax.all_gather(value, ("fsdp", "seq"), axis=0, tiled=True)


def fence(*values):
    return lax.optimization_barrier(values)


class Sum:
    def __init__(self, grad, row, replica):
        self.row, self.replica = row, replica
        self.value = grad.reshape(2, 2, grad.shape[0] // 4, grad.shape[1])

    def send(self, axis):
        self.at = (0, self.row) if axis == "fsdp" else (1, self.replica % 2)
        dim, mine = self.at
        self.got = swap(part(self.value, 1 - mine, 2, dim), axis)
        return self

    def add(self):
        dim, mine = self.at
        self.value = part(self.value, mine, 2, dim) + self.got
        return self

    def flat(self):
        return self.value.reshape(-1, self.value.shape[-1])

STRIP = 512


def strips(*values):
    return jnp.concatenate(
        [v[:, at : at + STRIP] for v in values for at in range(0, v.shape[1], STRIP)], axis=0
    )


def halve(value, replica, bit):
    return swap(part(value, 1 - ((replica >> bit) & 1), 2), "rep", bit)


def add_half(value, got, replica, bit):
    return part(value, (replica >> bit) & 1, 2) + got


def double(value, got, replica, bit):
    return ordered((replica >> bit) & 1 == 0, value, got)


def finish_gu(info, values, gots, quarter):
    rows = gots[0].shape[0] * STRIP // (2 * quarter)
    piece = 256

    def body(info_ref, ins, held, outs):
        for c in range(2):
            for side in range(2):

                @pl.when((info_ref[0] == c) & (info_ref[1] == side))
                def _():
                    for n in range(2):
                        own, got = ins[2 * n + (c != side)], ins[4 + n]
                        for half, ref in ((c, own), (1 - c, got)):
                            for at in range(0, 2 * quarter, piece):
                                r, col = at // STRIP * rows, at % STRIP
                                k, to = at // quarter, at % quarter
                                to += (half + 2 * k) * quarter
                                outs[n][:, to : to + piece] = ref[
                                    r : r + rows, col : col + piece
                                ].astype(F32)

    return tiled(
        "finish_gu",
        body,
        1,
        info,
        [const(a) for pair in values for a in pair] + [const(g) for g in gots],
        [],
        [(struct(rows, 4 * quarter, F32), (rows, 4 * quarter), once)] * 2,
        5,
    )


def finish_rows(info, values, firsts, width):
    strips_n = width // STRIP
    sizes = [(v[0].shape[0] - first) // strips_n for v, first in zip(values, firsts)]

    def body(info_ref, ins, held, outs):
        for side in range(2):

            @pl.when(info_ref[1] == side)
            def _():
                for n, (first, rows) in enumerate(zip(firsts, sizes)):
                    for which in range(2):
                        to = rows * (side if which == 0 else 1 - side)
                        for k in range(strips_n):
                            outs[n][to : to + rows, k * STRIP : (k + 1) * STRIP] = ins[
                                2 * n + which
                            ][first + k * rows : first + (k + 1) * rows, :].astype(F32)

    return tiled(
        "finish_rows",
        body,
        1,
        info,
        [const(a) for pair in values for a in pair],
        [],
        [(struct(2 * r, width, F32), (2 * r, width), once) for r in sizes],
        5,
    )


def land(sums, other):
    *gots, other = fence(*[s.got for s in sums], other)
    for s, got in zip(sums, gots):
        s.got = got
    return other


def take_rows(full, core):
    quarters = full.reshape(4, full.shape[0] // 4, full.shape[1])
    return jnp.concatenate(
        [
            lax.dynamic_index_in_dim(quarters, core, 0, keepdims=False),
            lax.dynamic_index_in_dim(quarters, 2 + core, 0, keepdims=False),
        ],
        axis=0,
    )


def whole_cols(core, mine, send):
    halves = jnp.where(core == 0, mine, send), jnp.where(core == 0, send, mine)
    full = [gather_any(h) for h in halves]
    return jnp.where(core == 0, full[0], full[1])


def scatter_any(full):
    shard = lax.psum_scatter(full, ("fsdp", "seq"), scatter_dimension=0, tiled=True)
    return lax.psum(shard, "rep")


def any_rows(core, grad):
    quarter = grad.shape[0] // 2
    full = jnp.zeros((4, quarter, grad.shape[1]), BF)
    full = lax.dynamic_update_slice(full, grad[None, :quarter], (core, 0, 0))
    full = lax.dynamic_update_slice(full, grad[None, quarter:], (2 + core, 0, 0))
    return scatter_any(full.reshape(4 * quarter, grad.shape[1]))


def any_cols(core, grads):
    keeps, gots = [], []
    for grad in grads:
        halves = [scatter_any(jnp.where(core == c, grad, jnp.zeros_like(grad))) for c in range(2)]
        keeps.append(jnp.where(core == 0, halves[0], halves[1]))
        gots.append(jnp.where(core == 0, halves[1], halves[0]))
    return keeps, gots


def gather_small(vec):
    value = vec[None, :]
    for axis in ("seq", "fsdp"):
        size = lax.axis_size(axis)
        if size & (size - 1):
            return gather_any(vec[None, :])
        for bit in range(size.bit_length() - 1):
            got = lax.ppermute(value, axis, [(i, i ^ (1 << bit)) for i in range(size)])
            value = ordered((lax.axis_index(axis) >> bit) % 2 == 0, value, got)
    return value


def sum_small(value):
    for axis in ("seq", "fsdp", "rep"):
        size = lax.axis_size(axis)
        if size & (size - 1):
            value = lax.psum(value, axis)
            continue
        for bit in range(size.bit_length() - 1):
            value = value + lax.ppermute(value, axis, [(i, i ^ (1 << bit)) for i in range(size)])
    return value


def on_device(
    tokens,
    segments,
    attn_norm,
    w_q,
    w_k,
    w_v,
    q_norm,
    k_norm,
    w_o,
    mlp_norm,
    w_gate,
    w_up,
    w_down,
    cotangent,
):
    core = lax.axis_index("seq")
    row = lax.axis_index("fsdp")
    replica = lax.axis_index("rep")
    rep_size = lax.axis_size("rep")
    pairs = lax.axis_size("fsdp") == 2 and rep_size == 8
    rows, width = tokens.shape
    length = 2 * rows
    order = Order(rows)
    quarter = w_gate.shape[1] // 4
    gu_layout = functools.partial(gu_columns, quarter=quarter)
    side = replica % 2

    def starts(size, blocks):
        return [size * b for b in blocks]

    if pairs:
        quad = [2 * row + core, 2 * row + 1 - core, 2 * (1 - row) + core, 2 * (1 - row) + 1 - core]
        near, far = 2 * (1 - row) + core, 2 * (1 - row) + 1 - core
        gu_far = [jnp.where(side == 0, near, far), jnp.where(side == 0, far, near)]
        o_rows, d_rows = w_o.shape[0], w_down.shape[0]
        layout = (
            starts(w_q.shape[0], quad)
            + [o_rows * row, o_rows * (1 - row)]
            + starts(w_gate.shape[0], quad[:2] + gu_far)
            + [d_rows * row, d_rows * (1 - row)]
        )
        bases = (2, 6, 8, 12)
    else:
        layout = [0 * core] * 4
        bases = (2, 3, 4, 5)
    info = jnp.stack([core, side] + layout).astype(jnp.int32)

    sizes = (attn_norm.shape[0], mlp_norm.shape[0], q_norm.shape[0], k_norm.shape[0])
    gains = gather_small(jnp.concatenate([attn_norm, mlp_norm, q_norm, k_norm])).astype(F32)
    offsets = [0, sizes[0], sizes[0] + sizes[1], sizes[0] + sizes[1] + sizes[2], sum(sizes)]
    attn_gain, mlp_gain, q_gain, k_gain = (
        gains[:, offsets[n] : offsets[n + 1]].reshape(1, -1) for n in range(4)
    )
    head_gains = jnp.concatenate([q_gain, k_gain], axis=0)

    seg = segments[0]
    start = jnp.sum((seg[None, :] < seg[:, None]).astype(jnp.int32), axis=1)
    position = (jnp.arange(length, dtype=jnp.int32) - start).astype(F32)
    inverse = ROPE_BASE ** (jnp.arange(HD // 2, dtype=F32) * (-2.0 / HD))
    angles = position[:, None] * inverse[None, :]
    cos_half, sin_half = jnp.cos(angles), jnp.sin(angles)
    cosine = jnp.concatenate([cos_half, cos_half], axis=1)
    sine = jnp.concatenate([-sin_half, sin_half], axis=1)

    mine, send = pack("pack_qkv", info, [w_q, w_k, w_v], qkv_columns)
    got = swap(send, "seq")
    tokens_other = swap(tokens, "seq")
    if pairs:
        mine_far, got_far = swap(mine, "fsdp"), swap(got, "fsdp")
        got, w_gate, w_up = fence(got, w_gate, w_up)
        gu_mine, send = pack("pack_gu", info, [w_gate, w_up], gu_layout)
        gu_got = swap(send, "seq")
        gu_here = jnp.where(side == 0, gu_mine, gu_got)
        mine_far, got_far, attn_gain, head_gains, cosine, sine, gu_here, w_o, w_down = fence(
            mine_far, got_far, attn_gain, head_gains, cosine, sine, gu_here, w_o, w_down
        )
        wqkv = Weight(list(zip([mine, got, mine_far, got_far], layout[:4])), bases[0])
        gu_here, o_there = swap(gu_here, "fsdp"), swap(w_o, "fsdp")
    else:
        wqkv = Weight([(whole_cols(core, mine, send), 0)], bases[0])
        wo = Weight([(take_rows(gather_any(w_o), core), 0)], bases[1])
        mine, send = pack("pack_gu", info, [w_gate, w_up], gu_layout)
        wgu = Weight([(whole_cols(core, mine, send), 0)], bases[2])
        wd = Weight([(take_rows(gather_any(w_down), core), 0)], bases[3])

    cot_other = swap(cotangent, "seq")

    low = start[::BLK] // BLK

    normed, qkv, raw = project(
        order, info, tokens, tokens_other, attn_gain, wqkv, cosine, sine, head_gains
    )
    done = attend(low, qkv, start, 0, 1)
    if pairs:
        *done, gu_here = fence(*done, gu_here)
        gu_there = swap(gu_here, "rep")
    done = attend(low, qkv, start, 1, 2, done)
    if pairs:
        *done, o_there, w_down = fence(*done, o_there, w_down)
        d_there = swap(w_down, "fsdp")
        wo = Weight(list(zip([w_o, o_there], layout[4:6])), bases[1])
    attended, lse = attend(low, qkv, start, 3, 1, done)

    sent = times("mix_other", order, info, [attended], order.other, wo, False, 5)
    if pairs:
        sent, gu_there, d_there = fence(sent, gu_there, d_there)
        wgu = Weight(list(zip([gu_mine, gu_got, gu_here, gu_there], layout[6:10])), bases[2])
        wd = Weight(list(zip([w_down, d_there], layout[10:])), bases[3])
    middle, m_own = mix_own(order, info, attended, tokens, swap(sent, "seq"), mlp_gain, wo)
    hidden, d_gu, m_all, g_all = mlp(
        order, info, m_own, swap(m_own, "seq"), cotangent, cot_other, wgu, wd
    )
    g_down = tn(hidden, g_all).astype(BF)
    if pairs:
        d_gu, g_down = fence(d_gu, g_down)

    sent = times("branch_other", order, info, [d_gu], order.later, wgu, True, 9)
    got = swap(sent, "seq")
    m_all, sent = fence(m_all, sent)
    g_gu = tn(m_all, d_gu).astype(BF)
    d_gu, got, g_gu = fence(d_gu, got, g_gu)
    d_middle, d_branch, dg_mlp = branch_own(
        order, info, d_gu, got, middle, cotangent, mlp_gain, wgu
    )
    branch_other = swap(d_branch, "seq")
    d_att, branch_all = attended_back(order, info, d_branch, branch_other, wo)
    g_o = tn(attended, branch_all).astype(BF)
    if pairs:
        down = Sum(g_down, row, replica).send("rep")
        gate, up = (
            Sum(g_gu[:, n * 2 * quarter : (n + 1) * 2 * quarter], row, replica).send("fsdp")
            for n in range(2)
        )
        o_sum = Sum(g_o, row, replica).send("fsdp")
        d_att, g_o = fence(d_att, g_o)

    def back(at, earlier=None):
        return attend_back(
            low, qkv, d_att, attended, lse, start, raw, cosine, sine, head_gains, at, earlier
        )

    d_qkv0, dg0 = back(0)
    if pairs:
        d_qkv0 = land([down, gate], d_qkv0)
        down.add().send("fsdp")
        gate.add().send("rep")
    d_qkv0, dg1 = back(1, d_qkv0)
    if pairs:
        d_qkv0 = land([down, gate, up], d_qkv0)
        early = strips(gate.add().flat(), down.add().flat())
        early_got = halve(early, replica, 1)
        up.add().send("rep")
    d_qkv0, dg2 = back(2, d_qkv0)
    if pairs:
        early_got, up.got, o_sum.got, d_qkv0 = fence(early_got, up.got, o_sum.got, d_qkv0)
        early = add_half(early, early_got, replica, 1)
        early_got = halve(early, replica, 2)
        o_sum.add().send("rep")
    g_qkv0 = tn(normed, d_qkv0).astype(BF)
    if pairs:
        qkv0 = Sum(g_qkv0, row, replica).send("fsdp")
    d_att, g_qkv0 = fence(d_att, g_qkv0)
    d_qkv1, dg3 = back(3)
    if pairs:
        early_got, o_sum.got, qkv0.got, d_qkv1 = fence(early_got, o_sum.got, qkv0.got, d_qkv1)
    g_qkv1 = tn(normed, d_qkv1).astype(BF)
    d_qkv1, g_qkv1 = fence(d_qkv1, g_qkv1)
    if pairs:
        qkv1 = Sum(g_qkv1, row, replica).send("fsdp")
        early = add_half(early, early_got, replica, 2)
        early_got = swap(early, "rep", 2)
        late = strips(up.add().flat(), o_sum.add().flat())
        late_got = halve(late, replica, 1)
        qkv0.add().send("rep")

    sent = times("tokens_other", order, info, [d_qkv0, d_qkv1], order.other, wqkv, True, 6)
    if pairs:
        early_got, late_got, qkv0.got, qkv1.got, sent = fence(
            early_got, late_got, qkv0.got, qkv1.got, sent
        )
        qkv1.add().send("rep")
        early = double(early, early_got, replica, 2)
        early_got = swap(early, "rep", 1)
        late = add_half(late, late_got, replica, 1)
        late_got = halve(late, replica, 2)
    hidden, sent = fence(hidden, sent)
    out_sent = times("output_other", order, info, [hidden], order.later, wd, False, 6)
    if pairs:
        early_got, late_got, qkv1.got, out_sent = fence(early_got, late_got, qkv1.got, out_sent)
        last = jnp.concatenate([qkv0.add().flat(), qkv1.add().flat()], axis=1)
        last_got = halve(last, replica, 1)
        early = double(early, early_got, replica, 1)
        early_far = swap(early, "rep", 0)
        late = add_half(late, late_got, replica, 2)
        late_got = swap(late, "rep", 2)
    sent, out_sent = fence(sent, out_sent)
    got, out_got = swap(sent, "seq"), swap(out_sent, "seq")
    tokens_grad, dg_attn = tokens_own(
        order, info, [d_qkv0, d_qkv1], got, tokens, d_middle, attn_gain, wqkv
    )
    dg_heads = dg0 + dg1 + dg2 + dg3
    small = jnp.concatenate([dg_attn[0], dg_mlp[0], dg_heads[0], dg_heads[1]])
    if pairs:
        late_got, last_got, tokens_grad = fence(late_got, last_got, tokens_grad)
        last = add_half(last, last_got, replica, 1)
        last_got = halve(last, replica, 2)
        late = double(late, late_got, replica, 2)
        late_got = swap(late, "rep", 1)
        hop = swap(small, "seq")
    hidden, tokens_grad = fence(hidden, tokens_grad)
    output = output_own(order, info, hidden, middle, out_got, wd)
    if pairs:
        early_far, last_got, hop, output = fence(early_far, last_got, hop, output)
        last = add_half(last, last_got, replica, 2)
        last_got = swap(last, "rep", 2)
        small = small + hop
        hop = swap(small, "fsdp")

        late_got, last_got, hop = fence(late_got, last_got, hop)
        last = double(last, last_got, replica, 2)
        last_got = swap(last, "rep", 1)
        late = double(late, late_got, replica, 1)
        late_far = swap(late, "rep", 0)
        small = small + hop
        hop = swap(small, "rep", 1)

        last_got, hop = fence(last_got, hop)
        last = double(last, last_got, replica, 1)
        last_far = swap(last, "rep", 0)
        small = small + hop
        hop = swap(small, "rep", 2)

        late_far, hop = fence(late_far, hop)
        small = small + hop
        hop = swap(small, "rep", 0)
        home = core == side
        gu_rows = early.shape[0] // 2
        values = [(early, early_far), (late, late_far)]
        gots = [swap(jnp.where(home, b[:gu_rows], a[:gu_rows]), "seq") for a, b in values]
        g_gate, g_up = finish_gu(info, values, gots, quarter)
        g_down, g_o = finish_rows(info, values, [gu_rows, gu_rows], width)

        last_far, g_gate, g_up, g_down, g_o, hop = fence(
            last_far, g_gate, g_up, g_down, g_o, hop
        )
        small = small + hop
        keep, send = jnp.where(home, last, last_far), jnp.where(home, last_far, last)
        qkv_parts = [keep], [swap(send, "seq")]
    else:
        small = sum_small(small)
        g_down, g_o = (any_rows(core, g).astype(F32) for g in (g_down, g_o))
        qkv_parts = any_cols(core, [jnp.concatenate([g_qkv0, g_qkv1], axis=1)])
        gu_parts = any_cols(core, [g_gu[:, : 2 * quarter], g_gu[:, 2 * quarter :]])
        g_gate, g_up = unpack("unpack_gu", info, *gu_parts, [w_gate.shape[1]] * 2, gu_layout)
    g_q, g_k, g_v = unpack(
        "unpack_qkv", info, *qkv_parts, [a.shape[1] for a in (w_q, w_k, w_v)], qkv_columns
    )

    shard = row * 2 + core
    pieces = []
    at = 0
    for size in sizes:
        total = size * lax.axis_size("fsdp") * 2
        pieces.append(lax.dynamic_slice_in_dim(small[at : at + total], shard * size, size, 0))
        at += total
    return (
        output,
        tokens_grad,
        pieces[0],
        g_q,
        g_k,
        g_v,
        pieces[2],
        pieces[3],
        g_o,
        pieces[1],
        g_gate,
        g_up,
        g_down,
    )


def solution(mesh):
    token_rows = P(("rep", "fsdp", "seq"), None)
    vec = P(("fsdp", "seq"))
    mat = P(("fsdp", "seq"), None)
    return jax.shard_map(
        on_device,
        mesh=mesh,
        in_specs=(
            token_rows,
            P(("rep", "fsdp"), None),
            vec,
            mat,
            mat,
            mat,
            vec,
            vec,
            mat,
            vec,
            mat,
            mat,
            mat,
            token_rows,
        ),
        out_specs=(
            token_rows,
            token_rows,
            vec,
            mat,
            mat,
            mat,
            vec,
            vec,
            mat,
            vec,
            mat,
            mat,
            mat,
        ),
        check_vma=False,
    )
```

time: 911 us -> 636 us (0.70)
  waiting for transfers between devices: 315 us -> 108 us
  Pallas kernels: 171 us -> 328 us
  blocking collectives: 120 us -> 0 us
  matrix products: 115 us -> 54.4 us
  other arithmetic: 98.9 us -> 52.2 us
  starting transfers between devices: 22.8 us -> 48.6 us
  between operations: 16 us -> 1.78 us
    pallas_call x4 -> x23, Pallas kernels: 171 us -> 328 us  [the longest x16 180 us: tiled(): pl.pallas_call(kernel, grid_spec=pltpu.PrefetchScalarGridSpec(num_scalar_...]
    psum x1 -> x0, waiting for transfers between devices: 117 us -> none  [over_rep(): mine = lax.psum(mine, 'rep', axis_index_groups=groups)]
    ppermute x31 -> x53, waiting for transfers between devices: 198 us -> 108 us  [the longest x51 102 us: swap(): return lax.ppermute(value, axis, [(i, i ^ 1 << bit) for i in range(size)])]
    psum x1 -> x0, blocking collectives: 77.8 us -> none  [on_device(): lax.psum(jnp.concatenate([dg_attn, dg_mlp, dg_heads[0], dg_heads[1]]), ('...]
    dot_general x9 -> x0, matrix products: 72.4 us -> none  [the longest x5 50.1 us: nt(): lax.dot_general(a, b, (((1,), (1,)), ((), ())), preferred_element_type=F32)]
    unnamed x1 -> x0, blocking collectives: 42.5 us -> none
    select_n x11 -> x7, other arithmetic: 37.3 us -> 9.44 us  [ordered(): jnp.where(first_is_mine, jnp.concatenate([mine, other], axis=0), jnp.conc...]
    ppermute x31 -> x53, starting transfers between devices: 22.8 us -> 48.6 us  [the longest x51 47.9 us: swap(): return lax.ppermute(value, axis, [(i, i ^ 1 << bit) for i in range(size)])]
  transfers between devices with their start and end apart: 32 -> 53, of which waited for: 10 -> 20; matrix products, arithmetic and copies ran while one was open for 25% -> 15% of each run, Pallas kernels for 16% -> 41%
where the time goes in v2:
time: 636 us; the launch traced here: 631 us
  Pallas kernels  328 us (52%)
  waiting for transfers between devices  108 us (17%)
  matrix products  54.4 us (9%)
  other arithmetic  52.2 us (8%)
  starting transfers between devices  48.6 us (8%)
  local copies, waits for them, and re-layouts  39 us (6%)
    pallas_call x16, Pallas kernels, tiled(): pl.pallas_call(kernel, grid_spec=pltpu.PrefetchScalarGridSpec(num_scalar_...  180 us
    ppermute x51, waiting for transfers between devices, swap(): return lax.ppermute(value, axis, [(i, i ^ 1 << bit) for i in range(size)])  102 us
    pallas_call x4, Pallas kernels, attend_back(): pl.pallas_call(body, grid_spec=pltpu.PrefetchScalarGridSpec(num_scalar_pr...  95 us
    dot_general x5, matrix products, tn(): lax.dot_general(a, b, (((0,), (0,)), ((), ())), preferred_element_type=F32)  54.4 us
    pallas_call x3, Pallas kernels, attend(): pl.pallas_call(body, grid_spec=pltpu.PrefetchScalarGridSpec(num_scalar_pr...  53 us
    ppermute x51, starting transfers between devices, swap(): return lax.ppermute(value, axis, [(i, i ^ 1 << bit) for i in range(size)])  47.9 us
    dynamic_slice x17, local copies, waits for them, and re-layouts, part(): return lax.dynamic_slice_in_dim(value, index * size, size, axis)  15.6 us
    unnamed x121, local copies, waits for them, and re-layouts  15.3 us
  transfers between devices with their start and end apart: 53, of which 20 were waited for; matrix products, arithmetic and copies ran while one was open for 15% of the time, Pallas kernels for 41%

profile of v2, /device:TPU:0, one launch (start us, length us, event | category | flops | bytes accessed | tf_op | source)
XLA Modules:
  0.0 631.3 jit_solution(13977728181834712402)
XLA Ops:
  1.4 3.8 pack_qkv.1
  5.6 2.5 collective-permute-start.1
  8.8 1.8 convert_reduce_fusion
  10.6 4.9 pack_gu.1
  15.8 5.7 fusion.3
  22.0 4.2 pad_maximum_fusion
  26.3 6.1 collective-permute-done.5
  37.2 20.7 %collective-permute-done.3.refs_9_.refs_5_ = bf16[256,2048]{1,0:T(8,128)(2,1)S(1)} collective-permute-done((bf16[256,2048]{1,0:T(8,128)(2,1)}, bf16[256,2048]{1,0:T(8,128)(2,1)S(1)}, u32[]{:S(2)}, u32[]{:S(2)}) %collective-permute-start.3) | collective-permute-done | bytes 1048608 | tf_op jit(solution)/shard_map/ppermute | solution.py:716
  62.9 19.2 %project.1 = (bf16[2048,1024]{1,0:T(8,128)(2,1)}, bf16[2048,2048]{1,0:T(8,128)(2,1)}, bf16[2048,1536]{1,0:T(8,128)(2,1)}) custom-call(s32[14]{0:T(128)} %stack.53.info_ref, bf16[1024,1024]{1,0:T(8,128)(2,1)} %refs_3_.3, bf16[1024,1024]{1,0:T(8,128)(2,1)} %collective-permute-done.refs_1_, f32[1,1024]{1,0:T(1,128)} %bitcast.74, ...), custom_call_target="tpu_custom_call" | custom-call | flops 170000000 | tf_op jit(solution)/shard_map/project/pallas_call | solution.py:83
  82.1 14.1 %attend.3 = (bf16[2048,1024]{1,0:T(8,128)(2,1)}, f32[4,2,2048]{2,1,0:T(2,128)}) custom-call(s32[8]{0:T(128)} %and_select_fusion.low_ref.refs_0_, bf16[2048,2048]{1,0:T(8,128)(2,1)} %get-tuple-element.149.qkv_ref.refs_1_, s32[2048,1]{1,0:T(8,128)} %copy.38.start_ref), custom_call_target="tpu_custom_call" | custom-call | flops 115000000 | tf_op jit(solution)/shard_map/attend/pallas_call | solution.py:467
  96.3 24.8 %attend.4 = (bf16[2048,1024]{1,0:T(8,128)(2,1)}, f32[4,2,2048]{2,1,0:T(2,128)}) custom-call(s32[8]{0:T(128)} %and_select_fusion.low_ref.refs_0_, bf16[2048,2048]{1,0:T(8,128)(2,1)} %get-tuple-element.149.qkv_ref.refs_1_, s32[2048,1]{1,0:T(8,128)} %copy.38.start_ref, ...), custom_call_target="tpu_custom_call", output_to_operand_aliasing={{0}: (3, {}), {1}: (4, {})} | custom-call | flops 230000000 | tf_op jit(solution)/shard_map/attend/pallas_call | solution.py:467
  125.1 14.1 %attend.5 = (bf16[2048,1024]{1,0:T(8,128)(2,1)}, f32[4,2,2048]{2,1,0:T(2,128)}) custom-call(s32[8]{0:T(128)} %and_select_fusion.low_ref.refs_0_, bf16[2048,2048]{1,0:T(8,128)(2,1)} %get-tuple-element.149.qkv_ref.refs_1_, s32[2048,1]{1,0:T(8,128)} %copy.38.start_ref, ...), custom_call_target="tpu_custom_call", output_to_operand_aliasing={{0}: (3, {}), {1}: (4, {})} | custom-call | flops 115000000 | tf_op jit(solution)/shard_map/attend/pallas_call | solution.py:467
  139.2 7.5 %mix_other.1 = bf16[1024,1024]{1,0:T(8,128)(2,1)} custom-call(s32[14]{0:T(128)} %stack.53.info_ref, bf16[2048,1024]{1,0:T(8,128)(2,1)} %get-tuple-element.161.refs_0_.refs_3_, bf16[512,1024]{1,0:T(8,128)(2,1)} %refs_2_.4, bf16[512,1024]{1,0:T(8,128)(2,1)} %copy-done.9), custom_call_target="tpu_custom_call" | custom-call | flops 50000000 | tf_op jit(solution)/shard_map/mix_other/pallas_call | solution.py:83
  146.7 10.5 %collective-permute-done.10.refs_9_.refs_2_.refs_4_ = bf16[768,1024]{1,0:T(8,128)(2,1)} collective-permute-done((bf16[768,1024]{1,0:T(8,128)(2,1)}, bf16[768,1024]{1,0:T(8,128)(2,1)}, u32[]{:S(2)}, u32[]{:S(2)}) %collective-permute-start.10) | collective-permute-done | bytes 1572896 | tf_op jit(solution)/shard_map/ppermute | solution.py:716
  158.9 3.4 collective-permute-done.11.refs_2_
  162.3 9.5 %mix_own.1 = (f32[1024,1024]{1,0:T(8,128)}, bf16[1024,1024]{1,0:T(8,128)(2,1)}) custom-call(s32[14]{0:T(128)} %stack.53.info_ref, bf16[2048,1024]{1,0:T(8,128)(2,1)} %get-tuple-element.161.refs_0_.refs_3_, bf16[1024,1024]{1,0:T(8,128)(2,1)} %refs_3_.3, bf16[1024,1024]{1,0:T(8,128)(2,1)} %collective-permute-done.11.refs_2_, f32[1,1024]{1,0:T(1,128)} %bitcast.76, ...), custom_call_target="tpu_custom_call" | custom-call | flops 60000000 | tf_op jit(solution)/shard_map/mix_own/pallas_call | solution.py:83
  172.1 4.2 collective-permute-done.12.refs_1_
  177.6 32.0 %mlp.1 = (bf16[2048,1536]{1,0:T(8,128)(2,1)}, bf16[2048,3072]{1,0:T(8,128)(2,1)}, bf16[2048,1024]{1,0:T(8,128)(2,1)}, bf16[2048,1024]{1,0:T(8,128)(2,1)}) custom-call(s32[14]{0:T(128)} %stack.53.info_ref, bf16[1024,1024]{1,0:T(8,128)(2,1)} %get-tuple-element.166.refs_0_, bf16[1024,1024]{1,0:T(8,128)(2,1)} %copy-done.23, bf16[1024,1024]{1,0:T(8,128)(2,1)} %refs_3_.2, ...), custom_call_target="tpu_custom_call" | custom-call | flops 300000000 | tf_op jit(solution)/shard_map/mlp/pallas_call | solution.py:83
  209.6 10.3 %convolution_convert_fusion.2 = bf16[1536,1024]{1,0:T(8,128)(2,1)S(1)} fusion(bf16[2048,1536]{1,0:T(8,128)(2,1)} %get-tuple-element.231.refs_0_, bf16[2048,1024]{1,0:T(8,128)(2,1)} %get-tuple-element.171), kind=kOutput, calls=%fused_computation.3 | convolution fusion | flops 6444023808 | bytes 13631488 | tf_op jit(solution)/shard_map/dot_general | solution.py:31
  220.0 13.6 %branch_other.1 = bf16[1024,1024]{1,0:T(8,128)(2,1)} custom-call(s32[14]{0:T(128)} %stack.53.info_ref, bf16[2048,3072]{1,0:T(8,128)(2,1)} %get-tuple-element.177.refs_0_, bf16[256,3072]{1,0:T(8,128)(2,1)} %get-tuple-element.140.refs_4_.refs_1_.refs_5_, bf16[256,3072]{1,0:T(8,128)(2,1)} %copy-done.1, bf16[256,3072]{1,0:T(8,128)(2,1)} %copy-done.4, ...), custom_call_target="tpu_custom_call" | custom-call | flops 90000000 | tf_op jit(solution)/shard_map/branch_other/pallas_call | solution.py:83
  233.8 18.7 %convolution_convert_fusion = bf16[1024,3072]{1,0:T(8,128)(2,1)} fusion(bf16[2048,1024]{1,0:T(8,128)(2,1)} %get-tuple-element.174, bf16[2048,3072]{1,0:T(8,128)(2,1)} %get-tuple-element.177.refs_0_), kind=kOutput, calls=%fused_computation.1 | convolution fusion | flops 12888047616 | bytes 23068672 | tf_op jit(solution)/shard_map/dot_general | solution.py:31
  252.5 16.5 %branch_own.1 = (f32[1024,1024]{1,0:T(8,128)}, bf16[1024,1024]{1,0:T(8,128)(2,1)}, f32[1,1024]{1,0:T(1,128)}) custom-call(s32[14]{0:T(128)} %stack.53.info_ref, bf16[2048,3072]{1,0:T(8,128)(2,1)} %get-tuple-element.177.refs_0_, bf16[1024,1024]{1,0:T(8,128)(2,1)} %collective-permute-done.14.refs_1_, f32[1024,1024]{1,0:T(8,128)} %get-tuple-element.179.refs_2_.refs_1_, ...), custom_call_target="tpu_custom_call" | custom-call | flops 110000000 | tf_op jit(solution)/shard_map/branch_own/pallas_call | solution.py:83
  272.2 3.2 fusion.6
  281.0 12.1 %attended_back.1 = (bf16[2048,1024]{1,0:T(8,128)(2,1)}, bf16[2048,1024]{1,0:T(8,128)(2,1)}) custom-call(s32[14]{0:T(128)} %stack.53.info_ref, bf16[1024,1024]{1,0:T(8,128)(2,1)} %get-tuple-element.180.refs_0_, bf16[1024,1024]{1,0:T(8,128)(2,1)} %collective-permute-done.17.refs_1_, bf16[512,1024]{1,0:T(8,128)(2,1)} %refs_2_.4, bf16[512,1024]{1,0:T(8,128)(2,1)} %copy-done.9), custom_call_target="tpu_custom_call" | custom-call | flops 80000000 | tf_op jit(solution)/shard_map/attended_back/pallas_call | solution.py:83
  293.1 9.4 %convolution_convert_fusion.3 = bf16[1024,1024]{1,0:T(8,128)(2,1)} fusion(bf16[2048,1024]{1,0:T(8,128)(2,1)} %get-tuple-element.161.refs_0_.refs_3_, bf16[2048,1024]{1,0:T(8,128)(2,1)} %get-tuple-element.182), kind=kOutput, calls=%fused_computation.4 | convolution fusion | flops 4296015872 | bytes 10485760 | tf_op jit(solution)/shard_map/dot_general | solution.py:31
  302.4 23.7 %attend_back.4 = (bf16[2048,1536]{1,0:T(8,128)(2,1)}, f32[2,128]{1,0:T(2,128)}) custom-call(s32[8]{0:T(128)} %and_select_fusion.low_ref.refs_0_, bf16[2048,2048]{1,0:T(8,128)(2,1)} %get-tuple-element.149.qkv_ref.refs_1_, bf16[2048,1024]{1,0:T(8,128)(2,1)} %get-tuple-element.200.refs_2_, bf16[2048,1024]{1,0:T(8,128)(2,1)} %get-tuple-element.161.refs_0_.refs_3_, ...), custom_call_target="tpu_custom_call" | custom-call | flops 210000000 | tf_op jit(solution)/shard_map/attend_back/pallas_call | solution.py:605
  326.1 2.2 dynamic-slice_add_fusion.3
  333.8 2.3 constant_dynamic-slice_fusion.9
  337.2 23.9 %attend_back.5 = (bf16[2048,1536]{1,0:T(8,128)(2,1)}, f32[2,128]{1,0:T(2,128)}) custom-call(s32[8]{0:T(128)} %and_select_fusion.low_ref.refs_0_, bf16[2048,2048]{1,0:T(8,128)(2,1)} %get-tuple-element.149.qkv_ref.refs_1_, bf16[2048,1024]{1,0:T(8,128)(2,1)} %get-tuple-element.200.refs_2_, ...), custom_call_target="tpu_custom_call", output_to_operand_aliasing={{0}: (10, {})} | custom-call | flops 210000000 | tf_op jit(solution)/shard_map/attend_back/pallas_call | solution.py:605
  361.1 4.7 collective-permute-done.18
  374.0 23.8 %attend_back.6 = (bf16[2048,1536]{1,0:T(8,128)(2,1)}, f32[2,128]{1,0:T(2,128)}) custom-call(s32[8]{0:T(128)} %and_select_fusion.low_ref.refs_0_, bf16[2048,2048]{1,0:T(8,128)(2,1)} %get-tuple-element.149.qkv_ref.refs_1_, bf16[2048,1024]{1,0:T(8,128)(2,1)} %get-tuple-element.200.refs_2_, ...), custom_call_target="tpu_custom_call", output_to_operand_aliasing={{0}: (10, {})} | custom-call | flops 210000000 | tf_op jit(solution)/shard_map/attend_back/pallas_call | solution.py:605
  397.9 10.7 %convolution_convert_fusion.1 = bf16[1024,1536]{1,0:T(8,128)(2,1)S(1)} fusion(bf16[2048,1024]{1,0:T(8,128)(2,1)} %get-tuple-element.198, bf16[2048,1536]{1,0:T(8,128)(2,1)} %get-tuple-element.199.refs_0_), kind=kOutput, calls=%fused_computation.2 | convolution fusion | flops 6444023808 | bytes 13631488 | tf_op jit(solution)/shard_map/dot_general | solution.py:31
  415.6 3.8 collective-permute-start.24
  420.2 23.7 %attend_back.7 = (bf16[2048,512]{1,0:T(8,128)(2,1)}, f32[2,128]{1,0:T(2,128)}) custom-call(s32[8]{0:T(128)} %and_select_fusion.low_ref.refs_0_, bf16[2048,2048]{1,0:T(8,128)(2,1)} %get-tuple-element.149.qkv_ref.refs_1_, bf16[2048,1024]{1,0:T(8,128)(2,1)} %get-tuple-element.200.refs_2_, bf16[2048,1024]{1,0:T(8,128)(2,1)} %get-tuple-element.161.refs_0_.refs_3_, ...), custom_call_target="tpu_custom_call" | custom-call | flops 210000000 | tf_op jit(solution)/shard_map/attend_back/pallas_call | solution.py:605
  446.1 5.4 convolution_convert_fusion.4
  451.5 2.0 dynamic-slice_add_fusion
  459.6 2.9 collective-permute-start.27
  462.5 10.2 %tokens_other.1 = bf16[1024,1024]{1,0:T(8,128)(2,1)} custom-call(s32[14]{0:T(128)} %stack.53.info_ref, bf16[2048,1536]{1,0:T(8,128)(2,1)} %get-tuple-element.199.refs_0_, bf16[2048,512]{1,0:T(8,128)(2,1)} %get-tuple-element.208.refs_1_, bf16[256,2048]{1,0:T(8,128)(2,1)} %get-tuple-element.136.refs_6_.refs_2_, ...), custom_call_target="tpu_custom_call" | custom-call | flops 60000000 | tf_op jit(solution)/shard_map/tokens_other/pallas_call | solution.py:83
  472.8 4.6 collective-permute-done.27
  477.4 2.2 collective-permute-done.28
  481.8 1.9 collective-permute-start.31
  490.1 9.1 %output_other.1 = bf16[1024,1024]{1,0:T(8,128)(2,1)} custom-call(s32[14]{0:T(128)} %stack.53.info_ref, bf16[2048,1536]{1,0:T(8,128)(2,1)} %get-tuple-element.231.refs_0_, bf16[768,1024]{1,0:T(8,128)(2,1)} %refs_3_.4, bf16[768,1024]{1,0:T(8,128)(2,1)} %collective-permute-done.10.refs_9_.refs_2_.refs_4_), custom_call_target="tpu_custom_call" | custom-call | flops 60000000 | tf_op jit(solution)/shard_map/output_other/pallas_call | solution.py:83
  499.2 4.3 collective-permute-done.32
  503.6 2.3 collective-permute-done.31
  509.6 1.9 maximum_select_fusion.refs_0_
  514.8 13.3 %tokens_own.1 = (f32[1024,1024]{1,0:T(8,128)}, f32[1,1024]{1,0:T(1,128)}) custom-call(s32[14]{0:T(128)} %stack.53.info_ref, bf16[2048,1536]{1,0:T(8,128)(2,1)} %get-tuple-element.199.refs_0_, bf16[2048,512]{1,0:T(8,128)(2,1)} %get-tuple-element.208.refs_1_, bf16[1024,1024]{1,0:T(8,128)(2,1)} %collective-permute-done.37.refs_2_, bf16[1024,1024]{1,0:T(8,128)(2,1)} %refs_3_.3, ...), custom_call_target="tpu_custom_call" | custom-call | flops 90000000 | tf_op jit(solution)/shard_map/tokens_own/pallas_call | solution.py:83
  528.9 2.1 collective-permute-done.36
  534.6 2.3 maximum_select_fusion.4
  536.9 1.9 collective-permute-start.41
  538.8 10.1 %output_own.1 = bf16[1024,1024]{1,0:T(8,128)(2,1)} custom-call(s32[14]{0:T(128)} %stack.53.info_ref, bf16[2048,1536]{1,0:T(8,128)(2,1)} %get-tuple-element.231.refs_0_, f32[1024,1024]{1,0:T(8,128)} %get-tuple-element.179.refs_2_.refs_1_, bf16[1024,1024]{1,0:T(8,128)(2,1)} %collective-permute-done.40.refs_2_, bf16[768,1024]{1,0:T(8,128)(2,1)} %refs_3_.4, ...), custom_call_target="tpu_custom_call" | custom-call | flops 60000000 | tf_op jit(solution)/shard_map/output_own/pallas_call | solution.py:83
  552.6 2.3 collective-permute-done.43
  555.0 10.5 %collective-permute-done.42 = bf16[64,2048]{1,0:T(8,128)(2,1)S(1)} collective-permute-done((bf16[64,2048]{1,0:T(8,128)(2,1)S(1)}, bf16[64,2048]{1,0:T(8,128)(2,1)S(1)}, u32[]{:S(2)}, u32[]{:S(2)}) %collective-permute-start.42) | collective-permute-done | bytes 262176 | tf_op jit(solution)/shard_map/ppermute | solution.py:716
  565.5 2.1 maximum_select_fusion.1.refs_2_
  568.7 2.0 collective-permute-start.45
  570.7 2.1 slice_select_fusion.1
  572.8 9.0 %collective-permute-done.45 = f32[2304]{0:T(1024)S(1)} collective-permute-done((f32[2304]{0:T(1024)S(1)}, f32[2304]{0:T(1024)S(1)}, u32[]{:S(2)}, u32[]{:S(2)}) %collective-permute-start.45) | collective-permute-done | bytes 9248 | tf_op jit(solution)/shard_map/ppermute | solution.py:716
  584.7 1.7 collective-permute-done.47
  586.5 13.0 %collective-permute-done.46.refs_3_ = bf16[1280,512]{1,0:T(8,128)(2,1)} collective-permute-done((bf16[1280,512]{1,0:T(8,128)(2,1)S(1)}, bf16[1280,512]{1,0:T(8,128)(2,1)}, u32[]{:S(2)}, u32[]{:S(2)}) %collective-permute-start.46) | collective-permute-done | bytes 1310752 | tf_op jit(solution)/shard_map/ppermute | solution.py:716
  599.4 2.1 slice_select_fusion
  602.4 6.0 finish_rows.1
  609.3 6.9 %finish_gu.1 = (f32[256,3072]{1,0:T(8,128)}, f32[256,3072]{1,0:T(8,128)}) custom-call(s32[14]{0:T(128)} %stack.53.info_ref, bf16[1536,512]{1,0:T(8,128)(2,1)} %copy-done.2, bf16[1536,512]{1,0:T(8,128)(2,1)} %copy-done.7, bf16[1280,512]{1,0:T(8,128)(2,1)} %copy-done.3, bf16[1280,512]{1,0:T(8,128)(2,1)} %collective-permute-done.46.refs_3_, ...), custom_call_target="tpu_custom_call" | custom-call | flops 50000000 | tf_op jit(solution)/shard_map/finish_gu/pallas_call | solution.py:83
  616.2 4.3 collective-permute-done.51
  620.5 2.4 broadcast_select_fusion.1
  626.5 4.7 unpack_qkv.1
  (271 shorter events, 92.1 us)
Async XLA Ops:
  5.2 5.5 collective-permute-start.2
  5.6 31.5 %collective-permute-start.1 = (bf16[256,2048]{1,0:T(8,128)(2,1)}, bf16[256,2048]{1,0:T(8,128)(2,1)}, u32[]{:S(2)}, u32[]{:S(2)}) collective-permute-start(bf16[256,2048]{1,0:T(8,128)(2,1)} %get-tuple-element.136.refs_6_.refs_2_), channel_id=1, source_target_pairs={{0,2},{2,0},{1,3},{3,1},{4,6},{6,4},{5,7},{7,5},{8,10},{10,8},{9,1... | collective-permute-start | bytes 3145736 | tf_op jit(solution)/shard_map/ppermute | solution.py:716
  8.3 13.2 %collective-permute-start.4 = (bf16[1,576]{1,0:T(2,128)(2,1)S(1)}, bf16[1,576]{1,0:T(2,128)(2,1)S(1)}, u32[]{:S(2)}, u32[]{:S(2)}) collective-permute-start(bf16[1,576]{1,0:T(2,128)(2,1)S(1)} %broadcast_in_dim.2), channel_id=1, source_target_pairs={{0,1},{1,0},{2,3},{3,2},{4,5},{5,4},{6,7},{7,6},{8,9},{9,8},{10,11... | collective-permute-start | bytes 3464 | tf_op jit(solution)/shard_map/ppermute | solution.py:895
  8.5 54.4 %collective-permute-start = (bf16[1024,1024]{1,0:T(8,128)(2,1)}, bf16[1024,1024]{1,0:T(8,128)(2,1)}, u32[]{:S(2)}, u32[]{:S(2)}) collective-permute-start(bf16[1024,1024]{1,0:T(8,128)(2,1)} %refs_3_.3), channel_id=1, source_target_pairs={{0,1},{1,0},{2,3},{3,2},{4,5},{5,4},{6,7},{7,6},{8,9},{9,8},{10,11... | collective-permute-start | bytes 6291464 | tf_op jit(solution)/shard_map/ppermute | solution.py:716
  10.6 50.3 %copy-start.43 = (s32[2048]{0:T(1024)}, s32[2048]{0:T(1024)S(1)}, u32[]{:S(2)}) copy-start(s32[2048]{0:T(1024)S(1)} %convert_reduce_fusion) | copy-start | bytes 24580
  15.6 19.9 %collective-permute-start.6 = (bf16[256,3072]{1,0:T(8,128)(2,1)}, bf16[256,3072]{1,0:T(8,128)(2,1)S(1)}, u32[]{:S(2)}, u32[]{:S(2)}) collective-permute-start(bf16[256,3072]{1,0:T(8,128)(2,1)} %get-tuple-element.141), channel_id=1, source_target_pairs={{0,1},{1,0},{2,3},{3,2},{4,5},{5,4},{6,7},{7,6},{8,9},{9,8},{10,11... | collective-permute-start | bytes 4718600 | tf_op jit(solution)/shard_map/ppermute | solution.py:716
  21.5 10.8 %collective-permute-start.5 = (bf16[2,576]{1,0:T(2,128)(2,1)S(1)}, bf16[2,576]{1,0:T(2,128)(2,1)S(1)}, u32[]{:S(2)}, u32[]{:S(2)}) collective-permute-start(bf16[2,576]{1,0:T(2,128)(2,1)S(1)} %broadcast_select_fusion.3), channel_id=1, source_target_pairs={{0,2},{2,0},{1,3},{3,1},{4,6},{6,4},{5,7},{7,5},{8,10},{10,8},{9,1... | collective-permute-start | bytes 6920 | tf_op jit(solution)/shard_map/ppermute | solution.py:895
  22.0 13.5 %copy-start = (bf16[256,3072]{1,0:T(8,128)(2,1)S(1)}, bf16[256,3072]{1,0:T(8,128)(2,1)}, u32[]{:S(2)}) copy-start(bf16[256,3072]{1,0:T(8,128)(2,1)} %get-tuple-element.140.refs_4_.refs_1_.refs_5_) | copy-start | bytes 4718596
  32.6 25.2 %collective-permute-start.3 = (bf16[256,2048]{1,0:T(8,128)(2,1)}, bf16[256,2048]{1,0:T(8,128)(2,1)S(1)}, u32[]{:S(2)}, u32[]{:S(2)}) collective-permute-start(bf16[256,2048]{1,0:T(8,128)(2,1)} %collective-permute-done.2.refs_7_.refs_3_), channel_id=1, source_target_pairs={{0,2},{2,0},{1,3},{3,1},{4,6},{6,4},{5,7},{7,5},{8,10},{10,8},{9,1... | collective-permute-start | bytes 3145736 | tf_op jit(solution)/shard_map/ppermute | solution.py:716
  58.8 37.5 %collective-permute-start.7 = (bf16[256,3072]{1,0:T(8,128)(2,1)}, bf16[256,3072]{1,0:T(8,128)(2,1)S(1)}, u32[]{:S(2)}, u32[]{:S(2)}) collective-permute-start(bf16[256,3072]{1,0:T(8,128)(2,1)} %broadcast_select_fusion), channel_id=1, source_target_pairs={{0,2},{2,0},{1,3},{3,1},{4,6},{6,4},{5,7},{7,5},{8,10},{10,8},{9,1... | collective-permute-start | bytes 4718600 | tf_op jit(solution)/shard_map/ppermute | solution.py:716
  60.3 60.9 %collective-permute-start.8 = (bf16[512,1024]{1,0:T(8,128)(2,1)}, bf16[512,1024]{1,0:T(8,128)(2,1)S(1)}, u32[]{:S(2)}, u32[]{:S(2)}) collective-permute-start(bf16[512,1024]{1,0:T(8,128)(2,1)} %refs_2_.4), channel_id=1, source_target_pairs={{0,2},{2,0},{1,3},{3,1},{4,6},{6,4},{5,7},{7,5},{8,10},{10,8},{9,1... | collective-permute-start | bytes 3145736 | tf_op jit(solution)/shard_map/ppermute | solution.py:716
  96.3 27.3 %copy-start.4 = (bf16[256,3072]{1,0:T(8,128)(2,1)}, bf16[256,3072]{1,0:T(8,128)(2,1)S(1)}, u32[]{:S(2)}) copy-start(bf16[256,3072]{1,0:T(8,128)(2,1)S(1)} %collective-permute-done.7.refs_6_.refs_3_.refs_7_) | copy-start | bytes 4718596
  122.1 35.1 %collective-permute-start.10 = (bf16[768,1024]{1,0:T(8,128)(2,1)}, bf16[768,1024]{1,0:T(8,128)(2,1)}, u32[]{:S(2)}, u32[]{:S(2)}) collective-permute-start(bf16[768,1024]{1,0:T(8,128)(2,1)} %refs_3_.4), channel_id=1, source_target_pairs={{0,2},{2,0},{1,3},{3,1},{4,6},{6,4},{5,7},{7,5},{8,10},{10,8},{9,1... | collective-permute-start | bytes 4718600 | tf_op jit(solution)/shard_map/ppermute | solution.py:716
  123.6 34.2 %collective-permute-start.9 = (bf16[256,3072]{1,0:T(8,128)(2,1)S(1)}, bf16[256,3072]{1,0:T(8,128)(2,1)S(1)}, u32[]{:S(2)}, u32[]{:S(2)}) collective-permute-start(bf16[256,3072]{1,0:T(8,128)(2,1)S(1)} %collective-permute-done.7.refs_6_.refs_3_.refs_7_), channel_id=1, source_target_pairs={{0,4},{4,0},{8,12},{12,8},{16,20},{20,16},{24,28},{28,24},{1,5},{5... | collective-permute-start | bytes 4718600 | tf_op jit(solution)/shard_map/ppermute | solution.py:716
  157.8 14.0 %copy-start.5 = (bf16[256,3072]{1,0:T(8,128)(2,1)}, bf16[256,3072]{1,0:T(8,128)(2,1)S(1)}, u32[]{:S(2)}) copy-start(bf16[256,3072]{1,0:T(8,128)(2,1)S(1)} %collective-permute-done.9.refs_7_.refs_4_.refs_8_) | copy-start | bytes 4718596
  157.8 4.5 collective-permute-start.11
  157.8 14.2 %collective-permute-start.13 = (bf16[1024,1024]{1,0:T(8,128)(2,1)}, bf16[1024,1024]{1,0:T(8,128)(2,1)}, u32[]{:S(2)}, u32[]{:S(2)}) collective-permute-start(bf16[1024,1024]{1,0:T(8,128)(2,1)} %refs_3_.2), channel_id=1, source_target_pairs={{0,1},{1,0},{2,3},{3,2},{4,5},{5,4},{6,7},{7,6},{8,9},{9,8},{10,11... | collective-permute-start | bytes 6291464 | tf_op jit(solution)/shard_map/ppermute | solution.py:716
  171.9 4.4 collective-permute-start.12
  219.9 49.5 %copy-start.17 = (bf16[1536,1024]{1,0:T(8,128)(2,1)}, bf16[1536,1024]{1,0:T(8,128)(2,1)S(1)}, u32[]{:S(2)}) copy-start(bf16[1536,1024]{1,0:T(8,128)(2,1)S(1)} %convolution_convert_fusion.2) | copy-start | bytes 9437188
  233.6 18.9 %collective-permute-start.14 = (bf16[1024,1024]{1,0:T(8,128)(2,1)}, bf16[1024,1024]{1,0:T(8,128)(2,1)}, u32[]{:S(2)}, u32[]{:S(2)}) collective-permute-start(bf16[1024,1024]{1,0:T(8,128)(2,1)} %branch_other.1), channel_id=1, source_target_pairs={{0,1},{1,0},{2,3},{3,2},{4,5},{5,4},{6,7},{7,6},{8,9},{9,8},{10,11... | collective-permute-start | bytes 6291464 | tf_op jit(solution)/shard_map/ppermute | solution.py:716
  269.1 11.9 %collective-permute-start.17 = (bf16[1024,1024]{1,0:T(8,128)(2,1)}, bf16[1024,1024]{1,0:T(8,128)(2,1)}, u32[]{:S(2)}, u32[]{:S(2)}) collective-permute-start(bf16[1024,1024]{1,0:T(8,128)(2,1)} %get-tuple-element.180.refs_0_), channel_id=1, source_target_pairs={{0,1},{1,0},{2,3},{3,2},{4,5},{5,4},{6,7},{7,6},{8,9},{9,8},{10,11... | collective-permute-start | bytes 6291464 | tf_op jit(solution)/shard_map/ppermute | solution.py:716
  270.7 55.4 %collective-permute-start.15 = (bf16[2,1,384,1024]{3,2,1,0:T(8,128)(2,1)}, bf16[2,1,384,1024]{3,2,1,0:T(8,128)(2,1)}, u32[]{:S(2)}, u32[]{:S(2)}) collective-permute-start(bf16[2,1,384,1024]{3,2,1,0:T(8,128)(2,1)} %constant_dynamic-slice_fusion.16), channel_id=1, source_target_pairs={{0,4},{4,0},{8,12},{12,8},{16,20},{20,16},{24,28},{28,24},{1,5},{5... | collective-permute-start | bytes 4718600 | tf_op jit(solution)/shard_map/ppermute | solution.py:716
  277.7 48.4 %collective-permute-start.16 = (bf16[1,2,256,1536]{3,2,1,0:T(8,128)(2,1)}, bf16[1,2,256,1536]{3,2,1,0:T(8,128)(2,1)}, u32[]{:S(2)}, u32[]{:S(2)}) collective-permute-start(bf16[1,2,256,1536]{3,2,1,0:T(8,128)(2,1)} %constant_dynamic-slice_fusion.15), channel_id=1, source_target_pairs={{0,2},{2,0},{1,3},{3,1},{4,6},{6,4},{5,7},{7,5},{8,10},{10,8},{9,1... | collective-permute-start | bytes 4718600 | tf_op jit(solution)/shard_map/ppermute | solution.py:716
  279.5 81.6 %collective-permute-start.20 = (bf16[1,2,256,1536]{3,2,1,0:T(8,128)(2,1)}, bf16[1,2,256,1536]{3,2,1,0:T(8,128)(2,1)}, u32[]{:S(2)}, u32[]{:S(2)}) collective-permute-start(bf16[1,2,256,1536]{3,2,1,0:T(8,128)(2,1)} %constant_dynamic-slice_fusion.12), channel_id=1, source_target_pairs={{0,2},{2,0},{1,3},{3,1},{4,6},{6,4},{5,7},{7,5},{8,10},{10,8},{9,1... | collective-permute-start | bytes 4718600 | tf_op jit(solution)/shard_map/ppermute | solution.py:716
  329.4 31.7 %collective-permute-start.19 = (bf16[1,1,256,1536]{3,2,1,0:T(8,128)(2,1)}, bf16[1,1,256,1536]{3,2,1,0:T(8,128)(2,1)}, u32[]{:S(2)}, u32[]{:S(2)}) collective-permute-start(bf16[1,1,256,1536]{3,2,1,0:T(8,128)(2,1)} %constant_dynamic-slice_fusion.13), channel_id=1, source_target_pairs={{0,4},{4,0},{8,12},{12,8},{16,20},{20,16},{24,28},{28,24},{1,5},{5... | collective-permute-start | bytes 2359304 | tf_op jit(solution)/shard_map/ppermute | solution.py:716
  332.9 32.9 %collective-permute-start.18 = (bf16[1,1,384,1024]{3,2,1,0:T(8,128)(2,1)}, bf16[1,1,384,1024]{3,2,1,0:T(8,128)(2,1)}, u32[]{:S(2)}, u32[]{:S(2)}) collective-permute-start(bf16[1,1,384,1024]{3,2,1,0:T(8,128)(2,1)} %constant_dynamic-slice_fusion.14), channel_id=1, source_target_pairs={{0,2},{2,0},{1,3},{3,1},{4,6},{6,4},{5,7},{7,5},{8,10},{10,8},{9,1... | collective-permute-start | bytes 2359304 | tf_op jit(solution)/shard_map/ppermute | solution.py:716
  336.1 61.8 %collective-permute-start.23 = (bf16[1,2,256,1024]{3,2,1,0:T(8,128)(2,1)}, bf16[1,2,256,1024]{3,2,1,0:T(8,128)(2,1)}, u32[]{:S(2)}, u32[]{:S(2)}) collective-permute-start(bf16[1,2,256,1024]{3,2,1,0:T(8,128)(2,1)} %constant_dynamic-slice_fusion.9), channel_id=1, source_target_pairs={{0,2},{2,0},{1,3},{3,1},{4,6},{6,4},{5,7},{7,5},{8,10},{10,8},{9,1... | collective-permute-start | bytes 3145736 | tf_op jit(solution)/shard_map/ppermute | solution.py:716
  368.4 29.5 %collective-permute-start.22 = (bf16[1,1,256,1536]{3,2,1,0:T(8,128)(2,1)}, bf16[1,1,256,1536]{3,2,1,0:T(8,128)(2,1)S(1)}, u32[]{:S(2)}, u32[]{:S(2)}) collective-permute-start(bf16[1,1,256,1536]{3,2,1,0:T(8,128)(2,1)} %constant_dynamic-slice_fusion.10), channel_id=1, source_target_pairs={{0,4},{4,0},{8,12},{12,8},{16,20},{20,16},{24,28},{28,24},{1,5},{5... | collective-permute-start | bytes 2359304 | tf_op jit(solution)/shard_map/ppermute | solution.py:716
  373.2 24.6 %collective-permute-start.21 = (bf16[768,512]{1,0:T(8,128)(2,1)}, bf16[768,512]{1,0:T(8,128)(2,1)S(1)}, u32[]{:S(2)}, u32[]{:S(2)}) collective-permute-start(bf16[768,512]{1,0:T(8,128)(2,1)} %constant_dynamic-slice_fusion.11), channel_id=1, source_target_pairs={{0,8},{4,12},{8,0},{12,4},{16,24},{20,28},{24,16},{28,20},{1,9},{5... | collective-permute-start | bytes 2359304 | tf_op jit(solution)/shard_map/ppermute | solution.py:716
  397.9 10.8 %copy-start.33 = (bf16[1,1,256,1536]{3,2,1,0:T(8,128)(2,1)}, bf16[1,1,256,1536]{3,2,1,0:T(8,128)(2,1)S(1)}, u32[]{:S(2)}) copy-start(bf16[1,1,256,1536]{3,2,1,0:T(8,128)(2,1)S(1)} %collective-permute-done.22) | copy-start | bytes 2359300
  411.0 34.3 %collective-permute-start.26 = (bf16[1,2,256,1536]{3,2,1,0:T(8,128)(2,1)}, bf16[1,2,256,1536]{3,2,1,0:T(8,128)(2,1)}, u32[]{:S(2)}, u32[]{:S(2)}) collective-permute-start(bf16[1,2,256,1536]{3,2,1,0:T(8,128)(2,1)} %constant_dynamic-slice_fusion.6), channel_id=1, source_target_pairs={{0,2},{2,0},{1,3},{3,1},{4,6},{6,4},{5,7},{7,5},{8,10},{10,8},{9,1... | collective-permute-start | bytes 4718600 | tf_op jit(solution)/shard_map/ppermute | solution.py:716
  414.5 30.8 %collective-permute-start.25 = (bf16[1,1,256,1024]{3,2,1,0:T(8,128)(2,1)}, bf16[1,1,256,1024]{3,2,1,0:T(8,128)(2,1)}, u32[]{:S(2)}, u32[]{:S(2)}) collective-permute-start(bf16[1,1,256,1024]{3,2,1,0:T(8,128)(2,1)} %constant_dynamic-slice_fusion.7), channel_id=1, source_target_pairs={{0,4},{4,0},{8,12},{12,8},{16,20},{20,16},{24,28},{28,24},{1,5},{5... | collective-permute-start | bytes 1572872 | tf_op jit(solution)/shard_map/ppermute | solution.py:716
  415.6 29.7 %collective-permute-start.24 = (bf16[384,512]{1,0:T(8,128)(2,1)S(1)}, bf16[384,512]{1,0:T(8,128)(2,1)S(1)}, u32[]{:S(2)}, u32[]{:S(2)}) collective-permute-start(bf16[384,512]{1,0:T(8,128)(2,1)S(1)} %constant_dynamic-slice_fusion.8), channel_id=1, source_target_pairs={{0,16},{4,20},{8,24},{12,28},{16,0},{20,4},{24,8},{28,12},{1,17},{... | collective-permute-start | bytes 1179656 | tf_op jit(solution)/shard_map/ppermute | solution.py:716
  454.4 26.0 %collective-permute-start.29 = (bf16[1,1,256,1536]{3,2,1,0:T(8,128)(2,1)}, bf16[1,1,256,1536]{3,2,1,0:T(8,128)(2,1)}, u32[]{:S(2)}, u32[]{:S(2)}) collective-permute-start(bf16[1,1,256,1536]{3,2,1,0:T(8,128)(2,1)} %constant_dynamic-slice_fusion.4), channel_id=1, source_target_pairs={{0,4},{4,0},{8,12},{12,8},{16,20},{20,16},{24,28},{28,24},{1,5},{5... | collective-permute-start | bytes 2359304 | tf_op jit(solution)/shard_map/ppermute | solution.py:716
  457.8 21.8 %collective-permute-start.28 = (bf16[640,512]{1,0:T(8,128)(2,1)}, bf16[640,512]{1,0:T(8,128)(2,1)S(1)}, u32[]{:S(2)}, u32[]{:S(2)}) collective-permute-start(bf16[640,512]{1,0:T(8,128)(2,1)} %constant_dynamic-slice_fusion.5), channel_id=1, source_target_pairs={{0,8},{4,12},{8,0},{12,4},{16,24},{20,28},{24,16},{28,20},{1,9},{5... | collective-permute-start | bytes 1966088 | tf_op jit(solution)/shard_map/ppermute | solution.py:716
  458.6 18.7 %collective-permute-start.30 = (bf16[1,2,256,512]{3,2,1,0:T(8,128)(2,1)}, bf16[1,2,256,512]{3,2,1,0:T(8,128)(2,1)}, u32[]{:S(2)}, u32[]{:S(2)}) collective-permute-start(bf16[1,2,256,512]{3,2,1,0:T(8,128)(2,1)} %constant_dynamic-slice_fusion.3), channel_id=1, source_target_pairs={{0,2},{2,0},{1,3},{3,1},{4,6},{6,4},{5,7},{7,5},{8,10},{10,8},{9,1... | collective-permute-start | bytes 1572872 | tf_op jit(solution)/shard_map/ppermute | solution.py:716
  459.6 13.2 %copy-start.29 = (bf16[384,512]{1,0:T(8,128)(2,1)}, bf16[384,512]{1,0:T(8,128)(2,1)S(1)}, u32[]{:S(2)}) copy-start(bf16[384,512]{1,0:T(8,128)(2,1)S(1)} %dynamic-slice_add_fusion.8) | copy-start | bytes 1179652
  459.6 17.8 %collective-permute-start.27 = (bf16[384,512]{1,0:T(8,128)(2,1)S(1)}, bf16[384,512]{1,0:T(8,128)(2,1)S(1)}, u32[]{:S(2)}, u32[]{:S(2)}) collective-permute-start(bf16[384,512]{1,0:T(8,128)(2,1)S(1)} %dynamic-slice_add_fusion.8), channel_id=1, source_target_pairs={{0,16},{4,20},{8,24},{12,28},{16,0},{20,4},{24,8},{28,12},{1,17},{... | collective-permute-start | bytes 1179656 | tf_op jit(solution)/shard_map/ppermute | solution.py:716
  472.8 10.9 %copy-start.28 = (bf16[1280,512]{1,0:T(8,128)(2,1)S(1)}, bf16[1280,512]{1,0:T(8,128)(2,1)}, u32[]{:S(2)}) copy-start(bf16[1280,512]{1,0:T(8,128)(2,1)} %copy-done.27) | copy-start | bytes 3932164
  481.8 24.1 %collective-permute-start.31 = (bf16[768,512]{1,0:T(8,128)(2,1)S(1)}, bf16[768,512]{1,0:T(8,128)(2,1)}, u32[]{:S(2)}, u32[]{:S(2)}) collective-permute-start(bf16[768,512]{1,0:T(8,128)(2,1)S(1)} %maximum_select_fusion.3), channel_id=1, source_target_pairs={{0,8},{4,12},{8,0},{12,4},{16,24},{20,28},{24,16},{28,20},{1,9},{5... | collective-permute-start | bytes 2359304 | tf_op jit(solution)/shard_map/ppermute | solution.py:716
  485.8 17.8 %collective-permute-start.32 = (bf16[320,512]{1,0:T(8,128)(2,1)S(1)}, bf16[320,512]{1,0:T(8,128)(2,1)S(1)}, u32[]{:S(2)}, u32[]{:S(2)}) collective-permute-start(bf16[320,512]{1,0:T(8,128)(2,1)S(1)} %constant_dynamic-slice_fusion.2), channel_id=1, source_target_pairs={{0,16},{4,20},{8,24},{12,28},{16,0},{20,4},{24,8},{28,12},{1,17},{... | collective-permute-start | bytes 983048 | tf_op jit(solution)/shard_map/ppermute | solution.py:716
  488.6 10.6 %collective-permute-start.33 = (bf16[1,1,256,512]{3,2,1,0:T(8,128)(2,1)}, bf16[1,1,256,512]{3,2,1,0:T(8,128)(2,1)}, u32[]{:S(2)}, u32[]{:S(2)}) collective-permute-start(bf16[1,1,256,512]{3,2,1,0:T(8,128)(2,1)} %constant_dynamic-slice_fusion.1), channel_id=1, source_target_pairs={{0,4},{4,0},{8,12},{12,8},{16,20},{20,16},{24,28},{28,24},{1,5},{5... | collective-permute-start | bytes 786440 | tf_op jit(solution)/shard_map/ppermute | solution.py:716
  505.9 8.9 %collective-permute-start.37 = (bf16[1024,1024]{1,0:T(8,128)(2,1)}, bf16[1024,1024]{1,0:T(8,128)(2,1)}, u32[]{:S(2)}, u32[]{:S(2)}) collective-permute-start(bf16[1024,1024]{1,0:T(8,128)(2,1)} %tokens_other.1), channel_id=1, source_target_pairs={{0,1},{1,0},{2,3},{3,2},{4,5},{5,4},{6,7},{7,6},{8,9},{9,8},{10,11... | collective-permute-start | bytes 6291464 | tf_op jit(solution)/shard_map/ppermute | solution.py:716
  507.1 31.7 %collective-permute-start.40 = (bf16[1024,1024]{1,0:T(8,128)(2,1)}, bf16[1024,1024]{1,0:T(8,128)(2,1)}, u32[]{:S(2)}, u32[]{:S(2)}) collective-permute-start(bf16[1024,1024]{1,0:T(8,128)(2,1)} %output_other.1), channel_id=1, source_target_pairs={{0,1},{1,0},{2,3},{3,2},{4,5},{5,4},{6,7},{7,6},{8,9},{9,8},{10,11... | collective-permute-start | bytes 6291464 | tf_op jit(solution)/shard_map/ppermute | solution.py:716
  509.6 21.5 %collective-permute-start.36 = (bf16[128,2048]{1,0:T(8,128)(2,1)}, bf16[128,2048]{1,0:T(8,128)(2,1)}, u32[]{:S(2)}, u32[]{:S(2)}) collective-permute-start(bf16[128,2048]{1,0:T(8,128)(2,1)} %fusion), channel_id=1, source_target_pairs={{0,8},{4,12},{8,0},{12,4},{16,24},{20,28},{24,16},{28,20},{1,9},{5... | collective-permute-start | bytes 1572872 | tf_op jit(solution)/shard_map/ppermute | solution.py:716
  511.6 59.2 %copy-start.2 = (bf16[1536,512]{1,0:T(8,128)(2,1)}, bf16[1536,512]{1,0:T(8,128)(2,1)S(1)}, u32[]{:S(2)}) copy-start(bf16[1536,512]{1,0:T(8,128)(2,1)S(1)} %maximum_select_fusion.refs_0_) | copy-start | bytes 4718596
  511.6 37.3 %collective-permute-start.34 = (bf16[1536,512]{1,0:T(8,128)(2,1)S(1)}, bf16[1536,512]{1,0:T(8,128)(2,1)S(1)}, u32[]{:S(2)}, u32[]{:S(2)}) collective-permute-start(bf16[1536,512]{1,0:T(8,128)(2,1)S(1)} %maximum_select_fusion.refs_0_), channel_id=1, source_target_pairs={{0,4},{4,0},{8,12},{12,8},{16,20},{20,16},{24,28},{28,24},{1,5},{5... | collective-permute-start | bytes 4718600 | tf_op jit(solution)/shard_map/ppermute | solution.py:716
  513.5 15.3 %collective-permute-start.35 = (bf16[320,512]{1,0:T(8,128)(2,1)}, bf16[320,512]{1,0:T(8,128)(2,1)}, u32[]{:S(2)}, u32[]{:S(2)}) collective-permute-start(bf16[320,512]{1,0:T(8,128)(2,1)} %dynamic-slice_add_fusion.9), channel_id=1, source_target_pairs={{0,16},{4,20},{8,24},{12,28},{16,0},{20,4},{24,8},{28,12},{1,17},{... | collective-permute-start | bytes 983048 | tf_op jit(solution)/shard_map/ppermute | solution.py:716
  533.1 15.8 %collective-permute-start.38 = (bf16[64,2048]{1,0:T(8,128)(2,1)S(1)}, bf16[64,2048]{1,0:T(8,128)(2,1)}, u32[]{:S(2)}, u32[]{:S(2)}) collective-permute-start(bf16[64,2048]{1,0:T(8,128)(2,1)S(1)} %constant_dynamic-slice_fusion), channel_id=1, source_target_pairs={{0,16},{4,20},{8,24},{12,28},{16,0},{20,4},{24,8},{28,12},{1,17},{... | collective-permute-start | bytes 786440 | tf_op jit(solution)/shard_map/ppermute | solution.py:716
  534.5 14.4 %collective-permute-start.39 = (f32[2304]{0:T(1024)S(1)}, f32[2304]{0:T(1024)S(1)}, u32[]{:S(2)}, u32[]{:S(2)}) collective-permute-start(f32[2304]{0:T(1024)S(1)} %pad_maximum_fusion.2), channel_id=1, source_target_pairs={{0,1},{1,0},{2,3},{3,2},{4,5},{5,4},{6,7},{7,6},{8,9},{9,8},{10,11... | collective-permute-start | bytes 27656 | tf_op jit(solution)/shard_map/ppermute | solution.py:716
  536.9 28.6 %collective-permute-start.41 = (bf16[640,512]{1,0:T(8,128)(2,1)}, bf16[640,512]{1,0:T(8,128)(2,1)}, u32[]{:S(2)}, u32[]{:S(2)}) collective-permute-start(bf16[640,512]{1,0:T(8,128)(2,1)} %maximum_select_fusion.4), channel_id=1, source_target_pairs={{0,8},{4,12},{8,0},{12,4},{16,24},{20,28},{24,16},{28,20},{1,9},{5... | collective-permute-start | bytes 1966088 | tf_op jit(solution)/shard_map/ppermute | solution.py:716
  548.9 16.6 %copy-start.7 = (bf16[1536,512]{1,0:T(8,128)(2,1)}, bf16[1536,512]{1,0:T(8,128)(2,1)S(1)}, u32[]{:S(2)}) copy-start(bf16[1536,512]{1,0:T(8,128)(2,1)S(1)} %collective-permute-done.34.refs_1_) | copy-start | bytes 4718596
  550.4 15.1 %collective-permute-start.42 = (bf16[64,2048]{1,0:T(8,128)(2,1)S(1)}, bf16[64,2048]{1,0:T(8,128)(2,1)S(1)}, u32[]{:S(2)}, u32[]{:S(2)}) collective-permute-start(bf16[64,2048]{1,0:T(8,128)(2,1)S(1)} %dynamic-slice_add_fusion.10), channel_id=1, source_target_pairs={{0,16},{4,20},{8,24},{12,28},{16,0},{20,4},{24,8},{28,12},{1,17},{... | collective-permute-start | bytes 786440 | tf_op jit(solution)/shard_map/ppermute | solution.py:716
  551.3 3.7 collective-permute-start.43
  567.6 31.8 %copy-start.3 = (bf16[1280,512]{1,0:T(8,128)(2,1)}, bf16[1280,512]{1,0:T(8,128)(2,1)S(1)}, u32[]{:S(2)}) copy-start(bf16[1280,512]{1,0:T(8,128)(2,1)S(1)} %maximum_select_fusion.1.refs_2_) | copy-start | bytes 3932164
  567.6 31.8 %collective-permute-start.46 = (bf16[1280,512]{1,0:T(8,128)(2,1)S(1)}, bf16[1280,512]{1,0:T(8,128)(2,1)}, u32[]{:S(2)}, u32[]{:S(2)}) collective-permute-start(bf16[1280,512]{1,0:T(8,128)(2,1)S(1)} %maximum_select_fusion.1.refs_2_), channel_id=1, source_target_pairs={{0,4},{4,0},{8,12},{12,8},{16,20},{20,16},{24,28},{28,24},{1,5},{5... | collective-permute-start | bytes 3932168 | tf_op jit(solution)/shard_map/ppermute | solution.py:716
  568.6 13.2 %collective-permute-start.44 = (bf16[128,2048]{1,0:T(8,128)(2,1)S(1)}, bf16[128,2048]{1,0:T(8,128)(2,1)}, u32[]{:S(2)}, u32[]{:S(2)}) collective-permute-start(bf16[128,2048]{1,0:T(8,128)(2,1)S(1)} %maximum_select_fusion.5), channel_id=1, source_target_pairs={{0,8},{4,12},{8,0},{12,4},{16,24},{20,28},{24,16},{28,20},{1,9},{5... | collective-permute-start | bytes 1572872 | tf_op jit(solution)/shard_map/ppermute | solution.py:716
  568.7 13.1 %collective-permute-start.45 = (f32[2304]{0:T(1024)S(1)}, f32[2304]{0:T(1024)S(1)}, u32[]{:S(2)}, u32[]{:S(2)}) collective-permute-start(f32[2304]{0:T(1024)S(1)} %add.233), channel_id=1, source_target_pairs={{0,8},{4,12},{8,0},{12,4},{16,24},{20,28},{24,16},{28,20},{1,9},{5... | collective-permute-start | bytes 27656 | tf_op jit(solution)/shard_map/ppermute | solution.py:716
  572.8 35.6 %collective-permute-start.49 = (bf16[768,512]{1,0:T(8,128)(2,1)}, bf16[768,512]{1,0:T(8,128)(2,1)}, u32[]{:S(2)}, u32[]{:S(2)}) collective-permute-start(bf16[768,512]{1,0:T(8,128)(2,1)} %slice_select_fusion.1), channel_id=1, source_target_pairs={{0,1},{1,0},{2,3},{3,2},{4,5},{5,4},{6,7},{7,6},{8,9},{9,8},{10,11... | collective-permute-start | bytes 2359304 | tf_op jit(solution)/shard_map/ppermute | solution.py:716
  581.9 4.6 collective-permute-start.47
  583.5 37.0 %collective-permute-start.48 = (bf16[256,2048]{1,0:T(8,128)(2,1)S(1)}, bf16[256,2048]{1,0:T(8,128)(2,1)}, u32[]{:S(2)}, u32[]{:S(2)}) collective-permute-start(bf16[256,2048]{1,0:T(8,128)(2,1)S(1)} %maximum_select_fusion.2), channel_id=1, source_target_pairs={{0,4},{4,0},{8,12},{12,8},{16,20},{20,16},{24,28},{28,24},{1,5},{5... | collective-permute-start | bytes 3145736 | tf_op jit(solution)/shard_map/ppermute | solution.py:716
  601.5 6.9 %collective-permute-start.50 = (bf16[768,512]{1,0:T(8,128)(2,1)}, bf16[768,512]{1,0:T(8,128)(2,1)S(1)}, u32[]{:S(2)}, u32[]{:S(2)}) collective-permute-start(bf16[768,512]{1,0:T(8,128)(2,1)} %slice_select_fusion), channel_id=1, source_target_pairs={{0,1},{1,0},{2,3},{3,2},{4,5},{5,4},{6,7},{7,6},{8,9},{9,8},{10,11... | collective-permute-start | bytes 2359304 | tf_op jit(solution)/shard_map/ppermute | solution.py:716
  601.6 18.9 %collective-permute-start.51 = (f32[2304]{0:T(1024)S(1)}, f32[2304]{0:T(1024)S(1)}, u32[]{:S(2)}, u32[]{:S(2)}) collective-permute-start(f32[2304]{0:T(1024)S(1)} %add.235), channel_id=1, source_target_pairs={{0,4},{4,0},{8,12},{12,8},{16,20},{20,16},{24,28},{28,24},{1,5},{5... | collective-permute-start | bytes 27656 | tf_op jit(solution)/shard_map/ppermute | solution.py:716
  622.8 2.7 collective-permute-start.52
  (44 other events, 169.3 us)

commit v3 on v2

--- a/solution.py
+++ b/solution.py
@@ -787,8 +787,8 @@
 
                 @pl.when((info_ref[0] == c) & (info_ref[1] == side))
                 def _():
-                    for n in range(2):
-                        own, got = ins[2 * n + (c != side)], ins[4 + n]
+                    for n in range(len(gots)):
+                        own, got = ins[2 * n + (c != side)], ins[2 * len(gots) + n]
                         for half, ref in ((c, own), (1 - c, got)):
                             for at in range(0, 2 * quarter, piece):
                                 r, col = at // STRIP * rows, at % STRIP
@@ -805,7 +805,7 @@
         info,
         [const(a) for pair in values for a in pair] + [const(g) for g in gots],
         [],
-        [(struct(rows, 4 * quarter, F32), (rows, 4 * quarter), once)] * 2,
+        [(struct(rows, 4 * quarter, F32), (rows, 4 * quarter), once)] * len(gots),
         5,
     )
 
@@ -1121,17 +1121,27 @@
     hidden, tokens_grad = fence(hidden, tokens_grad)
     output = output_own(order, info, hidden, middle, out_got, wd)
     if pairs:
-        early_far, last_got, hop, output = fence(early_far, last_got, hop, output)
+        last_got, hop, output = fence(last_got, hop, output)
         last = add_half(last, last_got, replica, 2)
         last_got = swap(last, "rep", 2)
         small = small + hop
         hop = swap(small, "fsdp")
-
-        late_got, last_got, hop = fence(late_got, last_got, hop)
+        home = core == side
+        gu_rows = early.shape[0] // 2
+
+        def finish(own, far):
+            send = jnp.where(home, far[:gu_rows], own[:gu_rows])
+            columns = finish_gu(info, [(own, far)], [swap(send, "seq")], quarter)
+            return columns + finish_rows(info, [(own, far)], [gu_rows], width)
+
+        late_got, early_far, output = fence(late_got, early_far, output)
+        late = double(late, late_got, replica, 1)
+        late_far = swap(late, "rep", 0)
+        g_gate, g_down = finish(early, early_far)
+
+        last_got, hop, g_gate, g_down = fence(last_got, hop, g_gate, g_down)
         last = double(last, last_got, replica, 2)
         last_got = swap(last, "rep", 1)
-        late = double(late, late_got, replica, 1)
-        late_far = swap(late, "rep", 0)
         small = small + hop
         hop = swap(small, "rep", 1)
 
@@ -1144,16 +1154,9 @@
         late_far, hop = fence(late_far, hop)
         small = small + hop
         hop = swap(small, "rep", 0)
-        home = core == side
-        gu_rows = early.shape[0] // 2
-        values = [(early, early_far), (late, late_far)]
-        gots = [swap(jnp.where(home, b[:gu_rows], a[:gu_rows]), "seq") for a, b in values]
-        g_gate, g_up = finish_gu(info, values, gots, quarter)
-        g_down, g_o = finish_rows(info, values, [gu_rows, gu_rows], width)
-
-        last_far, g_gate, g_up, g_down, g_o, hop = fence(
-            last_far, g_gate, g_up, g_down, g_o, hop
-        )
+        g_up, g_o = finish(late, late_far)
+
+        last_far, g_up, g_o, hop = fence(last_far, g_up, g_o, hop)
         small = small + hop
         keep, send = jnp.where(home, last, last_far), jnp.where(home, last_far, last)
         qkv_parts = [keep], [swap(send, "seq")]

time: 636 us -> 629 us (0.989)
  waiting for transfers between devices: 108 us -> 100 us
    ppermute x51, waiting for transfers between devices: 102 us -> 94.2 us  [swap(): return lax.ppermute(value, axis, [(i, i ^ 1 << bit) for i in range(size)])]
    pallas_call x16 -> x18, Pallas kernels: 180 us -> 184 us  [tiled(): pl.pallas_call(kernel, grid_spec=pltpu.PrefetchScalarGridSpec(num_scalar_...]
    unnamed x121 -> x125, local copies, waits for them, and re-layouts: 15.3 us -> 14 us
  transfers between devices with their start and end apart: 53 -> 53, of which waited for: 20 -> 21; matrix products, arithmetic and copies ran while one was open for 15% -> 15% of each run, Pallas kernels for 41% -> 42%
where the time goes in v3:
time: 629 us; the launch traced here: 625 us
  Pallas kernels  332 us (53%)
  waiting for transfers between devices  100 us (16%)
  matrix products  54.4 us (9%)
  starting transfers between devices  50.9 us (8%)
  other arithmetic  48.1 us (8%)
  local copies, waits for them, and re-layouts  37.7 us (6%)
    pallas_call x18, Pallas kernels, tiled(): pl.pallas_call(kernel, grid_spec=pltpu.PrefetchScalarGridSpec(num_scalar_...  184 us
    pallas_call x4, Pallas kernels, attend_back(): pl.pallas_call(body, grid_spec=pltpu.PrefetchScalarGridSpec(num_scalar_pr...  95 us
    ppermute x51, waiting for transfers between devices, swap(): return lax.ppermute(value, axis, [(i, i ^ 1 << bit) for i in range(size)])  94.2 us
    dot_general x5, matrix products, tn(): lax.dot_general(a, b, (((0,), (0,)), ((), ())), preferred_element_type=F32)  54.4 us
    pallas_call x3, Pallas kernels, attend(): pl.pallas_call(body, grid_spec=pltpu.PrefetchScalarGridSpec(num_scalar_pr...  53 us
    ppermute x51, starting transfers between devices, swap(): return lax.ppermute(value, axis, [(i, i ^ 1 << bit) for i in range(size)])  50.1 us
    dynamic_slice x17, local copies, waits for them, and re-layouts, part(): return lax.dynamic_slice_in_dim(value, index * size, size, axis)  15.6 us
    unnamed x125, local copies, waits for them, and re-layouts  14 us
  transfers between devices with their start and end apart: 53, of which 21 were waited for; matrix products, arithmetic and copies ran while one was open for 15% of the time, Pallas kernels for 42%

profile of v3, /device:TPU:0, one launch (start us, length us, event | category | flops | bytes accessed | tf_op | source)
XLA Modules:
  0.0 625.3 jit_solution(17729431597474995265)
XLA Ops:
  1.4 3.8 pack_qkv.1
  5.6 2.5 collective-permute-start.1
  10.7 4.9 pack_gu.1
  15.8 5.7 fusion.3
  22.0 4.2 pad_maximum_fusion
  26.3 6.1 collective-permute-done.5
  37.2 20.7 %collective-permute-done.3.refs_9_.refs_5_ = bf16[256,2048]{1,0:T(8,128)(2,1)S(1)} collective-permute-done((bf16[256,2048]{1,0:T(8,128)(2,1)}, bf16[256,2048]{1,0:T(8,128)(2,1)S(1)}, u32[]{:S(2)}, u32[]{:S(2)}) %collective-permute-start.3) | collective-permute-done | bytes 1048608 | tf_op jit(solution)/shard_map/ppermute | solution.py:716
  62.9 19.2 %project.1 = (bf16[2048,1024]{1,0:T(8,128)(2,1)}, bf16[2048,2048]{1,0:T(8,128)(2,1)}, bf16[2048,1536]{1,0:T(8,128)(2,1)}) custom-call(s32[14]{0:T(128)} %stack.53.info_ref, bf16[1024,1024]{1,0:T(8,128)(2,1)} %refs_3_.3, bf16[1024,1024]{1,0:T(8,128)(2,1)} %collective-permute-done.refs_1_, f32[1,1024]{1,0:T(1,128)} %bitcast.74, ...), custom_call_target="tpu_custom_call" | custom-call | flops 170000000 | tf_op jit(solution)/shard_map/project/pallas_call | solution.py:83
  82.1 14.1 %attend.3 = (bf16[2048,1024]{1,0:T(8,128)(2,1)}, f32[4,2,2048]{2,1,0:T(2,128)}) custom-call(s32[8]{0:T(128)} %and_select_fusion.low_ref.refs_0_, bf16[2048,2048]{1,0:T(8,128)(2,1)} %get-tuple-element.146.qkv_ref.refs_1_, s32[2048,1]{1,0:T(8,128)} %copy.38.start_ref), custom_call_target="tpu_custom_call" | custom-call | flops 115000000 | tf_op jit(solution)/shard_map/attend/pallas_call | solution.py:467
  96.3 24.8 %attend.4 = (bf16[2048,1024]{1,0:T(8,128)(2,1)}, f32[4,2,2048]{2,1,0:T(2,128)}) custom-call(s32[8]{0:T(128)} %and_select_fusion.low_ref.refs_0_, bf16[2048,2048]{1,0:T(8,128)(2,1)} %get-tuple-element.146.qkv_ref.refs_1_, s32[2048,1]{1,0:T(8,128)} %copy.38.start_ref, ...), custom_call_target="tpu_custom_call", output_to_operand_aliasing={{0}: (3, {}), {1}: (4, {})} | custom-call | flops 230000000 | tf_op jit(solution)/shard_map/attend/pallas_call | solution.py:467
  123.6 14.1 %attend.5 = (bf16[2048,1024]{1,0:T(8,128)(2,1)}, f32[4,2,2048]{2,1,0:T(2,128)}) custom-call(s32[8]{0:T(128)} %and_select_fusion.low_ref.refs_0_, bf16[2048,2048]{1,0:T(8,128)(2,1)} %get-tuple-element.146.qkv_ref.refs_1_, s32[2048,1]{1,0:T(8,128)} %copy.38.start_ref, ...), custom_call_target="tpu_custom_call", output_to_operand_aliasing={{0}: (3, {}), {1}: (4, {})} | custom-call | flops 115000000 | tf_op jit(solution)/shard_map/attend/pallas_call | solution.py:467
  137.7 7.5 %mix_other.1 = bf16[1024,1024]{1,0:T(8,128)(2,1)} custom-call(s32[14]{0:T(128)} %stack.53.info_ref, bf16[2048,1024]{1,0:T(8,128)(2,1)} %get-tuple-element.158.refs_0_.refs_3_, bf16[512,1024]{1,0:T(8,128)(2,1)} %refs_2_.4, bf16[512,1024]{1,0:T(8,128)(2,1)} %copy-done.9), custom_call_target="tpu_custom_call" | custom-call | flops 50000000 | tf_op jit(solution)/shard_map/mix_other/pallas_call | solution.py:83
  145.3 12.0 %collective-permute-done.10.refs_9_.refs_2_.refs_4_ = bf16[768,1024]{1,0:T(8,128)(2,1)} collective-permute-done((bf16[768,1024]{1,0:T(8,128)(2,1)}, bf16[768,1024]{1,0:T(8,128)(2,1)}, u32[]{:S(2)}, u32[]{:S(2)}) %collective-permute-start.10) | collective-permute-done | bytes 1572896 | tf_op jit(solution)/shard_map/ppermute | solution.py:716
  158.9 3.4 collective-permute-done.11.refs_2_
  162.3 9.5 %mix_own.1 = (f32[1024,1024]{1,0:T(8,128)}, bf16[1024,1024]{1,0:T(8,128)(2,1)}) custom-call(s32[14]{0:T(128)} %stack.53.info_ref, bf16[2048,1024]{1,0:T(8,128)(2,1)} %get-tuple-element.158.refs_0_.refs_3_, bf16[1024,1024]{1,0:T(8,128)(2,1)} %refs_3_.3, bf16[1024,1024]{1,0:T(8,128)(2,1)} %collective-permute-done.11.refs_2_, f32[1,1024]{1,0:T(1,128)} %bitcast.76, ...), custom_call_target="tpu_custom_call" | custom-call | flops 60000000 | tf_op jit(solution)/shard_map/mix_own/pallas_call | solution.py:83
  172.1 4.2 collective-permute-done.12.refs_1_
  177.6 32.0 %mlp.1 = (bf16[2048,1536]{1,0:T(8,128)(2,1)}, bf16[2048,3072]{1,0:T(8,128)(2,1)}, bf16[2048,1024]{1,0:T(8,128)(2,1)}, bf16[2048,1024]{1,0:T(8,128)(2,1)}) custom-call(s32[14]{0:T(128)} %stack.53.info_ref, bf16[1024,1024]{1,0:T(8,128)(2,1)} %get-tuple-element.163.refs_0_, bf16[1024,1024]{1,0:T(8,128)(2,1)} %copy-done.24, bf16[1024,1024]{1,0:T(8,128)(2,1)} %refs_3_.2, ...), custom_call_target="tpu_custom_call" | custom-call | flops 300000000 | tf_op jit(solution)/shard_map/mlp/pallas_call | solution.py:83
  209.6 10.3 %convolution_convert_fusion.2 = bf16[1536,1024]{1,0:T(8,128)(2,1)S(1)} fusion(bf16[2048,1536]{1,0:T(8,128)(2,1)} %get-tuple-element.229.refs_0_, bf16[2048,1024]{1,0:T(8,128)(2,1)} %get-tuple-element.168), kind=kOutput, calls=%fused_computation.3 | convolution fusion | flops 6444023808 | bytes 13631488 | tf_op jit(solution)/shard_map/dot_general | solution.py:31
  220.0 13.6 %branch_other.1 = bf16[1024,1024]{1,0:T(8,128)(2,1)} custom-call(s32[14]{0:T(128)} %stack.53.info_ref, bf16[2048,3072]{1,0:T(8,128)(2,1)} %get-tuple-element.174.refs_0_, bf16[256,3072]{1,0:T(8,128)(2,1)} %get-tuple-element.137.refs_4_.refs_1_.refs_5_, bf16[256,3072]{1,0:T(8,128)(2,1)} %copy-done.1, bf16[256,3072]{1,0:T(8,128)(2,1)} %copy-done.4, ...), custom_call_target="tpu_custom_call" | custom-call | flops 90000000 | tf_op jit(solution)/shard_map/branch_other/pallas_call | solution.py:83
  233.8 18.7 %convolution_convert_fusion = bf16[1024,3072]{1,0:T(8,128)(2,1)} fusion(bf16[2048,1024]{1,0:T(8,128)(2,1)} %get-tuple-element.171, bf16[2048,3072]{1,0:T(8,128)(2,1)} %get-tuple-element.174.refs_0_), kind=kOutput, calls=%fused_computation.1 | convolution fusion | flops 12888047616 | bytes 23068672 | tf_op jit(solution)/shard_map/dot_general | solution.py:31
  252.5 16.5 %branch_own.1 = (f32[1024,1024]{1,0:T(8,128)}, bf16[1024,1024]{1,0:T(8,128)(2,1)}, f32[1,1024]{1,0:T(1,128)}) custom-call(s32[14]{0:T(128)} %stack.53.info_ref, bf16[2048,3072]{1,0:T(8,128)(2,1)} %get-tuple-element.174.refs_0_, bf16[1024,1024]{1,0:T(8,128)(2,1)} %collective-permute-done.14.refs_1_, f32[1024,1024]{1,0:T(8,128)} %get-tuple-element.176.refs_2_.refs_1_, ...), custom_call_target="tpu_custom_call" | custom-call | flops 110000000 | tf_op jit(solution)/shard_map/branch_own/pallas_call | solution.py:83
  271.0 3.2 fusion.6
  279.7 12.1 %attended_back.1 = (bf16[2048,1024]{1,0:T(8,128)(2,1)}, bf16[2048,1024]{1,0:T(8,128)(2,1)}) custom-call(s32[14]{0:T(128)} %stack.53.info_ref, bf16[1024,1024]{1,0:T(8,128)(2,1)} %get-tuple-element.177.refs_0_, bf16[1024,1024]{1,0:T(8,128)(2,1)} %collective-permute-done.17.refs_1_, bf16[512,1024]{1,0:T(8,128)(2,1)} %refs_2_.4, bf16[512,1024]{1,0:T(8,128)(2,1)} %copy-done.9), custom_call_target="tpu_custom_call" | custom-call | flops 80000000 | tf_op jit(solution)/shard_map/attended_back/pallas_call | solution.py:83
  291.8 9.4 %convolution_convert_fusion.3 = bf16[1024,1024]{1,0:T(8,128)(2,1)} fusion(bf16[2048,1024]{1,0:T(8,128)(2,1)} %get-tuple-element.158.refs_0_.refs_3_, bf16[2048,1024]{1,0:T(8,128)(2,1)} %get-tuple-element.179), kind=kOutput, calls=%fused_computation.4 | convolution fusion | flops 4296015872 | bytes 10485760 | tf_op jit(solution)/shard_map/dot_general | solution.py:31
  301.2 23.7 %attend_back.4 = (bf16[2048,1536]{1,0:T(8,128)(2,1)}, f32[2,128]{1,0:T(2,128)}) custom-call(s32[8]{0:T(128)} %and_select_fusion.low_ref.refs_0_, bf16[2048,2048]{1,0:T(8,128)(2,1)} %get-tuple-element.146.qkv_ref.refs_1_, bf16[2048,1024]{1,0:T(8,128)(2,1)} %get-tuple-element.198.refs_2_, bf16[2048,1024]{1,0:T(8,128)(2,1)} %get-tuple-element.158.refs_0_.refs_3_, ...), custom_call_target="tpu_custom_call" | custom-call | flops 210000000 | tf_op jit(solution)/shard_map/attend_back/pallas_call | solution.py:605
  324.9 2.2 dynamic-slice_add_fusion.1
  332.0 2.3 constant_dynamic-slice_fusion.9
  335.5 23.9 %attend_back.5 = (bf16[2048,1536]{1,0:T(8,128)(2,1)}, f32[2,128]{1,0:T(2,128)}) custom-call(s32[8]{0:T(128)} %and_select_fusion.low_ref.refs_0_, bf16[2048,2048]{1,0:T(8,128)(2,1)} %get-tuple-element.146.qkv_ref.refs_1_, bf16[2048,1024]{1,0:T(8,128)(2,1)} %get-tuple-element.198.refs_2_, ...), custom_call_target="tpu_custom_call", output_to_operand_aliasing={{0}: (10, {})} | custom-call | flops 210000000 | tf_op jit(solution)/shard_map/attend_back/pallas_call | solution.py:605
  359.4 5.3 collective-permute-done.18
  372.4 2.4 collective-permute-start.21
  374.8 23.8 %attend_back.6 = (bf16[2048,1536]{1,0:T(8,128)(2,1)}, f32[2,128]{1,0:T(2,128)}) custom-call(s32[8]{0:T(128)} %and_select_fusion.low_ref.refs_0_, bf16[2048,2048]{1,0:T(8,128)(2,1)} %get-tuple-element.146.qkv_ref.refs_1_, bf16[2048,1024]{1,0:T(8,128)(2,1)} %get-tuple-element.198.refs_2_, ...), custom_call_target="tpu_custom_call", output_to_operand_aliasing={{0}: (10, {})} | custom-call | flops 210000000 | tf_op jit(solution)/shard_map/attend_back/pallas_call | solution.py:605
  398.7 10.7 %convolution_convert_fusion.1 = bf16[1024,1536]{1,0:T(8,128)(2,1)S(1)} fusion(bf16[2048,1024]{1,0:T(8,128)(2,1)} %get-tuple-element.196, bf16[2048,1536]{1,0:T(8,128)(2,1)} %get-tuple-element.197.refs_0_), kind=kOutput, calls=%fused_computation.2 | convolution fusion | flops 6444023808 | bytes 13631488 | tf_op jit(solution)/shard_map/dot_general | solution.py:31
  415.1 3.0 collective-permute-start.24
  419.0 23.7 %attend_back.7 = (bf16[2048,512]{1,0:T(8,128)(2,1)}, f32[2,128]{1,0:T(2,128)}) custom-call(s32[8]{0:T(128)} %and_select_fusion.low_ref.refs_0_, bf16[2048,2048]{1,0:T(8,128)(2,1)} %get-tuple-element.146.qkv_ref.refs_1_, bf16[2048,1024]{1,0:T(8,128)(2,1)} %get-tuple-element.198.refs_2_, bf16[2048,1024]{1,0:T(8,128)(2,1)} %get-tuple-element.158.refs_0_.refs_3_, ...), custom_call_target="tpu_custom_call" | custom-call | flops 210000000 | tf_op jit(solution)/shard_map/attend_back/pallas_call | solution.py:605
  444.1 1.9 collective-permute-done.26
  446.0 5.4 convolution_convert_fusion.4
  451.4 2.0 dynamic-slice_add_fusion
  460.0 2.5 collective-permute-start.27
  462.5 10.2 %tokens_other.1 = bf16[1024,1024]{1,0:T(8,128)(2,1)} custom-call(s32[14]{0:T(128)} %stack.53.info_ref, bf16[2048,1536]{1,0:T(8,128)(2,1)} %get-tuple-element.197.refs_0_, bf16[2048,512]{1,0:T(8,128)(2,1)} %get-tuple-element.205.refs_1_, bf16[256,2048]{1,0:T(8,128)(2,1)} %get-tuple-element.133.refs_6_.refs_2_, ...), custom_call_target="tpu_custom_call" | custom-call | flops 60000000 | tf_op jit(solution)/shard_map/tokens_other/pallas_call | solution.py:83
  472.8 4.3 collective-permute-done.27
  480.7 2.8 collective-permute-start.31
  489.5 9.1 %output_other.1 = bf16[1024,1024]{1,0:T(8,128)(2,1)} custom-call(s32[14]{0:T(128)} %stack.53.info_ref, bf16[2048,1536]{1,0:T(8,128)(2,1)} %get-tuple-element.229.refs_0_, bf16[768,1024]{1,0:T(8,128)(2,1)} %refs_3_.4, bf16[768,1024]{1,0:T(8,128)(2,1)} %collective-permute-done.10.refs_9_.refs_2_.refs_4_), custom_call_target="tpu_custom_call" | custom-call | flops 60000000 | tf_op jit(solution)/shard_map/output_other/pallas_call | solution.py:83
  498.6 4.4 collective-permute-done.32
  507.6 3.7 collective-permute-start.35
  511.2 1.9 maximum_select_fusion.refs_0_
  514.3 1.8 collective-permute-start.34
  516.2 13.3 %tokens_own.1 = (f32[1024,1024]{1,0:T(8,128)}, f32[1,1024]{1,0:T(1,128)}) custom-call(s32[14]{0:T(128)} %stack.53.info_ref, bf16[2048,1536]{1,0:T(8,128)(2,1)} %get-tuple-element.197.refs_0_, bf16[2048,512]{1,0:T(8,128)(2,1)} %get-tuple-element.205.refs_1_, bf16[1024,1024]{1,0:T(8,128)(2,1)} %collective-permute-done.36.refs_2_, bf16[1024,1024]{1,0:T(8,128)(2,1)} %refs_3_.3, ...), custom_call_target="tpu_custom_call" | custom-call | flops 90000000 | tf_op jit(solution)/shard_map/tokens_own/pallas_call | solution.py:83
  530.9 2.3 maximum_select_fusion.4
  533.2 1.9 collective-permute-start.37
  539.0 10.1 %output_own.1 = bf16[1024,1024]{1,0:T(8,128)(2,1)} custom-call(s32[14]{0:T(128)} %stack.53.info_ref, bf16[2048,1536]{1,0:T(8,128)(2,1)} %get-tuple-element.229.refs_0_, f32[1024,1024]{1,0:T(8,128)} %get-tuple-element.176.refs_2_.refs_1_, bf16[1024,1024]{1,0:T(8,128)(2,1)} %collective-permute-done.41.refs_2_, bf16[768,1024]{1,0:T(8,128)(2,1)} %refs_3_.4, ...), custom_call_target="tpu_custom_call" | custom-call | flops 60000000 | tf_op jit(solution)/shard_map/output_own/pallas_call | solution.py:83
  549.1 5.6 collective-permute-done.39
  556.5 2.1 maximum_select_fusion.1.refs_0_
  558.6 1.9 collective-permute-start.47
  563.7 4.4 finish_rows.2
  568.1 4.6 finish_gu.2
  572.7 3.8 collective-permute-done.42
  576.7 2.0 collective-permute-start.46
  578.8 11.6 %collective-permute-done.46 = f32[2304]{0:T(1024)S(1)} collective-permute-done((f32[2304]{0:T(1024)S(1)}, f32[2304]{0:T(1024)S(1)}, u32[]{:S(2)}, u32[]{:S(2)}) %collective-permute-start.46) | collective-permute-done | bytes 9248 | tf_op jit(solution)/shard_map/ppermute | solution.py:716
  592.2 2.8 collective-permute-done.48
  594.9 2.1 slice_select_fusion
  597.5 3.8 finish_rows.3
  602.2 4.5 finish_gu.3
  606.7 8.9 %collective-permute-done.51 = f32[2304]{0:T(1024)S(1)} collective-permute-done((f32[2304]{0:T(1024)S(1)}, f32[2304]{0:T(1024)S(1)}, u32[]{:S(2)}, u32[]{:S(2)}) %collective-permute-start.51) | collective-permute-done | bytes 9248 | tf_op jit(solution)/shard_map/ppermute | solution.py:716
  620.4 4.7 unpack_qkv.1
  (277 shorter events, 89.5 us)
Async XLA Ops:
  5.2 5.5 collective-permute-start.2
  5.6 31.5 %collective-permute-start.1 = (bf16[256,2048]{1,0:T(8,128)(2,1)}, bf16[256,2048]{1,0:T(8,128)(2,1)}, u32[]{:S(2)}, u32[]{:S(2)}) collective-permute-start(bf16[256,2048]{1,0:T(8,128)(2,1)} %get-tuple-element.133.refs_6_.refs_2_), channel_id=1, source_target_pairs={{0,2},{2,0},{1,3},{3,1},{4,6},{6,4},{5,7},{7,5},{8,10},{10,8},{9,1... | collective-permute-start | bytes 3145736 | tf_op jit(solution)/shard_map/ppermute | solution.py:716
  8.3 13.2 %collective-permute-start.4 = (bf16[1,576]{1,0:T(2,128)(2,1)S(1)}, bf16[1,576]{1,0:T(2,128)(2,1)S(1)}, u32[]{:S(2)}, u32[]{:S(2)}) collective-permute-start(bf16[1,576]{1,0:T(2,128)(2,1)S(1)} %broadcast_in_dim.2), channel_id=1, source_target_pairs={{0,1},{1,0},{2,3},{3,2},{4,5},{5,4},{6,7},{7,6},{8,9},{9,8},{10,11... | collective-permute-start | bytes 3464 | tf_op jit(solution)/shard_map/ppermute | solution.py:895
  8.5 54.4 %collective-permute-start = (bf16[1024,1024]{1,0:T(8,128)(2,1)}, bf16[1024,1024]{1,0:T(8,128)(2,1)}, u32[]{:S(2)}, u32[]{:S(2)}) collective-permute-start(bf16[1024,1024]{1,0:T(8,128)(2,1)} %refs_3_.3), channel_id=1, source_target_pairs={{0,1},{1,0},{2,3},{3,2},{4,5},{5,4},{6,7},{7,6},{8,9},{9,8},{10,11... | collective-permute-start | bytes 6291464 | tf_op jit(solution)/shard_map/ppermute | solution.py:716
  10.6 50.3 %copy-start.45 = (s32[2048]{0:T(1024)}, s32[2048]{0:T(1024)S(1)}, u32[]{:S(2)}) copy-start(s32[2048]{0:T(1024)S(1)} %convert_reduce_fusion) | copy-start | bytes 24580
  15.6 19.9 %collective-permute-start.6 = (bf16[256,3072]{1,0:T(8,128)(2,1)}, bf16[256,3072]{1,0:T(8,128)(2,1)S(1)}, u32[]{:S(2)}, u32[]{:S(2)}) collective-permute-start(bf16[256,3072]{1,0:T(8,128)(2,1)} %get-tuple-element.138), channel_id=1, source_target_pairs={{0,1},{1,0},{2,3},{3,2},{4,5},{5,4},{6,7},{7,6},{8,9},{9,8},{10,11... | collective-permute-start | bytes 4718600 | tf_op jit(solution)/shard_map/ppermute | solution.py:716
  21.5 10.8 %collective-permute-start.5 = (bf16[2,576]{1,0:T(2,128)(2,1)S(1)}, bf16[2,576]{1,0:T(2,128)(2,1)S(1)}, u32[]{:S(2)}, u32[]{:S(2)}) collective-permute-start(bf16[2,576]{1,0:T(2,128)(2,1)S(1)} %broadcast_select_fusion.3), channel_id=1, source_target_pairs={{0,2},{2,0},{1,3},{3,1},{4,6},{6,4},{5,7},{7,5},{8,10},{10,8},{9,1... | collective-permute-start | bytes 6920 | tf_op jit(solution)/shard_map/ppermute | solution.py:895
  22.0 13.5 %copy-start = (bf16[256,3072]{1,0:T(8,128)(2,1)S(1)}, bf16[256,3072]{1,0:T(8,128)(2,1)}, u32[]{:S(2)}) copy-start(bf16[256,3072]{1,0:T(8,128)(2,1)} %get-tuple-element.137.refs_4_.refs_1_.refs_5_) | copy-start | bytes 4718596
  32.6 25.2 %collective-permute-start.3 = (bf16[256,2048]{1,0:T(8,128)(2,1)}, bf16[256,2048]{1,0:T(8,128)(2,1)S(1)}, u32[]{:S(2)}, u32[]{:S(2)}) collective-permute-start(bf16[256,2048]{1,0:T(8,128)(2,1)} %collective-permute-done.2.refs_7_.refs_3_), channel_id=1, source_target_pairs={{0,2},{2,0},{1,3},{3,1},{4,6},{6,4},{5,7},{7,5},{8,10},{10,8},{9,1... | collective-permute-start | bytes 3145736 | tf_op jit(solution)/shard_map/ppermute | solution.py:716
  58.8 37.5 %collective-permute-start.7 = (bf16[256,3072]{1,0:T(8,128)(2,1)}, bf16[256,3072]{1,0:T(8,128)(2,1)S(1)}, u32[]{:S(2)}, u32[]{:S(2)}) collective-permute-start(bf16[256,3072]{1,0:T(8,128)(2,1)} %broadcast_select_fusion), channel_id=1, source_target_pairs={{0,2},{2,0},{1,3},{3,1},{4,6},{6,4},{5,7},{7,5},{8,10},{10,8},{9,1... | collective-permute-start | bytes 4718600 | tf_op jit(solution)/shard_map/ppermute | solution.py:716
  60.3 60.9 %collective-permute-start.8 = (bf16[512,1024]{1,0:T(8,128)(2,1)}, bf16[512,1024]{1,0:T(8,128)(2,1)S(1)}, u32[]{:S(2)}, u32[]{:S(2)}) collective-permute-start(bf16[512,1024]{1,0:T(8,128)(2,1)} %refs_2_.4), channel_id=1, source_target_pairs={{0,2},{2,0},{1,3},{3,1},{4,6},{6,4},{5,7},{7,5},{8,10},{10,8},{9,1... | collective-permute-start | bytes 3145736 | tf_op jit(solution)/shard_map/ppermute | solution.py:716
  96.3 27.3 %copy-start.4 = (bf16[256,3072]{1,0:T(8,128)(2,1)}, bf16[256,3072]{1,0:T(8,128)(2,1)S(1)}, u32[]{:S(2)}) copy-start(bf16[256,3072]{1,0:T(8,128)(2,1)S(1)} %collective-permute-done.7.refs_6_.refs_3_.refs_7_) | copy-start | bytes 4718596
  122.1 35.1 %collective-permute-start.10 = (bf16[768,1024]{1,0:T(8,128)(2,1)}, bf16[768,1024]{1,0:T(8,128)(2,1)}, u32[]{:S(2)}, u32[]{:S(2)}) collective-permute-start(bf16[768,1024]{1,0:T(8,128)(2,1)} %refs_3_.4), channel_id=1, source_target_pairs={{0,2},{2,0},{1,3},{3,1},{4,6},{6,4},{5,7},{7,5},{8,10},{10,8},{9,1... | collective-permute-start | bytes 4718600 | tf_op jit(solution)/shard_map/ppermute | solution.py:716
  123.6 34.2 %collective-permute-start.9 = (bf16[256,3072]{1,0:T(8,128)(2,1)S(1)}, bf16[256,3072]{1,0:T(8,128)(2,1)S(1)}, u32[]{:S(2)}, u32[]{:S(2)}) collective-permute-start(bf16[256,3072]{1,0:T(8,128)(2,1)S(1)} %collective-permute-done.7.refs_6_.refs_3_.refs_7_), channel_id=1, source_target_pairs={{0,4},{4,0},{8,12},{12,8},{16,20},{20,16},{24,28},{28,24},{1,5},{5... | collective-permute-start | bytes 4718600 | tf_op jit(solution)/shard_map/ppermute | solution.py:716
  157.8 14.0 %copy-start.5 = (bf16[256,3072]{1,0:T(8,128)(2,1)}, bf16[256,3072]{1,0:T(8,128)(2,1)S(1)}, u32[]{:S(2)}) copy-start(bf16[256,3072]{1,0:T(8,128)(2,1)S(1)} %collective-permute-done.9.refs_7_.refs_4_.refs_8_) | copy-start | bytes 4718596
  157.8 4.5 collective-permute-start.11
  157.8 14.2 %collective-permute-start.13 = (bf16[1024,1024]{1,0:T(8,128)(2,1)}, bf16[1024,1024]{1,0:T(8,128)(2,1)}, u32[]{:S(2)}, u32[]{:S(2)}) collective-permute-start(bf16[1024,1024]{1,0:T(8,128)(2,1)} %refs_3_.2), channel_id=1, source_target_pairs={{0,1},{1,0},{2,3},{3,2},{4,5},{5,4},{6,7},{7,6},{8,9},{9,8},{10,11... | collective-permute-start | bytes 6291464 | tf_op jit(solution)/shard_map/ppermute | solution.py:716
  171.9 4.4 collective-permute-start.12
  219.9 49.5 %copy-start.18 = (bf16[1536,1024]{1,0:T(8,128)(2,1)}, bf16[1536,1024]{1,0:T(8,128)(2,1)S(1)}, u32[]{:S(2)}) copy-start(bf16[1536,1024]{1,0:T(8,128)(2,1)S(1)} %convolution_convert_fusion.2) | copy-start | bytes 9437188
  233.6 18.9 %collective-permute-start.14 = (bf16[1024,1024]{1,0:T(8,128)(2,1)}, bf16[1024,1024]{1,0:T(8,128)(2,1)}, u32[]{:S(2)}, u32[]{:S(2)}) collective-permute-start(bf16[1024,1024]{1,0:T(8,128)(2,1)} %branch_other.1), channel_id=1, source_target_pairs={{0,1},{1,0},{2,3},{3,2},{4,5},{5,4},{6,7},{7,6},{8,9},{9,8},{10,11... | collective-permute-start | bytes 6291464 | tf_op jit(solution)/shard_map/ppermute | solution.py:716
  269.1 10.7 %collective-permute-start.17 = (bf16[1024,1024]{1,0:T(8,128)(2,1)}, bf16[1024,1024]{1,0:T(8,128)(2,1)}, u32[]{:S(2)}, u32[]{:S(2)}) collective-permute-start(bf16[1024,1024]{1,0:T(8,128)(2,1)} %get-tuple-element.177.refs_0_), channel_id=1, source_target_pairs={{0,1},{1,0},{2,3},{3,2},{4,5},{5,4},{6,7},{7,6},{8,9},{9,8},{10,11... | collective-permute-start | bytes 6291464 | tf_op jit(solution)/shard_map/ppermute | solution.py:716
  270.7 54.2 %collective-permute-start.15 = (bf16[2,1,384,1024]{3,2,1,0:T(8,128)(2,1)}, bf16[2,1,384,1024]{3,2,1,0:T(8,128)(2,1)}, u32[]{:S(2)}, u32[]{:S(2)}) collective-permute-start(bf16[2,1,384,1024]{3,2,1,0:T(8,128)(2,1)} %constant_dynamic-slice_fusion.16), channel_id=1, source_target_pairs={{0,4},{4,0},{8,12},{12,8},{16,20},{20,16},{24,28},{28,24},{1,5},{5... | collective-permute-start | bytes 4718600 | tf_op jit(solution)/shard_map/ppermute | solution.py:716
  276.5 48.4 %collective-permute-start.16 = (bf16[1,2,256,1536]{3,2,1,0:T(8,128)(2,1)}, bf16[1,2,256,1536]{3,2,1,0:T(8,128)(2,1)}, u32[]{:S(2)}, u32[]{:S(2)}) collective-permute-start(bf16[1,2,256,1536]{3,2,1,0:T(8,128)(2,1)} %constant_dynamic-slice_fusion.15), channel_id=1, source_target_pairs={{0,2},{2,0},{1,3},{3,1},{4,6},{6,4},{5,7},{7,5},{8,10},{10,8},{9,1... | collective-permute-start | bytes 4718600 | tf_op jit(solution)/shard_map/ppermute | solution.py:716
  278.6 80.8 %collective-permute-start.20 = (bf16[1,2,256,1536]{3,2,1,0:T(8,128)(2,1)}, bf16[1,2,256,1536]{3,2,1,0:T(8,128)(2,1)}, u32[]{:S(2)}, u32[]{:S(2)}) collective-permute-start(bf16[1,2,256,1536]{3,2,1,0:T(8,128)(2,1)} %constant_dynamic-slice_fusion.12), channel_id=1, source_target_pairs={{0,2},{2,0},{1,3},{3,1},{4,6},{6,4},{5,7},{7,5},{8,10},{10,8},{9,1... | collective-permute-start | bytes 4718600 | tf_op jit(solution)/shard_map/ppermute | solution.py:716
  328.2 31.2 %collective-permute-start.19 = (bf16[1,1,256,1536]{3,2,1,0:T(8,128)(2,1)}, bf16[1,1,256,1536]{3,2,1,0:T(8,128)(2,1)}, u32[]{:S(2)}, u32[]{:S(2)}) collective-permute-start(bf16[1,1,256,1536]{3,2,1,0:T(8,128)(2,1)} %constant_dynamic-slice_fusion.13), channel_id=1, source_target_pairs={{0,4},{4,0},{8,12},{12,8},{16,20},{20,16},{24,28},{28,24},{1,5},{5... | collective-permute-start | bytes 2359304 | tf_op jit(solution)/shard_map/ppermute | solution.py:716
  331.2 33.4 %collective-permute-start.18 = (bf16[1,1,384,1024]{3,2,1,0:T(8,128)(2,1)}, bf16[1,1,384,1024]{3,2,1,0:T(8,128)(2,1)}, u32[]{:S(2)}, u32[]{:S(2)}) collective-permute-start(bf16[1,1,384,1024]{3,2,1,0:T(8,128)(2,1)} %constant_dynamic-slice_fusion.14), channel_id=1, source_target_pairs={{0,2},{2,0},{1,3},{3,1},{4,6},{6,4},{5,7},{7,5},{8,10},{10,8},{9,1... | collective-permute-start | bytes 2359304 | tf_op jit(solution)/shard_map/ppermute | solution.py:716
  334.3 64.3 %collective-permute-start.23 = (bf16[1,2,256,1024]{3,2,1,0:T(8,128)(2,1)}, bf16[1,2,256,1024]{3,2,1,0:T(8,128)(2,1)}, u32[]{:S(2)}, u32[]{:S(2)}) collective-permute-start(bf16[1,2,256,1024]{3,2,1,0:T(8,128)(2,1)} %constant_dynamic-slice_fusion.9), channel_id=1, source_target_pairs={{0,2},{2,0},{1,3},{3,1},{4,6},{6,4},{5,7},{7,5},{8,10},{10,8},{9,1... | collective-permute-start | bytes 3145736 | tf_op jit(solution)/shard_map/ppermute | solution.py:716
  367.2 31.5 %collective-permute-start.22 = (bf16[1,1,256,1536]{3,2,1,0:T(8,128)(2,1)}, bf16[1,1,256,1536]{3,2,1,0:T(8,128)(2,1)S(1)}, u32[]{:S(2)}, u32[]{:S(2)}) collective-permute-start(bf16[1,1,256,1536]{3,2,1,0:T(8,128)(2,1)} %constant_dynamic-slice_fusion.10), channel_id=1, source_target_pairs={{0,4},{4,0},{8,12},{12,8},{16,20},{20,16},{24,28},{28,24},{1,5},{5... | collective-permute-start | bytes 2359304 | tf_op jit(solution)/shard_map/ppermute | solution.py:716
  372.4 26.2 %collective-permute-start.21 = (bf16[768,512]{1,0:T(8,128)(2,1)}, bf16[768,512]{1,0:T(8,128)(2,1)S(1)}, u32[]{:S(2)}, u32[]{:S(2)}) collective-permute-start(bf16[768,512]{1,0:T(8,128)(2,1)} %constant_dynamic-slice_fusion.11), channel_id=1, source_target_pairs={{0,8},{4,12},{8,0},{12,4},{16,24},{20,28},{24,16},{28,20},{1,9},{5... | collective-permute-start | bytes 2359304 | tf_op jit(solution)/shard_map/ppermute | solution.py:716
  398.6 10.8 %copy-start.35 = (bf16[1,1,256,1536]{3,2,1,0:T(8,128)(2,1)}, bf16[1,1,256,1536]{3,2,1,0:T(8,128)(2,1)S(1)}, u32[]{:S(2)}) copy-start(bf16[1,1,256,1536]{3,2,1,0:T(8,128)(2,1)S(1)} %collective-permute-done.22) | copy-start | bytes 2359300
  398.7 10.8 %copy-start.37 = (bf16[768,512]{1,0:T(8,128)(2,1)}, bf16[768,512]{1,0:T(8,128)(2,1)S(1)}, u32[]{:S(2)}) copy-start(bf16[768,512]{1,0:T(8,128)(2,1)S(1)} %collective-permute-done.21) | copy-start | bytes 2359300
  411.8 34.2 %collective-permute-start.26 = (bf16[1,2,256,1536]{3,2,1,0:T(8,128)(2,1)}, bf16[1,2,256,1536]{3,2,1,0:T(8,128)(2,1)}, u32[]{:S(2)}, u32[]{:S(2)}) collective-permute-start(bf16[1,2,256,1536]{3,2,1,0:T(8,128)(2,1)} %constant_dynamic-slice_fusion.6), channel_id=1, source_target_pairs={{0,2},{2,0},{1,3},{3,1},{4,6},{6,4},{5,7},{7,5},{8,10},{10,8},{9,1... | collective-permute-start | bytes 4718600 | tf_op jit(solution)/shard_map/ppermute | solution.py:716
  414.8 29.3 %collective-permute-start.25 = (bf16[1,1,256,1024]{3,2,1,0:T(8,128)(2,1)}, bf16[1,1,256,1024]{3,2,1,0:T(8,128)(2,1)}, u32[]{:S(2)}, u32[]{:S(2)}) collective-permute-start(bf16[1,1,256,1024]{3,2,1,0:T(8,128)(2,1)} %constant_dynamic-slice_fusion.7), channel_id=1, source_target_pairs={{0,4},{4,0},{8,12},{12,8},{16,20},{20,16},{24,28},{28,24},{1,5},{5... | collective-permute-start | bytes 1572872 | tf_op jit(solution)/shard_map/ppermute | solution.py:716
  415.1 29.0 %collective-permute-start.24 = (bf16[384,512]{1,0:T(8,128)(2,1)S(1)}, bf16[384,512]{1,0:T(8,128)(2,1)S(1)}, u32[]{:S(2)}, u32[]{:S(2)}) collective-permute-start(bf16[384,512]{1,0:T(8,128)(2,1)S(1)} %constant_dynamic-slice_fusion.8), channel_id=1, source_target_pairs={{0,16},{4,20},{8,24},{12,28},{16,0},{20,4},{24,8},{28,12},{1,17},{... | collective-permute-start | bytes 1179656 | tf_op jit(solution)/shard_map/ppermute | solution.py:716
  454.3 25.0 %collective-permute-start.29 = (bf16[1,1,256,1536]{3,2,1,0:T(8,128)(2,1)}, bf16[1,1,256,1536]{3,2,1,0:T(8,128)(2,1)}, u32[]{:S(2)}, u32[]{:S(2)}) collective-permute-start(bf16[1,1,256,1536]{3,2,1,0:T(8,128)(2,1)} %constant_dynamic-slice_fusion.4), channel_id=1, source_target_pairs={{0,4},{4,0},{8,12},{12,8},{16,20},{20,16},{24,28},{28,24},{1,5},{5... | collective-permute-start | bytes 2359304 | tf_op jit(solution)/shard_map/ppermute | solution.py:716
  456.4 22.0 %collective-permute-start.28 = (bf16[640,512]{1,0:T(8,128)(2,1)}, bf16[640,512]{1,0:T(8,128)(2,1)S(1)}, u32[]{:S(2)}, u32[]{:S(2)}) collective-permute-start(bf16[640,512]{1,0:T(8,128)(2,1)} %constant_dynamic-slice_fusion.5), channel_id=1, source_target_pairs={{0,8},{4,12},{8,0},{12,4},{16,24},{20,28},{24,16},{28,20},{1,9},{5... | collective-permute-start | bytes 1966088 | tf_op jit(solution)/shard_map/ppermute | solution.py:716
  458.6 18.4 %collective-permute-start.30 = (bf16[1,2,256,512]{3,2,1,0:T(8,128)(2,1)}, bf16[1,2,256,512]{3,2,1,0:T(8,128)(2,1)}, u32[]{:S(2)}, u32[]{:S(2)}) collective-permute-start(bf16[1,2,256,512]{3,2,1,0:T(8,128)(2,1)} %constant_dynamic-slice_fusion.3), channel_id=1, source_target_pairs={{0,2},{2,0},{1,3},{3,1},{4,6},{6,4},{5,7},{7,5},{8,10},{10,8},{9,1... | collective-permute-start | bytes 1572872 | tf_op jit(solution)/shard_map/ppermute | solution.py:716
  460.0 12.8 %copy-start.31 = (bf16[384,512]{1,0:T(8,128)(2,1)}, bf16[384,512]{1,0:T(8,128)(2,1)S(1)}, u32[]{:S(2)}) copy-start(bf16[384,512]{1,0:T(8,128)(2,1)S(1)} %dynamic-slice_add_fusion.8) | copy-start | bytes 1179652
  460.0 17.1 %collective-permute-start.27 = (bf16[384,512]{1,0:T(8,128)(2,1)S(1)}, bf16[384,512]{1,0:T(8,128)(2,1)S(1)}, u32[]{:S(2)}, u32[]{:S(2)}) collective-permute-start(bf16[384,512]{1,0:T(8,128)(2,1)S(1)} %dynamic-slice_add_fusion.8), channel_id=1, source_target_pairs={{0,16},{4,20},{8,24},{12,28},{16,0},{20,4},{24,8},{28,12},{1,17},{... | collective-permute-start | bytes 1179656 | tf_op jit(solution)/shard_map/ppermute | solution.py:716
  472.8 10.7 %copy-start.30 = (bf16[1280,512]{1,0:T(8,128)(2,1)S(1)}, bf16[1280,512]{1,0:T(8,128)(2,1)}, u32[]{:S(2)}) copy-start(bf16[1280,512]{1,0:T(8,128)(2,1)} %copy-done.29) | copy-start | bytes 3932164
  480.7 23.2 %collective-permute-start.31 = (bf16[768,512]{1,0:T(8,128)(2,1)S(1)}, bf16[768,512]{1,0:T(8,128)(2,1)}, u32[]{:S(2)}, u32[]{:S(2)}) collective-permute-start(bf16[768,512]{1,0:T(8,128)(2,1)S(1)} %maximum_select_fusion.3), channel_id=1, source_target_pairs={{0,8},{4,12},{8,0},{12,4},{16,24},{20,28},{24,16},{28,20},{1,9},{5... | collective-permute-start | bytes 2359304 | tf_op jit(solution)/shard_map/ppermute | solution.py:716
  485.6 17.4 %collective-permute-start.32 = (bf16[320,512]{1,0:T(8,128)(2,1)S(1)}, bf16[320,512]{1,0:T(8,128)(2,1)S(1)}, u32[]{:S(2)}, u32[]{:S(2)}) collective-permute-start(bf16[320,512]{1,0:T(8,128)(2,1)S(1)} %constant_dynamic-slice_fusion.2), channel_id=1, source_target_pairs={{0,16},{4,20},{8,24},{12,28},{16,0},{20,4},{24,8},{28,12},{1,17},{... | collective-permute-start | bytes 983048 | tf_op jit(solution)/shard_map/ppermute | solution.py:716
  489.2 9.4 %collective-permute-start.33 = (bf16[1,1,256,512]{3,2,1,0:T(8,128)(2,1)}, bf16[1,1,256,512]{3,2,1,0:T(8,128)(2,1)}, u32[]{:S(2)}, u32[]{:S(2)}) collective-permute-start(bf16[1,1,256,512]{3,2,1,0:T(8,128)(2,1)} %constant_dynamic-slice_fusion.1), channel_id=1, source_target_pairs={{0,4},{4,0},{8,12},{12,8},{16,20},{20,16},{24,28},{28,24},{1,5},{5... | collective-permute-start | bytes 786440 | tf_op jit(solution)/shard_map/ppermute | solution.py:716
  503.9 12.3 %collective-permute-start.36 = (bf16[1024,1024]{1,0:T(8,128)(2,1)}, bf16[1024,1024]{1,0:T(8,128)(2,1)}, u32[]{:S(2)}, u32[]{:S(2)}) collective-permute-start(bf16[1024,1024]{1,0:T(8,128)(2,1)} %tokens_other.1), channel_id=1, source_target_pairs={{0,1},{1,0},{2,3},{3,2},{4,5},{5,4},{6,7},{7,6},{8,9},{9,8},{10,11... | collective-permute-start | bytes 6291464 | tf_op jit(solution)/shard_map/ppermute | solution.py:716
  505.1 33.9 %collective-permute-start.41 = (bf16[1024,1024]{1,0:T(8,128)(2,1)}, bf16[1024,1024]{1,0:T(8,128)(2,1)}, u32[]{:S(2)}, u32[]{:S(2)}) collective-permute-start(bf16[1024,1024]{1,0:T(8,128)(2,1)} %output_other.1), channel_id=1, source_target_pairs={{0,1},{1,0},{2,3},{3,2},{4,5},{5,4},{6,7},{7,6},{8,9},{9,8},{10,11... | collective-permute-start | bytes 6291464 | tf_op jit(solution)/shard_map/ppermute | solution.py:716
  507.6 23.3 %collective-permute-start.35 = (bf16[128,2048]{1,0:T(8,128)(2,1)}, bf16[128,2048]{1,0:T(8,128)(2,1)}, u32[]{:S(2)}, u32[]{:S(2)}) collective-permute-start(bf16[128,2048]{1,0:T(8,128)(2,1)} %fusion.2), channel_id=1, source_target_pairs={{0,8},{4,12},{8,0},{12,4},{16,24},{20,28},{24,16},{28,20},{1,9},{5... | collective-permute-start | bytes 1572872 | tf_op jit(solution)/shard_map/ppermute | solution.py:716
  513.1 42.4 %copy-start.2 = (bf16[1536,512]{1,0:T(8,128)(2,1)}, bf16[1536,512]{1,0:T(8,128)(2,1)S(1)}, u32[]{:S(2)}) copy-start(bf16[1536,512]{1,0:T(8,128)(2,1)S(1)} %maximum_select_fusion.refs_0_) | copy-start | bytes 4718596
  513.1 41.6 %collective-permute-start.38 = (bf16[1536,512]{1,0:T(8,128)(2,1)S(1)}, bf16[1536,512]{1,0:T(8,128)(2,1)S(1)}, u32[]{:S(2)}, u32[]{:S(2)}) collective-permute-start(bf16[1536,512]{1,0:T(8,128)(2,1)S(1)} %maximum_select_fusion.refs_0_), channel_id=1, source_target_pairs={{0,4},{4,0},{8,12},{12,8},{16,20},{20,16},{24,28},{28,24},{1,5},{5... | collective-permute-start | bytes 4718600 | tf_op jit(solution)/shard_map/ppermute | solution.py:716
  514.3 15.9 %collective-permute-start.34 = (bf16[320,512]{1,0:T(8,128)(2,1)}, bf16[320,512]{1,0:T(8,128)(2,1)}, u32[]{:S(2)}, u32[]{:S(2)}) collective-permute-start(bf16[320,512]{1,0:T(8,128)(2,1)} %dynamic-slice_add_fusion.9), channel_id=1, source_target_pairs={{0,16},{4,20},{8,24},{12,28},{16,0},{20,4},{24,8},{28,12},{1,17},{... | collective-permute-start | bytes 983048 | tf_op jit(solution)/shard_map/ppermute | solution.py:716
  533.2 22.3 %collective-permute-start.37 = (bf16[640,512]{1,0:T(8,128)(2,1)}, bf16[640,512]{1,0:T(8,128)(2,1)}, u32[]{:S(2)}, u32[]{:S(2)}) collective-permute-start(bf16[640,512]{1,0:T(8,128)(2,1)} %maximum_select_fusion.4), channel_id=1, source_target_pairs={{0,8},{4,12},{8,0},{12,4},{16,24},{20,28},{24,16},{28,20},{1,9},{5... | collective-permute-start | bytes 1966088 | tf_op jit(solution)/shard_map/ppermute | solution.py:716
  537.1 17.6 %collective-permute-start.39 = (bf16[64,2048]{1,0:T(8,128)(2,1)S(1)}, bf16[64,2048]{1,0:T(8,128)(2,1)}, u32[]{:S(2)}, u32[]{:S(2)}) collective-permute-start(bf16[64,2048]{1,0:T(8,128)(2,1)S(1)} %constant_dynamic-slice_fusion), channel_id=1, source_target_pairs={{0,16},{4,20},{8,24},{12,28},{16,0},{20,4},{24,8},{28,12},{1,17},{... | collective-permute-start | bytes 786440 | tf_op jit(solution)/shard_map/ppermute | solution.py:716
  538.9 10.2 %collective-permute-start.40 = (f32[2304]{0:T(1024)S(1)}, f32[2304]{0:T(1024)S(1)}, u32[]{:S(2)}, u32[]{:S(2)}) collective-permute-start(f32[2304]{0:T(1024)S(1)} %pad_maximum_fusion.2), channel_id=1, source_target_pairs={{0,1},{1,0},{2,3},{3,2},{4,5},{5,4},{6,7},{7,6},{8,9},{9,8},{10,11... | collective-permute-start | bytes 27656 | tf_op jit(solution)/shard_map/ppermute | solution.py:716
  556.5 11.6 %collective-permute-start.44 = (bf16[768,512]{1,0:T(8,128)(2,1)}, bf16[768,512]{1,0:T(8,128)(2,1)}, u32[]{:S(2)}, u32[]{:S(2)}) collective-permute-start(bf16[768,512]{1,0:T(8,128)(2,1)} %slice_select_fusion.1), channel_id=1, source_target_pairs={{0,1},{1,0},{2,3},{3,2},{4,5},{5,4},{6,7},{7,6},{8,9},{9,8},{10,11... | collective-permute-start | bytes 2359304 | tf_op jit(solution)/shard_map/ppermute | solution.py:716
  558.6 36.3 %copy-start.3 = (bf16[1280,512]{1,0:T(8,128)(2,1)}, bf16[1280,512]{1,0:T(8,128)(2,1)S(1)}, u32[]{:S(2)}) copy-start(bf16[1280,512]{1,0:T(8,128)(2,1)S(1)} %maximum_select_fusion.1.refs_0_) | copy-start | bytes 3932164
  558.6 33.5 %collective-permute-start.47 = (bf16[1280,512]{1,0:T(8,128)(2,1)S(1)}, bf16[1280,512]{1,0:T(8,128)(2,1)}, u32[]{:S(2)}, u32[]{:S(2)}) collective-permute-start(bf16[1280,512]{1,0:T(8,128)(2,1)S(1)} %maximum_select_fusion.1.refs_0_), channel_id=1, source_target_pairs={{0,4},{4,0},{8,12},{12,8},{16,20},{20,16},{24,28},{28,24},{1,5},{5... | collective-permute-start | bytes 3932168 | tf_op jit(solution)/shard_map/ppermute | solution.py:716
  561.5 15.0 %collective-permute-start.42 = (bf16[64,2048]{1,0:T(8,128)(2,1)S(1)}, bf16[64,2048]{1,0:T(8,128)(2,1)S(1)}, u32[]{:S(2)}, u32[]{:S(2)}) collective-permute-start(bf16[64,2048]{1,0:T(8,128)(2,1)S(1)} %dynamic-slice_add_fusion.10), channel_id=1, source_target_pairs={{0,16},{4,20},{8,24},{12,28},{16,0},{20,4},{24,8},{28,12},{1,17},{... | collective-permute-start | bytes 786440 | tf_op jit(solution)/shard_map/ppermute | solution.py:716
  562.9 9.8 %collective-permute-start.43 = (f32[2304]{0:T(1024)S(1)}, f32[2304]{0:T(1024)S(1)}, u32[]{:S(2)}, u32[]{:S(2)}) collective-permute-start(f32[2304]{0:T(1024)S(1)} %fusion.5), channel_id=1, source_target_pairs={{0,2},{2,0},{1,3},{3,1},{4,6},{6,4},{5,7},{7,5},{8,10},{10,8},{9,1... | collective-permute-start | bytes 27656 | tf_op jit(solution)/shard_map/ppermute | solution.py:716
  576.7 13.7 %collective-permute-start.45 = (bf16[128,2048]{1,0:T(8,128)(2,1)S(1)}, bf16[128,2048]{1,0:T(8,128)(2,1)S(1)}, u32[]{:S(2)}, u32[]{:S(2)}) collective-permute-start(bf16[128,2048]{1,0:T(8,128)(2,1)S(1)} %maximum_select_fusion.5), channel_id=1, source_target_pairs={{0,8},{4,12},{8,0},{12,4},{16,24},{20,28},{24,16},{28,20},{1,9},{5... | collective-permute-start | bytes 1572872 | tf_op jit(solution)/shard_map/ppermute | solution.py:716
  576.7 13.6 %collective-permute-start.46 = (f32[2304]{0:T(1024)S(1)}, f32[2304]{0:T(1024)S(1)}, u32[]{:S(2)}, u32[]{:S(2)}) collective-permute-start(f32[2304]{0:T(1024)S(1)} %add.233), channel_id=1, source_target_pairs={{0,8},{4,12},{8,0},{12,4},{16,24},{20,28},{24,16},{28,20},{1,9},{5... | collective-permute-start | bytes 27656 | tf_op jit(solution)/shard_map/ppermute | solution.py:716
  590.3 4.6 collective-permute-start.48
  591.4 24.2 %collective-permute-start.49 = (bf16[256,2048]{1,0:T(8,128)(2,1)S(1)}, bf16[256,2048]{1,0:T(8,128)(2,1)S(1)}, u32[]{:S(2)}, u32[]{:S(2)}) collective-permute-start(bf16[256,2048]{1,0:T(8,128)(2,1)S(1)} %maximum_select_fusion.2), channel_id=1, source_target_pairs={{0,4},{4,0},{8,12},{12,8},{16,20},{20,16},{24,28},{28,24},{1,5},{5... | collective-permute-start | bytes 3145736 | tf_op jit(solution)/shard_map/ppermute | solution.py:716
  597.0 4.3 collective-permute-start.50
  597.0 18.6 %collective-permute-start.51 = (f32[2304]{0:T(1024)S(1)}, f32[2304]{0:T(1024)S(1)}, u32[]{:S(2)}, u32[]{:S(2)}) collective-permute-start(f32[2304]{0:T(1024)S(1)} %add.235), channel_id=1, source_target_pairs={{0,4},{4,0},{8,12},{12,8},{16,20},{20,16},{24,28},{28,24},{1,5},{5... | collective-permute-start | bytes 27656 | tf_op jit(solution)/shard_map/ppermute | solution.py:716
  616.8 2.7 collective-permute-start.52
  (46 other events, 188.2 us)

commit v4 on v3

--- a/solution.py
+++ b/solution.py
@@ -945,7 +945,7 @@
         gu_far = [jnp.where(side == 0, near, far), jnp.where(side == 0, far, near)]
         o_rows, d_rows = w_o.shape[0], w_down.shape[0]
         layout = (
-            starts(w_q.shape[0], quad)
+            starts(w_q.shape[0], quad[:2] + gu_far)
             + [o_rows * row, o_rows * (1 - row)]
             + starts(w_gate.shape[0], quad[:2] + gu_far)
             + [d_rows * row, d_rows * (1 - row)]
@@ -964,6 +964,31 @@
     )
     head_gains = jnp.concatenate([q_gain, k_gain], axis=0)
 
+    mine, send = pack("pack_qkv", info, [w_q, w_k, w_v], qkv_columns)
+    got = swap(send, "seq")
+    tokens_other = swap(tokens, "seq")
+    if pairs:
+        here = swap(jnp.where(side == 0, mine, got), "fsdp")
+        wqkv_near = [mine, got]
+        got, w_gate, w_up = fence(got, w_gate, w_up)
+        gu_mine, send = pack("pack_gu", info, [w_gate, w_up], gu_layout)
+        gu_got = swap(send, "seq")
+        gu_here = jnp.where(side == 0, gu_mine, gu_got)
+        here, attn_gain, head_gains, gu_here, w_o, segments = fence(
+            here, attn_gain, head_gains, gu_here, w_o, segments
+        )
+        there = swap(here, "rep")
+        gu_here, o_there = swap(gu_here, "fsdp"), swap(w_o, "fsdp")
+        wqkv = Weight(list(zip([*wqkv_near, here, there], layout[:4])), bases[0])
+    else:
+        wqkv = Weight([(whole_cols(core, mine, send), 0)], bases[0])
+        wo = Weight([(take_rows(gather_any(w_o), core), 0)], bases[1])
+        mine, send = pack("pack_gu", info, [w_gate, w_up], gu_layout)
+        wgu = Weight([(whole_cols(core, mine, send), 0)], bases[2])
+        wd = Weight([(take_rows(gather_any(w_down), core), 0)], bases[3])
+
+    cot_other = swap(cotangent, "seq")
+
     seg = segments[0]
     start = jnp.sum((seg[None, :] < seg[:, None]).astype(jnp.int32), axis=1)
     position = (jnp.arange(length, dtype=jnp.int32) - start).astype(F32)
@@ -972,30 +997,6 @@
     cos_half, sin_half = jnp.cos(angles), jnp.sin(angles)
     cosine = jnp.concatenate([cos_half, cos_half], axis=1)
     sine = jnp.concatenate([-sin_half, sin_half], axis=1)
-
-    mine, send = pack("pack_qkv", info, [w_q, w_k, w_v], qkv_columns)
-    got = swap(send, "seq")
-    tokens_other = swap(tokens, "seq")
-    if pairs:
-        mine_far, got_far = swap(mine, "fsdp"), swap(got, "fsdp")
-        got, w_gate, w_up = fence(got, w_gate, w_up)
-        gu_mine, send = pack("pack_gu", info, [w_gate, w_up], gu_layout)
-        gu_got = swap(send, "seq")
-        gu_here = jnp.where(side == 0, gu_mine, gu_got)
-        mine_far, got_far, attn_gain, head_gains, cosine, sine, gu_here, w_o, w_down = fence(
-            mine_far, got_far, attn_gain, head_gains, cosine, sine, gu_here, w_o, w_down
-        )
-        wqkv = Weight(list(zip([mine, got, mine_far, got_far], layout[:4])), bases[0])
-        gu_here, o_there = swap(gu_here, "fsdp"), swap(w_o, "fsdp")
-    else:
-        wqkv = Weight([(whole_cols(core, mine, send), 0)], bases[0])
-        wo = Weight([(take_rows(gather_any(w_o), core), 0)], bases[1])
-        mine, send = pack("pack_gu", info, [w_gate, w_up], gu_layout)
-        wgu = Weight([(whole_cols(core, mine, send), 0)], bases[2])
-        wd = Weight([(take_rows(gather_any(w_down), core), 0)], bases[3])
-
-    cot_other = swap(cotangent, "seq")
-
     low = start[::BLK] // BLK
 
     normed, qkv, raw = project(
@@ -1003,13 +1004,11 @@
     )
     done = attend(low, qkv, start, 0, 1)
     if pairs:
-        *done, gu_here = fence(*done, gu_here)
+        *done, gu_here, o_there, w_down = fence(*done, gu_here, o_there, w_down)
+        wo = Weight(list(zip([w_o, o_there], layout[4:6])), bases[1])
         gu_there = swap(gu_here, "rep")
+        d_there = swap(w_down, "fsdp")
     done = attend(low, qkv, start, 1, 2, done)
-    if pairs:
-        *done, o_there, w_down = fence(*done, o_there, w_down)
-        d_there = swap(w_down, "fsdp")
-        wo = Weight(list(zip([w_o, o_there], layout[4:6])), bases[1])
     attended, lse = attend(low, qkv, start, 3, 1, done)
 
     sent = times("mix_other", order, info, [attended], order.other, wo, False, 5)

time: 629 us -> 629 us (level)
  starting transfers between devices: 50.9 us -> 57.6 us
  transfers between devices with their start and end apart: 53 -> 53, of which waited for: 21 -> 22; matrix products, arithmetic and copies ran while one was open for 15% -> 15% of each run, Pallas kernels for 42% -> 41%
where the time goes in v4:
time: 629 us; the launch traced here: 621 us
  Pallas kernels  332 us (53%)
  waiting for transfers between devices  94.9 us (15%)
  starting transfers between devices  57.6 us (9%)
  matrix products  54.3 us (9%)
  other arithmetic  43.5 us (7%)
  local copies, waits for them, and re-layouts  36.6 us (6%)
    pallas_call x18, Pallas kernels, tiled(): pl.pallas_call(kernel, grid_spec=pltpu.PrefetchScalarGridSpec(num_scalar_...  184 us
    pallas_call x4, Pallas kernels, attend_back(): pl.pallas_call(body, grid_spec=pltpu.PrefetchScalarGridSpec(num_scalar_pr...  95 us
    ppermute x51, waiting for transfers between devices, swap(): return lax.ppermute(value, axis, [(i, i ^ 1 << bit) for i in range(size)])  90.7 us
    ppermute x51, starting transfers between devices, swap(): return lax.ppermute(value, axis, [(i, i ^ 1 << bit) for i in range(size)])  54.4 us
    dot_general x5, matrix products, tn(): lax.dot_general(a, b, (((0,), (0,)), ((), ())), preferred_element_type=F32)  54.3 us
    pallas_call x3, Pallas kernels, attend(): pl.pallas_call(body, grid_spec=pltpu.PrefetchScalarGridSpec(num_scalar_pr...  53 us
    dynamic_slice x17, local copies, waits for them, and re-layouts, part(): return lax.dynamic_slice_in_dim(value, index * size, size, axis)  15.6 us
    unnamed x125, local copies, waits for them, and re-layouts  12.9 us
  transfers between devices with their start and end apart: 53, of which 22 were waited for; matrix products, arithmetic and copies ran while one was open for 15% of the time, Pallas kernels for 41%

profile of v4, /device:TPU:0, one launch (start us, length us, event | category | flops | bytes accessed | tf_op | source)
XLA Modules:
  0.0 620.8 jit_solution(5388840853091652095)
XLA Ops:
  1.3 3.8 pack_qkv.1
  5.7 2.6 collective-permute-done.refs_7_.refs_3_
  8.3 4.4 pack_gu.1
  13.7 2.6 collective-permute-done.2
  16.4 3.0 collective-permute-start.3
  21.3 2.1 collective-permute-start.1
  26.2 19.6 %collective-permute-done.1.refs_8_.refs_4_ = bf16[256,2048]{1,0:T(8,128)(2,1)} collective-permute-done((bf16[256,2048]{1,0:T(8,128)(2,1)S(1)}, bf16[256,2048]{1,0:T(8,128)(2,1)}, u32[]{:S(2)}, u32[]{:S(2)}) %collective-permute-start.1) | collective-permute-done | bytes 1048608 | tf_op jit(solution)/shard_map/ppermute | solution.py:716
  45.8 3.1 collective-permute-start.6
  54.6 3.7 fusion.3
  58.4 1.9 pad_maximum_fusion
  60.3 10.3 %collective-permute-done.6.refs_9_.refs_5_ = bf16[256,2048]{1,0:T(8,128)(2,1)} collective-permute-done((bf16[256,2048]{1,0:T(8,128)(2,1)}, bf16[256,2048]{1,0:T(8,128)(2,1)}, u32[]{:S(2)}, u32[]{:S(2)}) %collective-permute-start.6) | collective-permute-done | bytes 1048608 | tf_op jit(solution)/shard_map/ppermute | solution.py:716
  70.6 19.4 %project.1 = (bf16[2048,1024]{1,0:T(8,128)(2,1)}, bf16[2048,2048]{1,0:T(8,128)(2,1)}, bf16[2048,1536]{1,0:T(8,128)(2,1)}) custom-call(s32[14]{0:T(128)} %stack.47.info_ref, bf16[1024,1024]{1,0:T(8,128)(2,1)} %refs_3_.3, bf16[1024,1024]{1,0:T(8,128)(2,1)} %collective-permute-done.5.refs_1_, f32[1,1024]{1,0:T(1,128)} %bitcast.72, ...), custom_call_target="tpu_custom_call" | custom-call | flops 170000000 | tf_op jit(solution)/shard_map/project/pallas_call | solution.py:83
  90.1 14.1 %attend.3 = (bf16[2048,1024]{1,0:T(8,128)(2,1)}, f32[4,2,2048]{2,1,0:T(2,128)}) custom-call(s32[8]{0:T(128)} %and_select_fusion.low_ref.refs_0_, bf16[2048,2048]{1,0:T(8,128)(2,1)} %get-tuple-element.137.qkv_ref.refs_1_, s32[2048,1]{1,0:T(8,128)} %copy.38.start_ref), custom_call_target="tpu_custom_call" | custom-call | flops 115000000 | tf_op jit(solution)/shard_map/attend/pallas_call | solution.py:467
  107.6 24.8 %attend.4 = (bf16[2048,1024]{1,0:T(8,128)(2,1)}, f32[4,2,2048]{2,1,0:T(2,128)}) custom-call(s32[8]{0:T(128)} %and_select_fusion.low_ref.refs_0_, bf16[2048,2048]{1,0:T(8,128)(2,1)} %get-tuple-element.137.qkv_ref.refs_1_, s32[2048,1]{1,0:T(8,128)} %copy.38.start_ref, ...), custom_call_target="tpu_custom_call", output_to_operand_aliasing={{0}: (3, {}), {1}: (4, {})} | custom-call | flops 230000000 | tf_op jit(solution)/shard_map/attend/pallas_call | solution.py:467
  132.4 14.1 %attend.5 = (bf16[2048,1024]{1,0:T(8,128)(2,1)}, f32[4,2,2048]{2,1,0:T(2,128)}) custom-call(s32[8]{0:T(128)} %and_select_fusion.low_ref.refs_0_, bf16[2048,2048]{1,0:T(8,128)(2,1)} %get-tuple-element.137.qkv_ref.refs_1_, s32[2048,1]{1,0:T(8,128)} %copy.38.start_ref, ...), custom_call_target="tpu_custom_call", output_to_operand_aliasing={{0}: (3, {}), {1}: (4, {})} | custom-call | flops 115000000 | tf_op jit(solution)/shard_map/attend/pallas_call | solution.py:467
  146.5 7.5 %mix_other.1 = bf16[1024,1024]{1,0:T(8,128)(2,1)} custom-call(s32[14]{0:T(128)} %stack.47.info_ref, bf16[2048,1024]{1,0:T(8,128)(2,1)} %get-tuple-element.146.refs_0_.refs_3_, bf16[512,1024]{1,0:T(8,128)(2,1)} %refs_2_.4, bf16[512,1024]{1,0:T(8,128)(2,1)} %collective-permute-done.8.refs_2_.refs_5_.refs_3_), custom_call_target="tpu_custom_call" | custom-call | flops 50000000 | tf_op jit(solution)/shard_map/mix_other/pallas_call | solution.py:83
  155.3 3.4 collective-permute-done.11.refs_2_
  158.7 9.5 %mix_own.1 = (f32[1024,1024]{1,0:T(8,128)}, bf16[1024,1024]{1,0:T(8,128)(2,1)}) custom-call(s32[14]{0:T(128)} %stack.47.info_ref, bf16[2048,1024]{1,0:T(8,128)(2,1)} %get-tuple-element.146.refs_0_.refs_3_, bf16[1024,1024]{1,0:T(8,128)(2,1)} %refs_3_.3, bf16[1024,1024]{1,0:T(8,128)(2,1)} %collective-permute-done.11.refs_2_, f32[1,1024]{1,0:T(1,128)} %bitcast.74, ...), custom_call_target="tpu_custom_call" | custom-call | flops 60000000 | tf_op jit(solution)/shard_map/mix_own/pallas_call | solution.py:83
  168.4 4.2 collective-permute-done.12.refs_1_
  174.0 32.0 %mlp.1 = (bf16[2048,1536]{1,0:T(8,128)(2,1)}, bf16[2048,3072]{1,0:T(8,128)(2,1)}, bf16[2048,1024]{1,0:T(8,128)(2,1)}, bf16[2048,1024]{1,0:T(8,128)(2,1)}) custom-call(s32[14]{0:T(128)} %stack.47.info_ref, bf16[1024,1024]{1,0:T(8,128)(2,1)} %get-tuple-element.151.refs_0_, bf16[1024,1024]{1,0:T(8,128)(2,1)} %copy-done.24, bf16[1024,1024]{1,0:T(8,128)(2,1)} %refs_3_.2, ...), custom_call_target="tpu_custom_call" | custom-call | flops 300000000 | tf_op jit(solution)/shard_map/mlp/pallas_call | solution.py:83
  206.0 10.1 %convolution_convert_fusion.2 = bf16[1536,1024]{1,0:T(8,128)(2,1)S(1)} fusion(bf16[2048,1536]{1,0:T(8,128)(2,1)} %get-tuple-element.217.refs_0_, bf16[2048,1024]{1,0:T(8,128)(2,1)} %get-tuple-element.156), kind=kOutput, calls=%fused_computation.3 | convolution fusion | flops 6444023808 | bytes 13631488 | tf_op jit(solution)/shard_map/dot_general | solution.py:31
  216.1 13.6 %branch_other.1 = bf16[1024,1024]{1,0:T(8,128)(2,1)} custom-call(s32[14]{0:T(128)} %stack.47.info_ref, bf16[2048,3072]{1,0:T(8,128)(2,1)} %get-tuple-element.162.refs_0_, bf16[256,3072]{1,0:T(8,128)(2,1)} %get-tuple-element.131.refs_4_.refs_1_.refs_5_, bf16[256,3072]{1,0:T(8,128)(2,1)} %copy-done.1, bf16[256,3072]{1,0:T(8,128)(2,1)} %copy-done.5, ...), custom_call_target="tpu_custom_call" | custom-call | flops 90000000 | tf_op jit(solution)/shard_map/branch_other/pallas_call | solution.py:83
  230.0 18.7 %convolution_convert_fusion = bf16[1024,3072]{1,0:T(8,128)(2,1)} fusion(bf16[2048,1024]{1,0:T(8,128)(2,1)} %get-tuple-element.159, bf16[2048,3072]{1,0:T(8,128)(2,1)} %get-tuple-element.162.refs_0_), kind=kOutput, calls=%fused_computation.1 | convolution fusion | flops 12888047616 | bytes 23068672 | tf_op jit(solution)/shard_map/dot_general | solution.py:31
  248.7 16.5 %branch_own.1 = (f32[1024,1024]{1,0:T(8,128)}, bf16[1024,1024]{1,0:T(8,128)(2,1)}, f32[1,1024]{1,0:T(1,128)}) custom-call(s32[14]{0:T(128)} %stack.47.info_ref, bf16[2048,3072]{1,0:T(8,128)(2,1)} %get-tuple-element.162.refs_0_, bf16[1024,1024]{1,0:T(8,128)(2,1)} %collective-permute-done.14.refs_1_, f32[1024,1024]{1,0:T(8,128)} %get-tuple-element.164.refs_2_.refs_1_, ...), custom_call_target="tpu_custom_call" | custom-call | flops 110000000 | tf_op jit(solution)/shard_map/branch_own/pallas_call | solution.py:83
  266.9 1.8 collective-permute-start.15
  268.7 3.2 fusion.6
  277.4 12.0 %attended_back.1 = (bf16[2048,1024]{1,0:T(8,128)(2,1)}, bf16[2048,1024]{1,0:T(8,128)(2,1)}) custom-call(s32[14]{0:T(128)} %stack.47.info_ref, bf16[1024,1024]{1,0:T(8,128)(2,1)} %get-tuple-element.165.refs_0_, bf16[1024,1024]{1,0:T(8,128)(2,1)} %collective-permute-done.17.refs_1_, bf16[512,1024]{1,0:T(8,128)(2,1)} %refs_2_.4, ...), custom_call_target="tpu_custom_call" | custom-call | flops 80000000 | tf_op jit(solution)/shard_map/attended_back/pallas_call | solution.py:83
  289.4 9.4 %convolution_convert_fusion.3 = bf16[1024,1024]{1,0:T(8,128)(2,1)} fusion(bf16[2048,1024]{1,0:T(8,128)(2,1)} %get-tuple-element.146.refs_0_.refs_3_, bf16[2048,1024]{1,0:T(8,128)(2,1)} %get-tuple-element.167), kind=kOutput, calls=%fused_computation.4 | convolution fusion | flops 4296015872 | bytes 10485760 | tf_op jit(solution)/shard_map/dot_general | solution.py:31
  298.8 23.7 %attend_back.4 = (bf16[2048,1536]{1,0:T(8,128)(2,1)}, f32[2,128]{1,0:T(2,128)}) custom-call(s32[8]{0:T(128)} %and_select_fusion.low_ref.refs_0_, bf16[2048,2048]{1,0:T(8,128)(2,1)} %get-tuple-element.137.qkv_ref.refs_1_, bf16[2048,1024]{1,0:T(8,128)(2,1)} %get-tuple-element.186.refs_2_, bf16[2048,1024]{1,0:T(8,128)(2,1)} %get-tuple-element.146.refs_0_.refs_3_, ...), custom_call_target="tpu_custom_call" | custom-call | flops 210000000 | tf_op jit(solution)/shard_map/attend_back/pallas_call | solution.py:605
  322.5 2.2 dynamic-slice_add_fusion.1
  329.5 2.3 constant_dynamic-slice_fusion.9
  333.3 23.8 %attend_back.5 = (bf16[2048,1536]{1,0:T(8,128)(2,1)}, f32[2,128]{1,0:T(2,128)}) custom-call(s32[8]{0:T(128)} %and_select_fusion.low_ref.refs_0_, bf16[2048,2048]{1,0:T(8,128)(2,1)} %get-tuple-element.137.qkv_ref.refs_1_, bf16[2048,1024]{1,0:T(8,128)(2,1)} %get-tuple-element.186.refs_2_, ...), custom_call_target="tpu_custom_call", output_to_operand_aliasing={{0}: (10, {})} | custom-call | flops 210000000 | tf_op jit(solution)/shard_map/attend_back/pallas_call | solution.py:605
  357.1 5.2 collective-permute-done.18
  371.2 23.8 %attend_back.6 = (bf16[2048,1536]{1,0:T(8,128)(2,1)}, f32[2,128]{1,0:T(2,128)}) custom-call(s32[8]{0:T(128)} %and_select_fusion.low_ref.refs_0_, bf16[2048,2048]{1,0:T(8,128)(2,1)} %get-tuple-element.137.qkv_ref.refs_1_, bf16[2048,1024]{1,0:T(8,128)(2,1)} %get-tuple-element.186.refs_2_, ...), custom_call_target="tpu_custom_call", output_to_operand_aliasing={{0}: (10, {})} | custom-call | flops 210000000 | tf_op jit(solution)/shard_map/attend_back/pallas_call | solution.py:605
  395.1 10.8 %convolution_convert_fusion.1 = bf16[1024,1536]{1,0:T(8,128)(2,1)S(1)} fusion(bf16[2048,1024]{1,0:T(8,128)(2,1)} %get-tuple-element.184, bf16[2048,1536]{1,0:T(8,128)(2,1)} %get-tuple-element.185.refs_0_), kind=kOutput, calls=%fused_computation.2 | convolution fusion | flops 6444023808 | bytes 13631488 | tf_op jit(solution)/shard_map/dot_general | solution.py:31
  415.8 23.7 %attend_back.7 = (bf16[2048,512]{1,0:T(8,128)(2,1)}, f32[2,128]{1,0:T(2,128)}) custom-call(s32[8]{0:T(128)} %and_select_fusion.low_ref.refs_0_, bf16[2048,2048]{1,0:T(8,128)(2,1)} %get-tuple-element.137.qkv_ref.refs_1_, bf16[2048,1024]{1,0:T(8,128)(2,1)} %get-tuple-element.186.refs_2_, bf16[2048,1024]{1,0:T(8,128)(2,1)} %get-tuple-element.146.refs_0_.refs_3_, ...), custom_call_target="tpu_custom_call" | custom-call | flops 210000000 | tf_op jit(solution)/shard_map/attend_back/pallas_call | solution.py:605
  442.5 5.4 convolution_convert_fusion.4
  447.8 2.0 dynamic-slice_add_fusion
  457.8 10.2 %tokens_other.1 = bf16[1024,1024]{1,0:T(8,128)(2,1)} custom-call(s32[14]{0:T(128)} %stack.47.info_ref, bf16[2048,1536]{1,0:T(8,128)(2,1)} %get-tuple-element.185.refs_0_, bf16[2048,512]{1,0:T(8,128)(2,1)} %get-tuple-element.193.refs_1_, bf16[256,2048]{1,0:T(8,128)(2,1)} %get-tuple-element.127.refs_6_.refs_2_, ...), custom_call_target="tpu_custom_call" | custom-call | flops 60000000 | tf_op jit(solution)/shard_map/tokens_other/pallas_call | solution.py:83
  468.1 5.8 collective-permute-done.27
  477.3 2.4 collective-permute-start.31
  486.0 9.1 %output_other.1 = bf16[1024,1024]{1,0:T(8,128)(2,1)} custom-call(s32[14]{0:T(128)} %stack.47.info_ref, bf16[2048,1536]{1,0:T(8,128)(2,1)} %get-tuple-element.217.refs_0_, bf16[768,1024]{1,0:T(8,128)(2,1)} %refs_3_.4, bf16[768,1024]{1,0:T(8,128)(2,1)} %collective-permute-done.10.refs_9_.refs_2_.refs_4_), custom_call_target="tpu_custom_call" | custom-call | flops 60000000 | tf_op jit(solution)/shard_map/output_other/pallas_call | solution.py:83
  495.2 3.5 collective-permute-done.32
  503.6 1.8 collective-permute-start.35
  505.4 1.9 maximum_select_fusion.refs_0_
  509.5 1.9 collective-permute-start.34
  511.4 13.4 %tokens_own.1 = (f32[1024,1024]{1,0:T(8,128)}, f32[1,1024]{1,0:T(1,128)}) custom-call(s32[14]{0:T(128)} %stack.47.info_ref, bf16[2048,1536]{1,0:T(8,128)(2,1)} %get-tuple-element.185.refs_0_, bf16[2048,512]{1,0:T(8,128)(2,1)} %get-tuple-element.193.refs_1_, bf16[1024,1024]{1,0:T(8,128)(2,1)} %collective-permute-done.36.refs_2_, bf16[1024,1024]{1,0:T(8,128)(2,1)} %refs_3_.3, ...), custom_call_target="tpu_custom_call" | custom-call | flops 90000000 | tf_op jit(solution)/shard_map/tokens_own/pallas_call | solution.py:83
  524.8 2.3 collective-permute-done.34
  527.1 2.3 maximum_select_fusion.4
  531.7 3.4 collective-permute-start.39
  535.2 10.1 %output_own.1 = bf16[1024,1024]{1,0:T(8,128)(2,1)} custom-call(s32[14]{0:T(128)} %stack.47.info_ref, bf16[2048,1536]{1,0:T(8,128)(2,1)} %get-tuple-element.217.refs_0_, f32[1024,1024]{1,0:T(8,128)} %get-tuple-element.164.refs_2_.refs_1_, bf16[1024,1024]{1,0:T(8,128)(2,1)} %collective-permute-done.41.refs_2_, bf16[768,1024]{1,0:T(8,128)(2,1)} %refs_3_.4, ...), custom_call_target="tpu_custom_call" | custom-call | flops 60000000 | tf_op jit(solution)/shard_map/output_own/pallas_call | solution.py:83
  545.4 3.5 collective-permute-done.39
  550.7 2.1 maximum_select_fusion.1.refs_0_
  552.8 2.6 collective-permute-start.47
  556.4 2.8 collective-permute-start.42
  561.0 4.4 finish_rows.2
  565.4 4.6 finish_gu.2
  571.7 2.0 collective-permute-start.46
  573.7 11.5 %collective-permute-done.46 = f32[2304]{0:T(1024)S(1)} collective-permute-done((f32[2304]{0:T(1024)S(1)}, f32[2304]{0:T(1024)S(1)}, u32[]{:S(2)}, u32[]{:S(2)}) %collective-permute-start.46) | collective-permute-done | bytes 9248 | tf_op jit(solution)/shard_map/ppermute | solution.py:716
  589.8 2.1 slice_select_fusion
  592.7 3.8 finish_rows.3
  597.4 4.5 finish_gu.3
  601.9 8.9 %collective-permute-done.51 = f32[2304]{0:T(1024)S(1)} collective-permute-done((f32[2304]{0:T(1024)S(1)}, f32[2304]{0:T(1024)S(1)}, u32[]{:S(2)}, u32[]{:S(2)}) %collective-permute-start.51) | collective-permute-done | bytes 9248 | tf_op jit(solution)/shard_map/ppermute | solution.py:716
  615.6 4.7 unpack_qkv.1
  (278 shorter events, 98.6 us)
Async XLA Ops:
  5.1 16.0 %copy-start.4 = (bf16[256,2048]{1,0:T(8,128)(2,1)S(1)}, bf16[256,2048]{1,0:T(8,128)(2,1)}, u32[]{:S(2)}) copy-start(bf16[256,2048]{1,0:T(8,128)(2,1)} %get-tuple-element.127.refs_6_.refs_2_) | copy-start | bytes 3145732
  5.2 3.2 collective-permute-start
  12.7 11.8 %collective-permute-start.4 = (bf16[256,3072]{1,0:T(8,128)(2,1)}, bf16[256,3072]{1,0:T(8,128)(2,1)S(1)}, u32[]{:S(2)}, u32[]{:S(2)}) collective-permute-start(bf16[256,3072]{1,0:T(8,128)(2,1)} %get-tuple-element.132), channel_id=1, source_target_pairs={{0,1},{1,0},{2,3},{3,2},{4,5},{5,4},{6,7},{7,6},{8,9},{9,8},{10,11... | collective-permute-start | bytes 4718600 | tf_op jit(solution)/shard_map/ppermute | solution.py:716
  13.2 3.2 collective-permute-start.2
  13.3 46.9 %collective-permute-start.5 = (bf16[1024,1024]{1,0:T(8,128)(2,1)}, bf16[1024,1024]{1,0:T(8,128)(2,1)}, u32[]{:S(2)}, u32[]{:S(2)}) collective-permute-start(bf16[1024,1024]{1,0:T(8,128)(2,1)} %refs_3_.3), channel_id=1, source_target_pairs={{0,1},{1,0},{2,3},{3,2},{4,5},{5,4},{6,7},{7,6},{8,9},{9,8},{10,11... | collective-permute-start | bytes 6291464 | tf_op jit(solution)/shard_map/ppermute | solution.py:716
  16.4 4.5 collective-permute-start.3
  21.3 24.5 %collective-permute-start.1 = (bf16[256,2048]{1,0:T(8,128)(2,1)S(1)}, bf16[256,2048]{1,0:T(8,128)(2,1)}, u32[]{:S(2)}, u32[]{:S(2)}) collective-permute-start(bf16[256,2048]{1,0:T(8,128)(2,1)S(1)} %broadcast_select_fusion.3), channel_id=1, source_target_pairs={{0,2},{2,0},{1,3},{3,1},{4,6},{6,4},{5,7},{7,5},{8,10},{10,8},{9,1... | collective-permute-start | bytes 3145736 | tf_op jit(solution)/shard_map/ppermute | solution.py:716
  24.6 25.8 %copy-start.56 = (s32[1,2048]{1,0:T(1,128)S(1)}, s32[1,2048]{1,0:T(1,128)}, u32[]{:S(2)}) copy-start(s32[1,2048]{1,0:T(1,128)} %param.15) | copy-start | bytes 24580
  24.6 29.1 %copy-start.9 = (bf16[512,1024]{1,0:T(8,128)(2,1)S(1)}, bf16[512,1024]{1,0:T(8,128)(2,1)}, u32[]{:S(2)}) copy-start(bf16[512,1024]{1,0:T(8,128)(2,1)} %refs_2_.4) | copy-start | bytes 3145732
  45.8 24.8 %collective-permute-start.6 = (bf16[256,2048]{1,0:T(8,128)(2,1)}, bf16[256,2048]{1,0:T(8,128)(2,1)}, u32[]{:S(2)}, u32[]{:S(2)}) collective-permute-start(bf16[256,2048]{1,0:T(8,128)(2,1)} %collective-permute-done.1.refs_8_.refs_4_), channel_id=1, source_target_pairs={{0,4},{4,0},{8,12},{12,8},{16,20},{20,16},{24,28},{28,24},{1,5},{5... | collective-permute-start | bytes 3145736 | tf_op jit(solution)/shard_map/ppermute | solution.py:716
  48.9 57.0 %collective-permute-start.7 = (bf16[256,3072]{1,0:T(8,128)(2,1)}, bf16[256,3072]{1,0:T(8,128)(2,1)S(1)}, u32[]{:S(2)}, u32[]{:S(2)}) collective-permute-start(bf16[256,3072]{1,0:T(8,128)(2,1)} %broadcast_select_fusion), channel_id=1, source_target_pairs={{0,2},{2,0},{1,3},{3,1},{4,6},{6,4},{5,7},{7,5},{8,10},{10,8},{9,1... | collective-permute-start | bytes 4718600 | tf_op jit(solution)/shard_map/ppermute | solution.py:716
  53.6 52.2 %collective-permute-start.8 = (bf16[512,1024]{1,0:T(8,128)(2,1)S(1)}, bf16[512,1024]{1,0:T(8,128)(2,1)}, u32[]{:S(2)}, u32[]{:S(2)}) collective-permute-start(bf16[512,1024]{1,0:T(8,128)(2,1)S(1)} %copy-done.9), channel_id=1, source_target_pairs={{0,2},{2,0},{1,3},{3,1},{4,6},{6,4},{5,7},{7,5},{8,10},{10,8},{9,1... | collective-permute-start | bytes 3145736 | tf_op jit(solution)/shard_map/ppermute | solution.py:716
  105.9 26.5 %copy-start.5 = (bf16[256,3072]{1,0:T(8,128)(2,1)}, bf16[256,3072]{1,0:T(8,128)(2,1)S(1)}, u32[]{:S(2)}) copy-start(bf16[256,3072]{1,0:T(8,128)(2,1)S(1)} %collective-permute-done.7.refs_6_.refs_3_.refs_7_) | copy-start | bytes 4718596
  105.9 48.2 %collective-permute-start.10 = (bf16[768,1024]{1,0:T(8,128)(2,1)}, bf16[768,1024]{1,0:T(8,128)(2,1)}, u32[]{:S(2)}, u32[]{:S(2)}) collective-permute-start(bf16[768,1024]{1,0:T(8,128)(2,1)} %refs_3_.4), channel_id=1, source_target_pairs={{0,2},{2,0},{1,3},{3,1},{4,6},{6,4},{5,7},{7,5},{8,10},{10,8},{9,1... | collective-permute-start | bytes 4718600 | tf_op jit(solution)/shard_map/ppermute | solution.py:716
  107.4 46.7 %collective-permute-start.9 = (bf16[256,3072]{1,0:T(8,128)(2,1)S(1)}, bf16[256,3072]{1,0:T(8,128)(2,1)S(1)}, u32[]{:S(2)}, u32[]{:S(2)}) collective-permute-start(bf16[256,3072]{1,0:T(8,128)(2,1)S(1)} %collective-permute-done.7.refs_6_.refs_3_.refs_7_), channel_id=1, source_target_pairs={{0,4},{4,0},{8,12},{12,8},{16,20},{20,16},{24,28},{28,24},{1,5},{5... | collective-permute-start | bytes 4718600 | tf_op jit(solution)/shard_map/ppermute | solution.py:716
  154.1 14.1 %copy-start.6 = (bf16[256,3072]{1,0:T(8,128)(2,1)}, bf16[256,3072]{1,0:T(8,128)(2,1)S(1)}, u32[]{:S(2)}) copy-start(bf16[256,3072]{1,0:T(8,128)(2,1)S(1)} %collective-permute-done.9.refs_7_.refs_4_.refs_8_) | copy-start | bytes 4718596
  154.1 4.6 collective-permute-start.11
  154.2 14.2 %collective-permute-start.13 = (bf16[1024,1024]{1,0:T(8,128)(2,1)}, bf16[1024,1024]{1,0:T(8,128)(2,1)}, u32[]{:S(2)}, u32[]{:S(2)}) collective-permute-start(bf16[1024,1024]{1,0:T(8,128)(2,1)} %refs_3_.2), channel_id=1, source_target_pairs={{0,1},{1,0},{2,3},{3,2},{4,5},{5,4},{6,7},{7,6},{8,9},{9,8},{10,11... | collective-permute-start | bytes 6291464 | tf_op jit(solution)/shard_map/ppermute | solution.py:716
  168.2 4.4 collective-permute-start.12
  216.1 49.5 %copy-start.18 = (bf16[1536,1024]{1,0:T(8,128)(2,1)}, bf16[1536,1024]{1,0:T(8,128)(2,1)S(1)}, u32[]{:S(2)}) copy-start(bf16[1536,1024]{1,0:T(8,128)(2,1)S(1)} %convolution_convert_fusion.2) | copy-start | bytes 9437188
  229.8 18.9 %collective-permute-start.14 = (bf16[1024,1024]{1,0:T(8,128)(2,1)}, bf16[1024,1024]{1,0:T(8,128)(2,1)}, u32[]{:S(2)}, u32[]{:S(2)}) collective-permute-start(bf16[1024,1024]{1,0:T(8,128)(2,1)} %branch_other.1), channel_id=1, source_target_pairs={{0,1},{1,0},{2,3},{3,2},{4,5},{5,4},{6,7},{7,6},{8,9},{9,8},{10,11... | collective-permute-start | bytes 6291464 | tf_op jit(solution)/shard_map/ppermute | solution.py:716
  265.1 12.2 %collective-permute-start.17 = (bf16[1024,1024]{1,0:T(8,128)(2,1)}, bf16[1024,1024]{1,0:T(8,128)(2,1)}, u32[]{:S(2)}, u32[]{:S(2)}) collective-permute-start(bf16[1024,1024]{1,0:T(8,128)(2,1)} %get-tuple-element.165.refs_0_), channel_id=1, source_target_pairs={{0,1},{1,0},{2,3},{3,2},{4,5},{5,4},{6,7},{7,6},{8,9},{9,8},{10,11... | collective-permute-start | bytes 6291464 | tf_op jit(solution)/shard_map/ppermute | solution.py:716
  266.9 55.6 %collective-permute-start.15 = (bf16[2,1,384,1024]{3,2,1,0:T(8,128)(2,1)}, bf16[2,1,384,1024]{3,2,1,0:T(8,128)(2,1)}, u32[]{:S(2)}, u32[]{:S(2)}) collective-permute-start(bf16[2,1,384,1024]{3,2,1,0:T(8,128)(2,1)} %constant_dynamic-slice_fusion.16), channel_id=1, source_target_pairs={{0,4},{4,0},{8,12},{12,8},{16,20},{20,16},{24,28},{28,24},{1,5},{5... | collective-permute-start | bytes 4718600 | tf_op jit(solution)/shard_map/ppermute | solution.py:716
  274.1 48.4 %collective-permute-start.16 = (bf16[1,2,256,1536]{3,2,1,0:T(8,128)(2,1)}, bf16[1,2,256,1536]{3,2,1,0:T(8,128)(2,1)}, u32[]{:S(2)}, u32[]{:S(2)}) collective-permute-start(bf16[1,2,256,1536]{3,2,1,0:T(8,128)(2,1)} %constant_dynamic-slice_fusion.15), channel_id=1, source_target_pairs={{0,2},{2,0},{1,3},{3,1},{4,6},{6,4},{5,7},{7,5},{8,10},{10,8},{9,1... | collective-permute-start | bytes 4718600 | tf_op jit(solution)/shard_map/ppermute | solution.py:716
  275.9 81.2 %collective-permute-start.20 = (bf16[1,2,256,1536]{3,2,1,0:T(8,128)(2,1)}, bf16[1,2,256,1536]{3,2,1,0:T(8,128)(2,1)}, u32[]{:S(2)}, u32[]{:S(2)}) collective-permute-start(bf16[1,2,256,1536]{3,2,1,0:T(8,128)(2,1)} %constant_dynamic-slice_fusion.12), channel_id=1, source_target_pairs={{0,2},{2,0},{1,3},{3,1},{4,6},{6,4},{5,7},{7,5},{8,10},{10,8},{9,1... | collective-permute-start | bytes 4718600 | tf_op jit(solution)/shard_map/ppermute | solution.py:716
  325.8 31.3 %collective-permute-start.19 = (bf16[1,1,256,1536]{3,2,1,0:T(8,128)(2,1)}, bf16[1,1,256,1536]{3,2,1,0:T(8,128)(2,1)}, u32[]{:S(2)}, u32[]{:S(2)}) collective-permute-start(bf16[1,1,256,1536]{3,2,1,0:T(8,128)(2,1)} %constant_dynamic-slice_fusion.13), channel_id=1, source_target_pairs={{0,4},{4,0},{8,12},{12,8},{16,20},{20,16},{24,28},{28,24},{1,5},{5... | collective-permute-start | bytes 2359304 | tf_op jit(solution)/shard_map/ppermute | solution.py:716
  329.0 33.3 %collective-permute-start.18 = (bf16[1,1,384,1024]{3,2,1,0:T(8,128)(2,1)}, bf16[1,1,384,1024]{3,2,1,0:T(8,128)(2,1)}, u32[]{:S(2)}, u32[]{:S(2)}) collective-permute-start(bf16[1,1,384,1024]{3,2,1,0:T(8,128)(2,1)} %constant_dynamic-slice_fusion.14), channel_id=1, source_target_pairs={{0,2},{2,0},{1,3},{3,1},{4,6},{6,4},{5,7},{7,5},{8,10},{10,8},{9,1... | collective-permute-start | bytes 2359304 | tf_op jit(solution)/shard_map/ppermute | solution.py:716
  331.8 63.3 %collective-permute-start.23 = (bf16[1,2,256,1024]{3,2,1,0:T(8,128)(2,1)}, bf16[1,2,256,1024]{3,2,1,0:T(8,128)(2,1)}, u32[]{:S(2)}, u32[]{:S(2)}) collective-permute-start(bf16[1,2,256,1024]{3,2,1,0:T(8,128)(2,1)} %constant_dynamic-slice_fusion.9), channel_id=1, source_target_pairs={{0,2},{2,0},{1,3},{3,1},{4,6},{6,4},{5,7},{7,5},{8,10},{10,8},{9,1... | collective-permute-start | bytes 3145736 | tf_op jit(solution)/shard_map/ppermute | solution.py:716
  364.8 30.3 %collective-permute-start.22 = (bf16[1,1,256,1536]{3,2,1,0:T(8,128)(2,1)}, bf16[1,1,256,1536]{3,2,1,0:T(8,128)(2,1)S(1)}, u32[]{:S(2)}, u32[]{:S(2)}) collective-permute-start(bf16[1,1,256,1536]{3,2,1,0:T(8,128)(2,1)} %constant_dynamic-slice_fusion.10), channel_id=1, source_target_pairs={{0,4},{4,0},{8,12},{12,8},{16,20},{20,16},{24,28},{28,24},{1,5},{5... | collective-permute-start | bytes 2359304 | tf_op jit(solution)/shard_map/ppermute | solution.py:716
  369.7 25.4 %collective-permute-start.21 = (bf16[768,512]{1,0:T(8,128)(2,1)}, bf16[768,512]{1,0:T(8,128)(2,1)S(1)}, u32[]{:S(2)}, u32[]{:S(2)}) collective-permute-start(bf16[768,512]{1,0:T(8,128)(2,1)} %constant_dynamic-slice_fusion.11), channel_id=1, source_target_pairs={{0,8},{4,12},{8,0},{12,4},{16,24},{20,28},{24,16},{28,20},{1,9},{5... | collective-permute-start | bytes 2359304 | tf_op jit(solution)/shard_map/ppermute | solution.py:716
  395.1 10.8 %copy-start.35 = (bf16[1,1,256,1536]{3,2,1,0:T(8,128)(2,1)}, bf16[1,1,256,1536]{3,2,1,0:T(8,128)(2,1)S(1)}, u32[]{:S(2)}) copy-start(bf16[1,1,256,1536]{3,2,1,0:T(8,128)(2,1)S(1)} %collective-permute-done.22) | copy-start | bytes 2359300
  408.3 34.2 %collective-permute-start.26 = (bf16[1,2,256,1536]{3,2,1,0:T(8,128)(2,1)}, bf16[1,2,256,1536]{3,2,1,0:T(8,128)(2,1)}, u32[]{:S(2)}, u32[]{:S(2)}) collective-permute-start(bf16[1,2,256,1536]{3,2,1,0:T(8,128)(2,1)} %constant_dynamic-slice_fusion.6), channel_id=1, source_target_pairs={{0,2},{2,0},{1,3},{3,1},{4,6},{6,4},{5,7},{7,5},{8,10},{10,8},{9,1... | collective-permute-start | bytes 4718600 | tf_op jit(solution)/shard_map/ppermute | solution.py:716
  412.2 28.7 %collective-permute-start.25 = (bf16[1,1,256,1024]{3,2,1,0:T(8,128)(2,1)}, bf16[1,1,256,1024]{3,2,1,0:T(8,128)(2,1)}, u32[]{:S(2)}, u32[]{:S(2)}) collective-permute-start(bf16[1,1,256,1024]{3,2,1,0:T(8,128)(2,1)} %constant_dynamic-slice_fusion.7), channel_id=1, source_target_pairs={{0,4},{4,0},{8,12},{12,8},{16,20},{20,16},{24,28},{28,24},{1,5},{5... | collective-permute-start | bytes 1572872 | tf_op jit(solution)/shard_map/ppermute | solution.py:716
  413.2 27.7 %collective-permute-start.24 = (bf16[384,512]{1,0:T(8,128)(2,1)S(1)}, bf16[384,512]{1,0:T(8,128)(2,1)S(1)}, u32[]{:S(2)}, u32[]{:S(2)}) collective-permute-start(bf16[384,512]{1,0:T(8,128)(2,1)S(1)} %constant_dynamic-slice_fusion.8), channel_id=1, source_target_pairs={{0,16},{4,20},{8,24},{12,28},{16,0},{20,4},{24,8},{28,12},{1,17},{... | collective-permute-start | bytes 1179656 | tf_op jit(solution)/shard_map/ppermute | solution.py:716
  450.8 25.1 %collective-permute-start.29 = (bf16[1,1,256,1536]{3,2,1,0:T(8,128)(2,1)}, bf16[1,1,256,1536]{3,2,1,0:T(8,128)(2,1)}, u32[]{:S(2)}, u32[]{:S(2)}) collective-permute-start(bf16[1,1,256,1536]{3,2,1,0:T(8,128)(2,1)} %constant_dynamic-slice_fusion.4), channel_id=1, source_target_pairs={{0,4},{4,0},{8,12},{12,8},{16,20},{20,16},{24,28},{28,24},{1,5},{5... | collective-permute-start | bytes 2359304 | tf_op jit(solution)/shard_map/ppermute | solution.py:716
  453.4 21.6 %collective-permute-start.28 = (bf16[640,512]{1,0:T(8,128)(2,1)}, bf16[640,512]{1,0:T(8,128)(2,1)S(1)}, u32[]{:S(2)}, u32[]{:S(2)}) collective-permute-start(bf16[640,512]{1,0:T(8,128)(2,1)} %constant_dynamic-slice_fusion.5), channel_id=1, source_target_pairs={{0,8},{4,12},{8,0},{12,4},{16,24},{20,28},{24,16},{28,20},{1,9},{5... | collective-permute-start | bytes 1966088 | tf_op jit(solution)/shard_map/ppermute | solution.py:716
  455.1 18.7 %collective-permute-start.30 = (bf16[1,2,256,512]{3,2,1,0:T(8,128)(2,1)}, bf16[1,2,256,512]{3,2,1,0:T(8,128)(2,1)}, u32[]{:S(2)}, u32[]{:S(2)}) collective-permute-start(bf16[1,2,256,512]{3,2,1,0:T(8,128)(2,1)} %constant_dynamic-slice_fusion.3), channel_id=1, source_target_pairs={{0,2},{2,0},{1,3},{3,1},{4,6},{6,4},{5,7},{7,5},{8,10},{10,8},{9,1... | collective-permute-start | bytes 1572872 | tf_op jit(solution)/shard_map/ppermute | solution.py:716
  457.0 11.0 %copy-start.31 = (bf16[384,512]{1,0:T(8,128)(2,1)}, bf16[384,512]{1,0:T(8,128)(2,1)S(1)}, u32[]{:S(2)}) copy-start(bf16[384,512]{1,0:T(8,128)(2,1)S(1)} %dynamic-slice_add_fusion.8) | copy-start | bytes 1179652
  457.0 16.8 %collective-permute-start.27 = (bf16[384,512]{1,0:T(8,128)(2,1)S(1)}, bf16[384,512]{1,0:T(8,128)(2,1)S(1)}, u32[]{:S(2)}, u32[]{:S(2)}) collective-permute-start(bf16[384,512]{1,0:T(8,128)(2,1)S(1)} %dynamic-slice_add_fusion.8), channel_id=1, source_target_pairs={{0,16},{4,20},{8,24},{12,28},{16,0},{20,4},{24,8},{28,12},{1,17},{... | collective-permute-start | bytes 1179656 | tf_op jit(solution)/shard_map/ppermute | solution.py:716
  468.0 11.6 %copy-start.30 = (bf16[1280,512]{1,0:T(8,128)(2,1)S(1)}, bf16[1280,512]{1,0:T(8,128)(2,1)}, u32[]{:S(2)}) copy-start(bf16[1280,512]{1,0:T(8,128)(2,1)} %copy-done.29) | copy-start | bytes 3932164
  477.3 22.6 %collective-permute-start.31 = (bf16[768,512]{1,0:T(8,128)(2,1)S(1)}, bf16[768,512]{1,0:T(8,128)(2,1)}, u32[]{:S(2)}, u32[]{:S(2)}) collective-permute-start(bf16[768,512]{1,0:T(8,128)(2,1)S(1)} %maximum_select_fusion.3), channel_id=1, source_target_pairs={{0,8},{4,12},{8,0},{12,4},{16,24},{20,28},{24,16},{28,20},{1,9},{5... | collective-permute-start | bytes 2359304 | tf_op jit(solution)/shard_map/ppermute | solution.py:716
  481.8 16.9 %collective-permute-start.32 = (bf16[320,512]{1,0:T(8,128)(2,1)S(1)}, bf16[320,512]{1,0:T(8,128)(2,1)S(1)}, u32[]{:S(2)}, u32[]{:S(2)}) collective-permute-start(bf16[320,512]{1,0:T(8,128)(2,1)S(1)} %constant_dynamic-slice_fusion.2), channel_id=1, source_target_pairs={{0,16},{4,20},{8,24},{12,28},{16,0},{20,4},{24,8},{28,12},{1,17},{... | collective-permute-start | bytes 983048 | tf_op jit(solution)/shard_map/ppermute | solution.py:716
  484.4 10.8 %collective-permute-start.33 = (bf16[1,1,256,512]{3,2,1,0:T(8,128)(2,1)}, bf16[1,1,256,512]{3,2,1,0:T(8,128)(2,1)}, u32[]{:S(2)}, u32[]{:S(2)}) collective-permute-start(bf16[1,1,256,512]{3,2,1,0:T(8,128)(2,1)} %constant_dynamic-slice_fusion.1), channel_id=1, source_target_pairs={{0,4},{4,0},{8,12},{12,8},{16,20},{20,16},{24,28},{28,24},{1,5},{5... | collective-permute-start | bytes 786440 | tf_op jit(solution)/shard_map/ppermute | solution.py:716
  499.9 11.5 %collective-permute-start.36 = (bf16[1024,1024]{1,0:T(8,128)(2,1)}, bf16[1024,1024]{1,0:T(8,128)(2,1)}, u32[]{:S(2)}, u32[]{:S(2)}) collective-permute-start(bf16[1024,1024]{1,0:T(8,128)(2,1)} %tokens_other.1), channel_id=1, source_target_pairs={{0,1},{1,0},{2,3},{3,2},{4,5},{5,4},{6,7},{7,6},{8,9},{9,8},{10,11... | collective-permute-start | bytes 6291464 | tf_op jit(solution)/shard_map/ppermute | solution.py:716
  501.1 34.1 %collective-permute-start.41 = (bf16[1024,1024]{1,0:T(8,128)(2,1)}, bf16[1024,1024]{1,0:T(8,128)(2,1)}, u32[]{:S(2)}, u32[]{:S(2)}) collective-permute-start(bf16[1024,1024]{1,0:T(8,128)(2,1)} %output_other.1), channel_id=1, source_target_pairs={{0,1},{1,0},{2,3},{3,2},{4,5},{5,4},{6,7},{7,6},{8,9},{9,8},{10,11... | collective-permute-start | bytes 6291464 | tf_op jit(solution)/shard_map/ppermute | solution.py:716
  503.6 23.5 %collective-permute-start.35 = (bf16[128,2048]{1,0:T(8,128)(2,1)}, bf16[128,2048]{1,0:T(8,128)(2,1)}, u32[]{:S(2)}, u32[]{:S(2)}) collective-permute-start(bf16[128,2048]{1,0:T(8,128)(2,1)} %fusion.2), channel_id=1, source_target_pairs={{0,8},{4,12},{8,0},{12,4},{16,24},{20,28},{24,16},{28,20},{1,9},{5... | collective-permute-start | bytes 1572872 | tf_op jit(solution)/shard_map/ppermute | solution.py:716
  507.3 42.4 %copy-start.2 = (bf16[1536,512]{1,0:T(8,128)(2,1)}, bf16[1536,512]{1,0:T(8,128)(2,1)S(1)}, u32[]{:S(2)}) copy-start(bf16[1536,512]{1,0:T(8,128)(2,1)S(1)} %maximum_select_fusion.refs_0_) | copy-start | bytes 4718596
  507.3 41.6 %collective-permute-start.38 = (bf16[1536,512]{1,0:T(8,128)(2,1)S(1)}, bf16[1536,512]{1,0:T(8,128)(2,1)S(1)}, u32[]{:S(2)}, u32[]{:S(2)}) collective-permute-start(bf16[1536,512]{1,0:T(8,128)(2,1)S(1)} %maximum_select_fusion.refs_0_), channel_id=1, source_target_pairs={{0,4},{4,0},{8,12},{12,8},{16,20},{20,16},{24,28},{28,24},{1,5},{5... | collective-permute-start | bytes 4718600 | tf_op jit(solution)/shard_map/ppermute | solution.py:716
  509.5 17.6 %collective-permute-start.34 = (bf16[320,512]{1,0:T(8,128)(2,1)}, bf16[320,512]{1,0:T(8,128)(2,1)}, u32[]{:S(2)}, u32[]{:S(2)}) collective-permute-start(bf16[320,512]{1,0:T(8,128)(2,1)} %dynamic-slice_add_fusion.9), channel_id=1, source_target_pairs={{0,16},{4,20},{8,24},{12,28},{16,0},{20,4},{24,8},{28,12},{1,17},{... | collective-permute-start | bytes 983048 | tf_op jit(solution)/shard_map/ppermute | solution.py:716
  529.3 20.4 %collective-permute-start.37 = (bf16[640,512]{1,0:T(8,128)(2,1)}, bf16[640,512]{1,0:T(8,128)(2,1)}, u32[]{:S(2)}, u32[]{:S(2)}) collective-permute-start(bf16[640,512]{1,0:T(8,128)(2,1)} %maximum_select_fusion.4), channel_id=1, source_target_pairs={{0,8},{4,12},{8,0},{12,4},{16,24},{20,28},{24,16},{28,20},{1,9},{5... | collective-permute-start | bytes 1966088 | tf_op jit(solution)/shard_map/ppermute | solution.py:716
  531.7 17.2 %collective-permute-start.39 = (bf16[64,2048]{1,0:T(8,128)(2,1)S(1)}, bf16[64,2048]{1,0:T(8,128)(2,1)}, u32[]{:S(2)}, u32[]{:S(2)}) collective-permute-start(bf16[64,2048]{1,0:T(8,128)(2,1)S(1)} %constant_dynamic-slice_fusion), channel_id=1, source_target_pairs={{0,16},{4,20},{8,24},{12,28},{16,0},{20,4},{24,8},{28,12},{1,17},{... | collective-permute-start | bytes 786440 | tf_op jit(solution)/shard_map/ppermute | solution.py:716
  535.2 10.2 %collective-permute-start.40 = (f32[2304]{0:T(1024)S(1)}, f32[2304]{0:T(1024)S(1)}, u32[]{:S(2)}, u32[]{:S(2)}) collective-permute-start(f32[2304]{0:T(1024)S(1)} %pad_maximum_fusion.2), channel_id=1, source_target_pairs={{0,1},{1,0},{2,3},{3,2},{4,5},{5,4},{6,7},{7,6},{8,9},{9,8},{10,11... | collective-permute-start | bytes 27656 | tf_op jit(solution)/shard_map/ppermute | solution.py:716
  550.7 14.7 %collective-permute-start.44 = (bf16[768,512]{1,0:T(8,128)(2,1)}, bf16[768,512]{1,0:T(8,128)(2,1)}, u32[]{:S(2)}, u32[]{:S(2)}) collective-permute-start(bf16[768,512]{1,0:T(8,128)(2,1)} %slice_select_fusion.1), channel_id=1, source_target_pairs={{0,1},{1,0},{2,3},{3,2},{4,5},{5,4},{6,7},{7,6},{8,9},{9,8},{10,11... | collective-permute-start | bytes 2359304 | tf_op jit(solution)/shard_map/ppermute | solution.py:716
  552.8 37.0 %copy-start.3 = (bf16[1280,512]{1,0:T(8,128)(2,1)}, bf16[1280,512]{1,0:T(8,128)(2,1)S(1)}, u32[]{:S(2)}) copy-start(bf16[1280,512]{1,0:T(8,128)(2,1)S(1)} %maximum_select_fusion.1.refs_0_) | copy-start | bytes 3932164
  552.8 35.3 %collective-permute-start.47 = (bf16[1280,512]{1,0:T(8,128)(2,1)S(1)}, bf16[1280,512]{1,0:T(8,128)(2,1)}, u32[]{:S(2)}, u32[]{:S(2)}) collective-permute-start(bf16[1280,512]{1,0:T(8,128)(2,1)S(1)} %maximum_select_fusion.1.refs_0_), channel_id=1, source_target_pairs={{0,4},{4,0},{8,12},{12,8},{16,20},{20,16},{24,28},{28,24},{1,5},{5... | collective-permute-start | bytes 3932168 | tf_op jit(solution)/shard_map/ppermute | solution.py:716
  556.4 15.1 %collective-permute-start.42 = (bf16[64,2048]{1,0:T(8,128)(2,1)S(1)}, bf16[64,2048]{1,0:T(8,128)(2,1)S(1)}, u32[]{:S(2)}, u32[]{:S(2)}) collective-permute-start(bf16[64,2048]{1,0:T(8,128)(2,1)S(1)} %dynamic-slice_add_fusion.10), channel_id=1, source_target_pairs={{0,16},{4,20},{8,24},{12,28},{16,0},{20,4},{24,8},{28,12},{1,17},{... | collective-permute-start | bytes 786440 | tf_op jit(solution)/shard_map/ppermute | solution.py:716
  559.2 10.8 %collective-permute-start.43 = (f32[2304]{0:T(1024)S(1)}, f32[2304]{0:T(1024)S(1)}, u32[]{:S(2)}, u32[]{:S(2)}) collective-permute-start(f32[2304]{0:T(1024)S(1)} %fusion.5), channel_id=1, source_target_pairs={{0,2},{2,0},{1,3},{3,1},{4,6},{6,4},{5,7},{7,5},{8,10},{10,8},{9,1... | collective-permute-start | bytes 27656 | tf_op jit(solution)/shard_map/ppermute | solution.py:716
  571.6 13.6 %collective-permute-start.45 = (bf16[128,2048]{1,0:T(8,128)(2,1)S(1)}, bf16[128,2048]{1,0:T(8,128)(2,1)S(1)}, u32[]{:S(2)}, u32[]{:S(2)}) collective-permute-start(bf16[128,2048]{1,0:T(8,128)(2,1)S(1)} %maximum_select_fusion.5), channel_id=1, source_target_pairs={{0,8},{4,12},{8,0},{12,4},{16,24},{20,28},{24,16},{28,20},{1,9},{5... | collective-permute-start | bytes 1572872 | tf_op jit(solution)/shard_map/ppermute | solution.py:716
  571.7 13.5 %collective-permute-start.46 = (f32[2304]{0:T(1024)S(1)}, f32[2304]{0:T(1024)S(1)}, u32[]{:S(2)}, u32[]{:S(2)}) collective-permute-start(f32[2304]{0:T(1024)S(1)} %add.231), channel_id=1, source_target_pairs={{0,8},{4,12},{8,0},{12,4},{16,24},{20,28},{24,16},{28,20},{1,9},{5... | collective-permute-start | bytes 27656 | tf_op jit(solution)/shard_map/ppermute | solution.py:716
  585.2 4.6 collective-permute-start.48
  586.6 24.3 %collective-permute-start.49 = (bf16[256,2048]{1,0:T(8,128)(2,1)S(1)}, bf16[256,2048]{1,0:T(8,128)(2,1)S(1)}, u32[]{:S(2)}, u32[]{:S(2)}) collective-permute-start(bf16[256,2048]{1,0:T(8,128)(2,1)S(1)} %maximum_select_fusion.2), channel_id=1, source_target_pairs={{0,4},{4,0},{8,12},{12,8},{16,20},{20,16},{24,28},{28,24},{1,5},{5... | collective-permute-start | bytes 3145736 | tf_op jit(solution)/shard_map/ppermute | solution.py:716
  591.9 4.6 collective-permute-start.50
  591.9 18.9 %collective-permute-start.51 = (f32[2304]{0:T(1024)S(1)}, f32[2304]{0:T(1024)S(1)}, u32[]{:S(2)}, u32[]{:S(2)}) collective-permute-start(f32[2304]{0:T(1024)S(1)} %add.233), channel_id=1, source_target_pairs={{0,4},{4,0},{8,12},{12,8},{16,20},{20,16},{24,28},{28,24},{1,5},{5... | collective-permute-start | bytes 27656 | tf_op jit(solution)/shard_map/ppermute | solution.py:716
  612.0 2.7 collective-permute-start.52
  (46 other events, 196.1 us)
